TPU v7x, 1024 devices: a whole 4x4x32 slice. The times are simulated.
1024 devices in a mesh: ta: 32 (over z_lo, x), gz: 4 (over z_hi), xy: 8 (over y, core).
Axes of the slice: x: 4, y: 4, z: 32 (z_hi: 4, z_lo: 8; z = z_hi * 8 + z_lo), core: 2. Of those that a mesh axis runs over, the one named last changes fastest.
Arguments:
- links: float32 [4, 2, 3, 3, 64, 8, 1024], P(None, None, None, None, 'ta', 'gz', 'xy'), may hold values from -1 to 1, as said below
- solutions: float32 [2, 2, 4, 3, 64, 8, 1024], P(None, None, None, None, 'ta', 'gz', 'xy'), may hold values from -6 to 6
Outputs:
- force: float32 [4, 2, 3, 3, 64, 8, 1024], P(None, None, None, None, 'ta', 'gz', 'xy')
Inputs may be any that keep to these rules, and one draw needn't show every extreme that they name: Each links[mu] at a site, read as a complex 3 x 3 matrix, is special unitary.
All inputs are finite; a program needn't handle non-finite values.
Results may differ from a plain program's by a relative error of at most 0.0001.
Values sent between devices are 32-bit elements; how exact they have to be, the bound alone decides.
No kernel may reach another device: no remote copies, remote signals or barrier semaphores. Data moves between devices by JAX's collectives and lax.ppermute only.
A program may use at most 32 MiB of HBM per device.

v0:
```python
from functools import reduce

import jax
import jax.numpy as jnp
import numpy as np
from jax import lax
from jax.sharding import PartitionSpec as P

Y_LEN = 64


HOPPING = 0.125
PLAQUETTE = 0.5


def padded_2(x, sides, width):
    for axis, dim in sides:
        size, length = (lax.axis_size(axis), x.shape[dim])
        up = [(i, (i + 1) % size) for i in range(size)]
        down = [(j, i) for i, j in up]
        last = lax.slice_in_dim(x, length - width, length, axis=dim)
        initial = lax.slice_in_dim(x, 0, width, axis=dim)
        before = lax.ppermute(last, axis, up)
        after = lax.ppermute(initial, axis, down)
        x = jnp.concatenate([before, x, after], axis=dim)
    return x


def padded_3(x, sides, width):
    edges = {}
    for axis, dim in sides:
        size, length = (lax.axis_size(axis), x.shape[dim])
        up = [(i, (i + 1) % size) for i in range(size)]
        last = lax.slice_in_dim(x, length - width, length, axis=dim)
        initial = lax.slice_in_dim(x, 0, width, axis=dim)
        edges[dim] = (
            lax.ppermute(last, axis, up),
            lax.ppermute(initial, axis, [(b, a) for a, b in up]),
        )
    done = []
    for _, dim in sides:
        low, high = edges[dim]
        around = [(width, width) if d in done else (0, 0) for d in range(x.ndim)]
        x = jnp.concatenate([jnp.pad(low, around), x, jnp.pad(high, around)], axis=dim)
        done.append(dim)
    return x


def shifted(x, axis, by):
    length = lax.axis_size(axis)
    return lax.ppermute(x, axis, [(i, (i + by) % length) for i in range(length)])


def projectors():
    identity = np.eye(4)
    zeros = np.zeros((4, 4))
    gamma_time = (np.array([[0, 0, 1, 0], [0, 0, 0, 1], [1, 0, 0, 0], [0, 1, 0, 0]]), zeros)
    gamma_depth = (zeros, np.array([[0, 0, 1, 0], [0, 0, 0, -1], [-1, 0, 0, 0], [0, 1, 0, 0]]))
    gamma_across = (zeros, np.array([[0, 0, 0, 1], [0, 0, 1, 0], [0, -1, 0, 0], [-1, 0, 0, 0]]))
    gamma_along = (np.array([[0, 0, 0, -1], [0, 0, 1, 0], [0, 1, 0, 0], [-1, 0, 0, 0]]), zeros)
    result = []
    for gamma_pair in (gamma_time, gamma_depth, gamma_across, gamma_along):
        result.append(
            ((identity - gamma_pair[0], -gamma_pair[1]), (identity + gamma_pair[0], gamma_pair[1]))
        )
    return result


def shift_rows(source, stride, row_length):
    positions = lax.iota(jnp.int32, source.shape[-1]) % row_length
    if stride > 0:
        return jnp.where(
            positions == row_length - 1,
            jnp.roll(source, row_length - 1, -1),
            jnp.roll(source, -1, -1),
        )
    return jnp.where(positions == 0, jnp.roll(source, 1 - row_length, -1), jnp.roll(source, 1, -1))


def offset(direction, stride):
    if direction == 3:
        return ((0, 0, 0), stride)
    anchor = [0, 0, 0]
    anchor[direction] = stride
    return (tuple(anchor), 0)


def combine(first_anchor, second_anchor):
    return (
        first_anchor[0] + second_anchor[0],
        first_anchor[1] + second_anchor[1],
        first_anchor[2] + second_anchor[2],
    )


def window(padded, margin, anchor, extent, stride):
    time_start = margin + anchor[0]
    depth_start = margin + anchor[1]
    row_start = (margin + anchor[2]) * Y_LEN
    region = padded[
        ...,
        time_start : time_start + extent[0],
        depth_start : depth_start + extent[1],
        row_start : row_start + extent[2] * Y_LEN,
    ]
    if stride != 0:
        region = shift_rows(region, stride, Y_LEN)
    return region


def face_window(face_box, direction, stride, flat_shape):
    starts = [1, 1, 1]
    if direction < 3:
        starts[direction] = 1 + stride
    time_count = face_box.shape[4] - 2
    depth_count = face_box.shape[5] - 2
    row_number = face_box.shape[6] - 2
    region = face_box[
        ...,
        starts[0] : starts[0] + time_count,
        starts[1] : starts[1] + depth_count,
        starts[2] : starts[2] + row_number,
        :,
    ]
    if direction == 3:
        region = jnp.roll(region, -stride, -1)
    return region.reshape(flat_shape)


def matrix_product(left, right):
    left_real, left_imaginary = (left[0], left[1])
    right_real, right_imaginary = (right[0], right[1])
    real_part = jnp.sum(
        left_real[:, :, None] * right_real[None]
        - left_imaginary[:, :, None] * right_imaginary[None],
        axis=1,
    )
    imaginary_part = jnp.sum(
        left_real[:, :, None] * right_imaginary[None]
        + left_imaginary[:, :, None] * right_real[None],
        axis=1,
    )
    return jnp.stack([real_part, imaginary_part])


def dagger(matrix):
    return jnp.stack([jnp.swapaxes(matrix[0], 0, 1), -jnp.swapaxes(matrix[1], 0, 1)])


def colour_apply(matrix, spinor):
    matrix_real = matrix[0][None, None]
    matrix_imaginary = matrix[1][None, None]
    spinor_real = spinor[:, 0][:, :, None]
    spinor_imaginary = spinor[:, 1][:, :, None]
    real_part = jnp.sum(matrix_real * spinor_real - matrix_imaginary * spinor_imaginary, axis=3)
    imaginary_part = jnp.sum(
        matrix_real * spinor_imaginary + matrix_imaginary * spinor_real, axis=3
    )
    return jnp.stack([real_part, imaginary_part], axis=1)


def spin_apply(projector, spinor):
    spinor_real = spinor[:, 0]
    spinor_imaginary = spinor[:, 1]
    rows_real = []
    rows_imaginary = []
    for spin_row in range(4):
        terms_real = []
        terms_imaginary = []
        for spin_column in range(4):
            weight_real = float(projector[0][spin_row, spin_column])
            weight_imaginary = float(projector[1][spin_row, spin_column])
            terms_real.append(
                weight_real * spinor_real[:, spin_column]
                - weight_imaginary * spinor_imaginary[:, spin_column]
            )
            terms_imaginary.append(
                weight_real * spinor_imaginary[:, spin_column]
                + weight_imaginary * spinor_real[:, spin_column]
            )
        rows_real.append(reduce(jnp.add, terms_real))
        rows_imaginary.append(reduce(jnp.add, terms_imaginary))
    return jnp.stack([jnp.stack(rows_real, 1), jnp.stack(rows_imaginary, 1)], 1)


def spin_outer(upper_spinor, lower_spinor):
    upper_real = upper_spinor[:, 0][:, :, :, None]
    upper_imaginary = upper_spinor[:, 1][:, :, :, None]
    lower_real = lower_spinor[:, 0][:, :, None]
    lower_imaginary = lower_spinor[:, 1][:, :, None]
    real_part = jnp.sum(upper_real * lower_real + upper_imaginary * lower_imaginary, axis=(0, 1))
    imaginary_part = jnp.sum(
        upper_imaginary * lower_real - upper_real * lower_imaginary, axis=(0, 1)
    )
    return jnp.stack([real_part, imaginary_part])


def traceless_part(matrix):
    real_part = 0.5 * (matrix[0] - jnp.swapaxes(matrix[0], 0, 1))
    imaginary_part = 0.5 * (matrix[1] + jnp.swapaxes(matrix[1], 0, 1))
    trace_third = (imaginary_part[0, 0] + imaginary_part[1, 1] + imaginary_part[2, 2]) / 3.0
    identity = jnp.eye(3, dtype=matrix.dtype).reshape((3, 3) + (1,) * (matrix.ndim - 3))
    imaginary_part = imaginary_part - identity * trace_third
    return jnp.stack([real_part, imaginary_part])


def on_device(links, solutions):
    time_block = links.shape[4]
    depth_block = links.shape[5]
    row_count = links.shape[6] // Y_LEN
    link_box = padded_2(links, (("ta", 4), ("gz", 5)), 1)
    link_box = padded_2(link_box, (("xy", 6),), Y_LEN)
    time_rank = lax.axis_index("ta")
    time_ranks = lax.axis_size("ta")
    projector_list = projectors()
    zero_anchor = (0, 0, 0)
    force_extent = (time_block, depth_block, row_count)
    flat_shape = solutions.shape
    grid_shape = solutions.shape[:4] + (time_block, depth_block, row_count, Y_LEN)
    grid = solutions.reshape(grid_shape)
    face_box = padded_3(grid, (("ta", 4), ("gz", 5), ("xy", 6)), 1)
    positions = lax.iota(jnp.int32, time_block + 2)
    flipped = (positions == 0) & (time_rank == 0) | (positions == time_block + 1) & (
        time_rank == time_ranks - 1
    )
    factor = jnp.where(flipped, -1.0, 1.0).astype(face_box.dtype)
    face_box = face_box * factor[:, None, None, None]
    hop_terms = []
    for direction in range(4):
        minus_projector, plus_projector = projector_list[direction]
        behind_anchor, behind_stride = offset(direction, -1)
        link_here = window(link_box[direction], 1, zero_anchor, force_extent, 0)
        forward = colour_apply(
            link_here, spin_apply(minus_projector, face_window(face_box, direction, 1, flat_shape))
        )
        link_behind = window(link_box[direction], 1, behind_anchor, force_extent, behind_stride)
        backward = colour_apply(
            dagger(link_behind),
            spin_apply(plus_projector, face_window(face_box, direction, -1, flat_shape)),
        )
        hop_terms.append(forward + backward)
    partner_here = solutions - HOPPING * reduce(jnp.add, hop_terms)
    partner_grid = partner_here.reshape(grid_shape)
    time_face = shifted(partner_grid[..., 0:1, :, :, :], "ta", -1)
    time_face = time_face * jnp.where(time_rank == time_ranks - 1, -1.0, 1.0).astype(
        time_face.dtype
    )
    depth_face = shifted(partner_grid[..., :, 0:1, :, :], "gz", -1)
    row_face = shifted(partner_grid[..., :, :, 0:1, :], "xy", -1)
    ahead_partner = [
        jnp.concatenate([partner_grid[..., 1:, :, :, :], time_face], axis=4).reshape(flat_shape),
        jnp.concatenate([partner_grid[..., :, 1:, :, :], depth_face], axis=5).reshape(flat_shape),
        jnp.concatenate([partner_grid[..., :, :, 1:, :], row_face], axis=6).reshape(flat_shape),
        jnp.roll(partner_grid, -1, -1).reshape(flat_shape),
    ]
    ahead_solution = [face_window(face_box, direction, 1, flat_shape) for direction in range(4)]
    forces = []
    for direction in range(4):
        minus_projector, plus_projector = projector_list[direction]
        ahead_anchor, ahead_stride = offset(direction, 1)
        link_main = window(link_box[direction], 1, zero_anchor, force_extent, 0)
        pieces = []
        for second in range(4):
            if second == direction:
                continue
            side_anchor, side_stride = offset(second, 1)
            back_anchor, back_stride = offset(second, -1)
            link_second = window(link_box[second], 1, zero_anchor, force_extent, 0)
            upper_staple = matrix_product(
                matrix_product(
                    window(link_box[second], 1, ahead_anchor, force_extent, ahead_stride),
                    dagger(window(link_box[direction], 1, side_anchor, force_extent, side_stride)),
                ),
                dagger(link_second),
            )
            shifted_back = window(link_box[second], 1, back_anchor, force_extent, back_stride)
            corner_link = window(
                link_box[second],
                1,
                combine(ahead_anchor, back_anchor),
                force_extent,
                ahead_stride + back_stride,
            )
            lower_staple = matrix_product(
                matrix_product(
                    dagger(corner_link),
                    dagger(window(link_box[direction], 1, back_anchor, force_extent, back_stride)),
                ),
                shifted_back,
            )
            pieces.append(upper_staple + lower_staple)
        staple = reduce(jnp.add, pieces)
        fermion = spin_outer(
            spin_apply(minus_projector, ahead_solution[direction]), partner_here
        ) + spin_outer(spin_apply(plus_projector, ahead_partner[direction]), solutions)
        forces.append(
            traceless_part(matrix_product(link_main, PLAQUETTE * staple + HOPPING * fermion))
        )
    return jnp.stack(forces)


def solution(mesh):
    return jax.shard_map(
        on_device,
        mesh=mesh,
        in_specs=(
            P(None, None, None, None, "ta", "gz", "xy"),
            P(None, None, None, None, "ta", "gz", "xy"),
        ),
        out_specs=P(None, None, None, None, "ta", "gz", "xy"),
        check_vma=False,
    )
```

profile of v0, /device:TPU:1, one launch (start us, length us, event | category | flops | bytes accessed | tf_op | source)
XLA Modules:
  0.0 164.8 jit_solution(7081603856449533949)
XLA Ops:
  0.0 1.1 reshape.304
  1.3 14.1 %collective-permute-start.11 = (f32[2,2,4,3,2,2,1,64]{7,6,5,4,3,2,0,1:T(1,128)S(1)}, f32[2,2,4,3,2,2,1,64]{7,6,5,4,3,2,0,1:T(1,128)S(1)}, u32[]{:S(2)}, u32[]{:S(2)}) collective-permute-start(f32[2,2,4,3,2,2,1,64]{7,6,5,4,3,2,0,1:T(1,128)S(1)} %get-tuple-element.355), channel_id=1, source_target_pairs={{1,0},{2,1},{3,2},{4,3},{5,4},{6,5},{7,6},{0,7},{9,8},{10,9},{11,1... | collective-permute-start | bytes 147464 | tf_op jit(solution)/shard_map/ppermute | solution.py:38
  15.5 10.1 %collective-permute-start.10 = (f32[2,2,4,3,2,1,2,64]{7,6,5,4,3,2,0,1:T(2,128)S(1)}, f32[2,2,4,3,2,1,2,64]{7,6,5,4,3,2,0,1:T(2,128)S(1)}, u32[]{:S(2)}, u32[]{:S(2)}) collective-permute-start(f32[2,2,4,3,2,1,2,64]{7,6,5,4,3,2,0,1:T(2,128)S(1)} %get-tuple-element.357), channel_id=1, source_target_pairs={{8,0},{16,8},{24,16},{0,24},{9,1},{17,9},{25,17},{1,25},{10,2},{18... | collective-permute-start | bytes 147464 | tf_op jit(solution)/shard_map/ppermute | solution.py:38
  25.6 3.9 %collective-permute-start.7 = (f32[2,2,4,3,2,1,2,64]{7,6,5,4,3,2,0,1:T(2,128)S(1)}, f32[2,2,4,3,2,1,2,64]{7,6,5,4,3,2,0,1:T(2,128)S(1)}, u32[]{:S(2)}, u32[]{:S(2)}) collective-permute-start(f32[2,2,4,3,2,1,2,64]{7,6,5,4,3,2,0,1:T(2,128)S(1)} %get-tuple-element.356), channel_id=1, source_target_pairs={{0,8},{8,16},{16,24},{24,0},{1,9},{9,17},{17,25},{25,1},{2,10},{10... | collective-permute-start | bytes 147464 | tf_op jit(solution)/shard_map/ppermute | solution.py:37
  29.6 7.3 %collective-permute-start.9 = (f32[2,2,4,3,1,2,2,64]{7,6,5,4,3,2,0,1:T(2,128)S(1)}, f32[2,2,4,3,1,2,2,64]{7,6,5,4,3,2,0,1:T(2,128)S(1)}, u32[]{:S(2)}, u32[]{:S(2)}) collective-permute-start(f32[2,2,4,3,1,2,2,64]{7,6,5,4,3,2,0,1:T(2,128)S(1)} %get-tuple-element.353), channel_id=1, source_target_pairs={{32,0},{64,32},{96,64},{128,96},{160,128},{192,160},{224,192},{256... | collective-permute-start | bytes 147464 | tf_op jit(solution)/shard_map/ppermute | solution.py:38
  39.4 1.9 %collective-permute-start.8 = (f32[2,2,4,3,1,2,2,64]{7,6,5,4,3,2,0,1:T(2,128)S(1)}, f32[2,2,4,3,1,2,2,64]{7,6,5,4,3,2,0,1:T(2,128)S(1)}, u32[]{:S(2)}, u32[]{:S(2)}) collective-permute-start(f32[2,2,4,3,1,2,2,64]{7,6,5,4,3,2,0,1:T(2,128)S(1)} %get-tuple-element.352), channel_id=1, source_target_pairs={{0,32},{32,64},{64,96},{96,128},{128,160},{160,192},{192,224},{224... | collective-permute-start | bytes 147464 | tf_op jit(solution)/shard_map/ppermute | solution.py:37
  41.4 1.9 %collective-permute-start = (f32[4,2,3,3,1,2,128]{6,5,4,3,2,1,0:T(2,128)S(1)}, f32[4,2,3,3,1,2,128]{6,5,4,3,2,1,0:T(2,128)S(1)}, u32[]{:S(2)}, u32[]{:S(2)}) collective-permute-start(f32[4,2,3,3,1,2,128]{6,5,4,3,2,1,0:T(2,128)S(1)} %get-tuple-element.359), channel_id=1, source_target_pairs={{0,32},{32,64},{64,96},{96,128},{128,160},{160,192},{192,224},{224... | collective-permute-start | bytes 221192 | tf_op jit(solution)/shard_map/ppermute | solution.py:23
  43.4 15.2 %collective-permute-start.1 = (f32[4,2,3,3,1,2,128]{6,5,4,3,2,1,0:T(2,128)S(1)}, f32[4,2,3,3,1,2,128]{6,5,4,3,2,1,0:T(2,128)S(1)}, u32[]{:S(2)}, u32[]{:S(2)}) collective-permute-start(f32[4,2,3,3,1,2,128]{6,5,4,3,2,1,0:T(2,128)S(1)} %get-tuple-element.358), channel_id=1, source_target_pairs={{32,0},{64,32},{96,64},{128,96},{160,128},{192,160},{224,192},{256... | collective-permute-start | bytes 221192 | tf_op jit(solution)/shard_map/ppermute | solution.py:24
  58.6 0.9 fusion.4
  65.1 11.7 %collective-permute-start.3 = (f32[4,2,3,3,4,1,128]{6,5,4,3,2,1,0:T(1,128)S(1)}, f32[4,2,3,3,4,1,128]{6,5,4,3,2,1,0:T(1,128)S(1)}, u32[]{:S(2)}, u32[]{:S(2)}) collective-permute-start(f32[4,2,3,3,4,1,128]{6,5,4,3,2,1,0:T(1,128)S(1)} %get-tuple-element.345), channel_id=1, source_target_pairs={{8,0},{16,8},{24,16},{0,24},{9,1},{17,9},{25,17},{1,25},{10,2},{18... | collective-permute-start | bytes 442376 | tf_op jit(solution)/shard_map/ppermute | solution.py:24
  76.8 2.5 %collective-permute-start.2 = (f32[4,2,3,3,4,1,128]{6,5,4,3,2,1,0:T(1,128)S(1)}, f32[4,2,3,3,4,1,128]{6,5,4,3,2,1,0:T(1,128)S(1)}, u32[]{:S(2)}, u32[]{:S(2)}) collective-permute-start(f32[4,2,3,3,4,1,128]{6,5,4,3,2,1,0:T(1,128)S(1)} %get-tuple-element.344), channel_id=1, source_target_pairs={{0,8},{8,16},{16,24},{24,0},{1,9},{9,17},{17,25},{25,1},{2,10},{10... | collective-permute-start | bytes 442376 | tf_op jit(solution)/shard_map/ppermute | solution.py:23
  79.7 18.1 %collective-permute-done.3 = f32[4,2,3,3,4,1,128]{6,5,4,3,2,1,0:T(1,128)S(1)} collective-permute-done((f32[4,2,3,3,4,1,128]{6,5,4,3,2,1,0:T(1,128)S(1)}, f32[4,2,3,3,4,1,128]{6,5,4,3,2,1,0:T(1,128)S(1)}, u32[]{:S(2)}, u32[]{:S(2)}) %collective-permute-start.3) | collective-permute-done | bytes 147488 | tf_op jit(solution)/shard_map/ppermute | solution.py:24
  97.8 6.3 %collective-permute-done.2 = f32[4,2,3,3,4,1,128]{6,5,4,3,2,1,0:T(1,128)S(1)} collective-permute-done((f32[4,2,3,3,4,1,128]{6,5,4,3,2,1,0:T(1,128)S(1)}, f32[4,2,3,3,4,1,128]{6,5,4,3,2,1,0:T(1,128)S(1)}, u32[]{:S(2)}, u32[]{:S(2)}) %collective-permute-start.2) | collective-permute-done | bytes 147488 | tf_op jit(solution)/shard_map/ppermute | solution.py:23
  105.6 2.4 %collective-permute-start.4 = (f32[4,2,3,3,4,4,64]{6,5,4,3,2,1,0:T(4,128)S(1)}, f32[4,2,3,3,4,4,64]{6,5,4,3,2,1,0:T(4,128)S(1)}, u32[]{:S(2)}, u32[]{:S(2)}) collective-permute-start(f32[4,2,3,3,4,4,64]{6,5,4,3,2,1,0:T(4,128)S(1)} %get-tuple-element.199), channel_id=1, source_target_pairs={{0,1},{1,2},{2,3},{3,4},{4,5},{5,6},{6,7},{7,0},{8,9},{9,10},{10,1... | collective-permute-start | bytes 884744 | tf_op jit(solution)/shard_map/ppermute | solution.py:23
  108.0 7.7 %collective-permute-done.5 = f32[4,2,3,3,4,4,64]{6,5,4,3,2,1,0:T(4,128)S(1)} collective-permute-done((f32[4,2,3,3,4,4,64]{6,5,4,3,2,1,0:T(4,128)S(1)}, f32[4,2,3,3,4,4,64]{6,5,4,3,2,1,0:T(4,128)S(1)}, u32[]{:S(2)}, u32[]{:S(2)}) %collective-permute-start.5) | collective-permute-done | bytes 294944 | tf_op jit(solution)/shard_map/ppermute | solution.py:24
  115.8 2.2 %pad_maximum_fusion = f32[4,2,3,3,4,4,256]{6,5,4,3,2,1,0:T(4,128)S(1)} fusion(f32[4,2,3,3,4,4,64]{6,5,4,3,2,1,0:T(4,128)S(1)} %collective-permute-done.5, f32[4,2,3,3,4,1,128]{6,5,4,3,2,1,0:T(1,128)S(1)} %collective-permute-done.3, f32[4,2,3,3,4,2,128]{6,5,4,3,2,1,0:T(2,128)S(1)} %constant_dynamic-update-slice_fusion, ...), kind=kLoop, calls=%fused_computation.15 | loop fusion | flops 1179648 | bytes 2359296 | tf_op jit(solution)/shard_map/concatenate | solution.py:25
  120.7 0.9 slice_bitcast_fusion.104
  125.7 1.0 slice_bitcast_fusion.85
  130.1 1.0 maximum_select_fusion.12
  132.3 1.0 maximum_select_fusion.9
  133.5 3.0 %collective-permute-start.12 = (f32[2,2,4,3,1,2,2,64]{7,6,5,4,3,2,0,1:T(2,128)S(1)}, f32[2,2,4,3,1,2,2,64]{7,6,5,4,3,2,0,1:T(2,128)S(1)}, u32[]{:S(2)}, u32[]{:S(2)}) collective-permute-start(f32[2,2,4,3,1,2,2,64]{7,6,5,4,3,2,0,1:T(2,128)S(1)} %copy.384), channel_id=1, source_target_pairs={{0,992},{32,0},{64,32},{96,64},{128,96},{160,128},{192,160},{224,1... | collective-permute-start | bytes 147464 | tf_op jit(solution)/shard_map/ppermute | solution.py:51
  136.5 8.0 %collective-permute-start.13 = (f32[2,2,4,3,2,1,2,64]{7,6,5,4,3,2,0,1:T(2,128)S(1)}, f32[2,2,4,3,2,1,2,64]{7,6,5,4,3,2,0,1:T(2,128)S(1)}, u32[]{:S(2)}, u32[]{:S(2)}) collective-permute-start(f32[2,2,4,3,2,1,2,64]{7,6,5,4,3,2,0,1:T(2,128)S(1)} %copy.386), channel_id=1, source_target_pairs={{0,24},{8,0},{16,8},{24,16},{1,25},{9,1},{17,9},{25,17},{2,26},{10... | collective-permute-start | bytes 147464 | tf_op jit(solution)/shard_map/ppermute | solution.py:51
  144.7 0.9 collective-permute-start.14
  145.7 1.3 add_reduce_fusion.7
  (373 shorter events, 37.7 us)
Async XLA Ops:
  0.0 38.8 %copy-start.1 = (f32[4,2,3,3,2,2,128]{6,5,4,3,2,1,0:T(2,128)S(1)}, f32[4,2,3,3,2,2,128]{6,5,4,3,2,1,0:T(2,128)}, u32[]{:S(2)}) copy-start(f32[4,2,3,3,2,2,128]{6,5,4,3,2,1,0:T(2,128)} %param.2) | copy-start | bytes 442372
  1.3 38.1 %collective-permute-start.11 = (f32[2,2,4,3,2,2,1,64]{7,6,5,4,3,2,0,1:T(1,128)S(1)}, f32[2,2,4,3,2,2,1,64]{7,6,5,4,3,2,0,1:T(1,128)S(1)}, u32[]{:S(2)}, u32[]{:S(2)}) collective-permute-start(f32[2,2,4,3,2,2,1,64]{7,6,5,4,3,2,0,1:T(1,128)S(1)} %get-tuple-element.355), channel_id=1, source_target_pairs={{1,0},{2,1},{3,2},{4,3},{5,4},{6,5},{7,6},{0,7},{9,8},{10,9},{11,1... | collective-permute-start | bytes 147464 | tf_op jit(solution)/shard_map/ppermute | solution.py:38
  15.5 25.9 %collective-permute-start.10 = (f32[2,2,4,3,2,1,2,64]{7,6,5,4,3,2,0,1:T(2,128)S(1)}, f32[2,2,4,3,2,1,2,64]{7,6,5,4,3,2,0,1:T(2,128)S(1)}, u32[]{:S(2)}, u32[]{:S(2)}) collective-permute-start(f32[2,2,4,3,2,1,2,64]{7,6,5,4,3,2,0,1:T(2,128)S(1)} %get-tuple-element.357), channel_id=1, source_target_pairs={{8,0},{16,8},{24,16},{0,24},{9,1},{17,9},{25,17},{1,25},{10,2},{18... | collective-permute-start | bytes 147464 | tf_op jit(solution)/shard_map/ppermute | solution.py:38
  25.6 17.8 %collective-permute-start.7 = (f32[2,2,4,3,2,1,2,64]{7,6,5,4,3,2,0,1:T(2,128)S(1)}, f32[2,2,4,3,2,1,2,64]{7,6,5,4,3,2,0,1:T(2,128)S(1)}, u32[]{:S(2)}, u32[]{:S(2)}) collective-permute-start(f32[2,2,4,3,2,1,2,64]{7,6,5,4,3,2,0,1:T(2,128)S(1)} %get-tuple-element.356), channel_id=1, source_target_pairs={{0,8},{8,16},{16,24},{24,0},{1,9},{9,17},{17,25},{25,1},{2,10},{10... | collective-permute-start | bytes 147464 | tf_op jit(solution)/shard_map/ppermute | solution.py:37
  29.5 29.1 %collective-permute-start.6 = (f32[2,2,4,3,2,2,1,64]{7,6,5,4,3,2,0,1:T(1,128)S(1)}, f32[2,2,4,3,2,2,1,64]{7,6,5,4,3,2,0,1:T(1,128)S(1)}, u32[]{:S(2)}, u32[]{:S(2)}) collective-permute-start(f32[2,2,4,3,2,2,1,64]{7,6,5,4,3,2,0,1:T(1,128)S(1)} %get-tuple-element.354), channel_id=1, source_target_pairs={{0,1},{1,2},{2,3},{3,4},{4,5},{5,6},{6,7},{7,0},{8,9},{9,10},{10,1... | collective-permute-start | bytes 147464 | tf_op jit(solution)/shard_map/ppermute | solution.py:37
  29.6 29.0 %collective-permute-start.9 = (f32[2,2,4,3,1,2,2,64]{7,6,5,4,3,2,0,1:T(2,128)S(1)}, f32[2,2,4,3,1,2,2,64]{7,6,5,4,3,2,0,1:T(2,128)S(1)}, u32[]{:S(2)}, u32[]{:S(2)}) collective-permute-start(f32[2,2,4,3,1,2,2,64]{7,6,5,4,3,2,0,1:T(2,128)S(1)} %get-tuple-element.353), channel_id=1, source_target_pairs={{32,0},{64,32},{96,64},{128,96},{160,128},{192,160},{224,192},{256... | collective-permute-start | bytes 147464 | tf_op jit(solution)/shard_map/ppermute | solution.py:38
  39.4 19.1 %collective-permute-start.8 = (f32[2,2,4,3,1,2,2,64]{7,6,5,4,3,2,0,1:T(2,128)S(1)}, f32[2,2,4,3,1,2,2,64]{7,6,5,4,3,2,0,1:T(2,128)S(1)}, u32[]{:S(2)}, u32[]{:S(2)}) collective-permute-start(f32[2,2,4,3,1,2,2,64]{7,6,5,4,3,2,0,1:T(2,128)S(1)} %get-tuple-element.352), channel_id=1, source_target_pairs={{0,32},{32,64},{64,96},{96,128},{128,160},{160,192},{192,224},{224... | collective-permute-start | bytes 147464 | tf_op jit(solution)/shard_map/ppermute | solution.py:37
  41.4 23.3 %collective-permute-start = (f32[4,2,3,3,1,2,128]{6,5,4,3,2,1,0:T(2,128)S(1)}, f32[4,2,3,3,1,2,128]{6,5,4,3,2,1,0:T(2,128)S(1)}, u32[]{:S(2)}, u32[]{:S(2)}) collective-permute-start(f32[4,2,3,3,1,2,128]{6,5,4,3,2,1,0:T(2,128)S(1)} %get-tuple-element.359), channel_id=1, source_target_pairs={{0,32},{32,64},{64,96},{96,128},{128,160},{160,192},{192,224},{224... | collective-permute-start | bytes 221192 | tf_op jit(solution)/shard_map/ppermute | solution.py:23
  43.4 21.5 %collective-permute-start.1 = (f32[4,2,3,3,1,2,128]{6,5,4,3,2,1,0:T(2,128)S(1)}, f32[4,2,3,3,1,2,128]{6,5,4,3,2,1,0:T(2,128)S(1)}, u32[]{:S(2)}, u32[]{:S(2)}) collective-permute-start(f32[4,2,3,3,1,2,128]{6,5,4,3,2,1,0:T(2,128)S(1)} %get-tuple-element.358), channel_id=1, source_target_pairs={{32,0},{64,32},{96,64},{128,96},{160,128},{192,160},{224,192},{256... | collective-permute-start | bytes 221192 | tf_op jit(solution)/shard_map/ppermute | solution.py:24
  65.1 32.7 %collective-permute-start.3 = (f32[4,2,3,3,4,1,128]{6,5,4,3,2,1,0:T(1,128)S(1)}, f32[4,2,3,3,4,1,128]{6,5,4,3,2,1,0:T(1,128)S(1)}, u32[]{:S(2)}, u32[]{:S(2)}) collective-permute-start(f32[4,2,3,3,4,1,128]{6,5,4,3,2,1,0:T(1,128)S(1)} %get-tuple-element.345), channel_id=1, source_target_pairs={{8,0},{16,8},{24,16},{0,24},{9,1},{17,9},{25,17},{1,25},{10,2},{18... | collective-permute-start | bytes 442376 | tf_op jit(solution)/shard_map/ppermute | solution.py:24
  76.8 27.3 %collective-permute-start.2 = (f32[4,2,3,3,4,1,128]{6,5,4,3,2,1,0:T(1,128)S(1)}, f32[4,2,3,3,4,1,128]{6,5,4,3,2,1,0:T(1,128)S(1)}, u32[]{:S(2)}, u32[]{:S(2)}) collective-permute-start(f32[4,2,3,3,4,1,128]{6,5,4,3,2,1,0:T(1,128)S(1)} %get-tuple-element.344), channel_id=1, source_target_pairs={{0,8},{8,16},{16,24},{24,0},{1,9},{9,17},{17,25},{25,1},{2,10},{10... | collective-permute-start | bytes 442376 | tf_op jit(solution)/shard_map/ppermute | solution.py:23
  104.9 10.9 %collective-permute-start.5 = (f32[4,2,3,3,4,4,64]{6,5,4,3,2,1,0:T(4,128)S(1)}, f32[4,2,3,3,4,4,64]{6,5,4,3,2,1,0:T(4,128)S(1)}, u32[]{:S(2)}, u32[]{:S(2)}) collective-permute-start(f32[4,2,3,3,4,4,64]{6,5,4,3,2,1,0:T(4,128)S(1)} %get-tuple-element.200), channel_id=1, source_target_pairs={{1,0},{2,1},{3,2},{4,3},{5,4},{6,5},{7,6},{0,7},{9,8},{10,9},{11,1... | collective-permute-start | bytes 884744 | tf_op jit(solution)/shard_map/ppermute | solution.py:24
  105.6 10.2 %collective-permute-start.4 = (f32[4,2,3,3,4,4,64]{6,5,4,3,2,1,0:T(4,128)S(1)}, f32[4,2,3,3,4,4,64]{6,5,4,3,2,1,0:T(4,128)S(1)}, u32[]{:S(2)}, u32[]{:S(2)}) collective-permute-start(f32[4,2,3,3,4,4,64]{6,5,4,3,2,1,0:T(4,128)S(1)} %get-tuple-element.199), channel_id=1, source_target_pairs={{0,1},{1,2},{2,3},{3,4},{4,5},{5,6},{6,7},{7,0},{8,9},{9,10},{10,1... | collective-permute-start | bytes 884744 | tf_op jit(solution)/shard_map/ppermute | solution.py:23
  133.4 21.4 %copy-start.22 = (f32[3,3,2,2,128]{4,3,2,0,1:T(2,128)S(1)}, f32[3,3,2,2,128]{4,3,2,0,1:T(2,128)}, u32[]{:S(2)}) copy-start(f32[3,3,2,2,128]{4,3,2,0,1:T(2,128)} %get-tuple-element.299) | copy-start | bytes 55300
  133.4 21.4 %copy-start.25 = (f32[3,3,2,2,128]{4,3,2,1,0:T(2,128)S(1)}, f32[3,3,2,2,128]{4,3,2,1,0:T(2,128)}, u32[]{:S(2)}) copy-start(f32[3,3,2,2,128]{4,3,2,1,0:T(2,128)} %get-tuple-element.338) | copy-start | bytes 55300
  133.4 21.4 %copy-start.26 = (f32[3,3,2,2,128]{4,3,2,1,0:T(2,128)S(1)}, f32[3,3,2,2,128]{4,3,2,1,0:T(2,128)}, u32[]{:S(2)}) copy-start(f32[3,3,2,2,128]{4,3,2,1,0:T(2,128)} %get-tuple-element.339) | copy-start | bytes 55300
  133.4 21.5 %copy-start.23 = (f32[3,3,2,2,128]{4,3,2,1,0:T(2,128)S(1)}, f32[3,3,2,2,128]{4,3,2,1,0:T(2,128)}, u32[]{:S(2)}) copy-start(f32[3,3,2,2,128]{4,3,2,1,0:T(2,128)} %get-tuple-element.334) | copy-start | bytes 55300
  133.4 21.5 %copy-start.24 = (f32[3,3,2,2,128]{4,3,2,1,0:T(2,128)S(1)}, f32[3,3,2,2,128]{4,3,2,1,0:T(2,128)}, u32[]{:S(2)}) copy-start(f32[3,3,2,2,128]{4,3,2,1,0:T(2,128)} %get-tuple-element.335) | copy-start | bytes 55300
  133.4 21.5 %copy-start.27 = (f32[3,3,2,2,128]{4,3,2,0,1:T(2,128)S(1)}, f32[3,3,2,2,128]{4,3,2,0,1:T(2,128)}, u32[]{:S(2)}) copy-start(f32[3,3,2,2,128]{4,3,2,0,1:T(2,128)} %get-tuple-element.276) | copy-start | bytes 55300
  133.5 21.5 %copy-start.29 = (f32[3,3,2,2,128]{4,3,2,0,1:T(2,128)S(1)}, f32[3,3,2,2,128]{4,3,2,0,1:T(2,128)}, u32[]{:S(2)}) copy-start(f32[3,3,2,2,128]{4,3,2,0,1:T(2,128)} %get-tuple-element.297) | copy-start | bytes 55300
  133.5 21.5 %copy-start.30 = (f32[3,3,2,2,128]{4,3,2,0,1:T(2,128)S(1)}, f32[3,3,2,2,128]{4,3,2,0,1:T(2,128)}, u32[]{:S(2)}) copy-start(f32[3,3,2,2,128]{4,3,2,0,1:T(2,128)} %get-tuple-element.529) | copy-start | bytes 55300
  133.5 26.4 %collective-permute-start.12 = (f32[2,2,4,3,1,2,2,64]{7,6,5,4,3,2,0,1:T(2,128)S(1)}, f32[2,2,4,3,1,2,2,64]{7,6,5,4,3,2,0,1:T(2,128)S(1)}, u32[]{:S(2)}, u32[]{:S(2)}) collective-permute-start(f32[2,2,4,3,1,2,2,64]{7,6,5,4,3,2,0,1:T(2,128)S(1)} %copy.384), channel_id=1, source_target_pairs={{0,992},{32,0},{64,32},{96,64},{128,96},{160,128},{192,160},{224,1... | collective-permute-start | bytes 147464 | tf_op jit(solution)/shard_map/ppermute | solution.py:51
  136.5 23.8 %collective-permute-start.13 = (f32[2,2,4,3,2,1,2,64]{7,6,5,4,3,2,0,1:T(2,128)S(1)}, f32[2,2,4,3,2,1,2,64]{7,6,5,4,3,2,0,1:T(2,128)S(1)}, u32[]{:S(2)}, u32[]{:S(2)}) collective-permute-start(f32[2,2,4,3,2,1,2,64]{7,6,5,4,3,2,0,1:T(2,128)S(1)} %copy.386), channel_id=1, source_target_pairs={{0,24},{8,0},{16,8},{24,16},{1,25},{9,1},{17,9},{25,17},{2,26},{10... | collective-permute-start | bytes 147464 | tf_op jit(solution)/shard_map/ppermute | solution.py:51
  144.7 16.2 %collective-permute-start.14 = (f32[2,2,4,3,2,2,1,64]{7,6,5,4,3,2,0,1:T(1,128)S(1)}, f32[2,2,4,3,2,2,1,64]{7,6,5,4,3,2,0,1:T(1,128)S(1)}, u32[]{:S(2)}, u32[]{:S(2)}) collective-permute-start(f32[2,2,4,3,2,2,1,64]{7,6,5,4,3,2,0,1:T(1,128)S(1)} %copy.388), channel_id=1, source_target_pairs={{0,7},{1,0},{2,1},{3,2},{4,3},{5,4},{6,5},{7,6},{8,15},{9,8},{10,9... | collective-permute-start | bytes 147464 | tf_op jit(solution)/shard_map/ppermute | solution.py:51
  (49 other events, 552.0 us)
where the time goes:
time: 166 us; the launch traced here: 165 us
  starting transfers between devices  83.6 us (50%)
  other arithmetic  34.4 us (21%)
  waiting for transfers between devices  32.2 us (19%)
  local copies, waits for them, and re-layouts  12.2 us (7%)
  between operations  2.44 us (1%)
    ppermute x3, starting transfers between devices, padded_3(): lax.ppermute(initial, axis, [(b, a) for a, b in up])  31.5 us
    ppermute x3, starting transfers between devices, padded_2(): after = lax.ppermute(initial, axis, down)  27.5 us
    ppermute x3, waiting for transfers between devices, padded_2(): after = lax.ppermute(initial, axis, down)  25.8 us
    reduce_sum x33, other arithmetic, matrix_product(): jnp.sum(left_real[:, :, None] * right_real[None] - left_imaginary[:, :, N...  12.5 us
    ppermute x3, starting transfers between devices, shifted(): lax.ppermute(x, axis, [(i, (i + by) % length) for i in range(length)])  12 us
    ppermute x3, starting transfers between devices, padded_2(): before = lax.ppermute(last, axis, up)  6.76 us
    ppermute x3, waiting for transfers between devices, padded_2(): before = lax.ppermute(last, axis, up)  6.35 us
    ppermute x3, starting transfers between devices, padded_3(): lax.ppermute(last, axis, up)  5.83 us
  transfers between devices with their start and end apart: 15, of which 3 were waited for; matrix products, arithmetic and copies ran while one was open for 14% of the time, Pallas kernels for 0%

commit v1 on v0

v1 whole, which is shorter than its diff:
```python
import jax
import jax.numpy as jnp
from jax import lax
from jax.experimental import pallas as pl
from jax.experimental.pallas import tpu as pltpu
from jax.sharding import PartitionSpec as P


HOPPING = 0.125
PLAQUETTE = 0.5
INTERPRET = False

BLOCKS = (
    ((0, 1), (1, 1)),
    ((0, 1j), (1, -1j)),
    ((1, 1j), (0, 1j)),
    ((1, -1), (0, 1)),
)
T, Z, R, Y = 0, 1, 2, 3
OFF = ((0, 1), (0, 2), (1, 2))
ROWS = tuple((a, b) for a in range(2) for b in range(3))
SPINS = tuple((n, s, c) for n in range(2) for s in range(2) for c in range(3))


def add_phase(a, phase, b):
    if phase == 1:
        return (a[0] + b[0], a[1] + b[1])
    if phase == -1:
        return (a[0] - b[0], a[1] - b[1])
    if phase == 1j:
        return (a[0] - b[1], a[1] + b[0])
    return (a[0] + b[1], a[1] - b[0])


def cmul(a, b):
    return (a[0] * b[0] - a[1] * b[1], a[0] * b[1] + a[1] * b[0])


def cmulc(a, b):
    return (a[0] * b[0] + a[1] * b[1], a[1] * b[0] - a[0] * b[1])


def conj(a):
    return (a[0], -a[1])


def csum(terms):
    re, im = terms[0]
    for t in terms[1:]:
        re, im = re + t[0], im + t[1]
    return (re, im)


def csub(a, b):
    return (a[0] - b[0], a[1] - b[1])


def matmul(left, right):
    return [[csum([cmul(left[a][k], right[k][b]) for k in range(3)]) for b in range(3)] for a in range(3)]


def matmul_dagger(left, right):
    return [[csum([cmulc(left[a][k], right[b][k]) for k in range(3)]) for b in range(3)] for a in range(3)]


def third_row(m):
    u, v = m
    cross = lambda i, j: conj(csub(cmul(u[i], v[j]), cmul(u[j], v[i])))
    return [u, v, [cross(1, 2), cross(2, 0), cross(0, 1)]]


def antihermitian(m, scale):
    out = []
    for a, b in OFF:
        out.append((0.5 * scale) * (m[a][b][0] - m[b][a][0]))
        out.append((0.5 * scale) * (m[a][b][1] + m[b][a][1]))
    third = (m[0][0][1] + m[1][1][1] + m[2][2][1]) * (1.0 / 3.0)
    out.append(scale * (m[0][0][1] - third))
    out.append(scale * (m[1][1][1] - third))
    return out


def transport(x, w):
    e = {}
    for i, (a, b) in enumerate(OFF):
        e[a, b] = (x[2 * i], x[2 * i + 1])
        e[b, a] = (-x[2 * i], x[2 * i + 1])
    d = (x[6], x[7], -(x[6] + x[7]))
    v = []
    for a in range(3):
        row = []
        for j in range(3):
            terms = [(-d[a] * w[a][j][1], d[a] * w[a][j][0])]
            terms += [cmul(e[a, b], w[b][j]) for b in range(3) if b != a]
            row.append(csum(terms))
        v.append(row)
    out = []
    for i, j in OFF:
        t = csum([cmulc(v[a][j], w[a][i]) for a in range(3)])
        out += [t[0], t[1]]
    for i in range(2):
        s = None
        for a in range(3):
            p = v[a][i][1] * w[a][i][0] - v[a][i][0] * w[a][i][1]
            s = p if s is None else s + p
        out.append(s)
    return out


class Sites:
    def __init__(self):
        rows = lax.broadcasted_iota(jnp.int32, (4, 128), 0)
        lanes = lax.broadcasted_iota(jnp.int32, (4, 128), 1)
        self.first = (rows < 2, rows % 2 == 0, lanes < 64)
        self.y_last = lanes % 64 == 63
        self.y_first = lanes % 64 == 0

    def swap(self, v, d):
        if d == R:
            return pltpu.roll(v, 64, 1)
        if d == T:
            return jnp.concatenate([v[2:4], v[0:2]], axis=0)
        return jnp.where(
            self.first[Z],
            jnp.concatenate([v[1:4], v[0:1]], axis=0),
            jnp.concatenate([v[3:4], v[0:3]], axis=0),
        )

    def pack_low(self, a, b, d):
        return jnp.where(self.first[d], a, self.swap(b, d))

    def pack_high(self, a, b, d):
        return jnp.where(self.first[d], self.swap(b, d), a)

    def ahead(self, a, b, m, d):
        return (
            self.swap(jnp.where(self.first[d], m, a), d),
            jnp.where(self.first[d], self.swap(b, d), m),
        )

    def behind(self, a, b, m, d):
        return (
            self.swap(jnp.where(self.first[d], a, m), d),
            jnp.where(self.first[d], m, self.swap(b, d)),
        )

    def y_ahead(self, v):
        return jnp.where(self.y_last, pltpu.roll(v, 63, 1), pltpu.roll(v, 127, 1))

    def y_behind(self, v):
        return jnp.where(self.y_first, pltpu.roll(v, 65, 1), pltpu.roll(v, 1, 1))


def link(ref, mu, rows=3):
    return [[tuple(ref[(mu * 2 + c) * 9 + a * 3 + b] for c in range(2)) for b in range(3)] for a in range(rows)]


def spinor(ref, n, s, c):
    return tuple(ref[((n * 2 + k) * 4 + s) * 3 + c] for k in range(2))


def upper(ref, mu, sign, n, s, c):
    col, phase = BLOCKS[mu][s]
    return add_phase(spinor(ref, n, s, c), sign * phase, spinor(ref, n, 2 + col, c))


def half(ref, mu, sign):
    return {k: upper(ref, mu, sign, *k) for k in SPINS}


def flat_half(h):
    return [h[k][c] for k in SPINS for c in range(2)]


def unflat_half(flat):
    return {k: (flat[2 * i], flat[2 * i + 1]) for i, k in enumerate(SPINS)}


def apply(m, h):
    return {(n, s, a): csum([cmul(m[a][b], h[n, s, b]) for b in range(3)]) for n, s, a in SPINS}


def apply_dagger(m, h):
    return {(n, s, a): csum([cmulc(h[n, s, b], m[b][a]) for b in range(3)]) for n, s, a in SPINS}


def others(d):
    return [nu for nu in range(4) if nu != d]


def low_values(lref, xref, d):
    out = []
    for nu in others(d):
        m = link(lref, nu, 2)
        out += [m[a][b][c] for a, b in ROWS for c in range(2)]
    return out + flat_half(half(xref, d, -1))


def put(ref, at, flat):
    for i, v in enumerate(flat):
        ref[at + i] = v


def get(ref, at, n):
    return [ref[at + i] for i in range(n)]


def pack_kernel(flags, lref, xref, zd, zu, ta, tb, ra, rb, gref):
    sites = Sites()
    g = []
    for d in range(3):
        flat = flat_half(apply_dagger(link(lref, d), half(xref, d, 1)))
        put(gref, 24 * d, flat)
        g.append(flat)
    for d in (Z, T, R):
        low = low_values(lref, xref, d)
        low_out = [sites.pack_low(low[2 * i], low[2 * i + 1], d) for i in range(30)]
        high_out = [sites.pack_high(g[d][2 * i], g[d][2 * i + 1], d) for i in range(12)]
        if d == T:
            low_out = low_out[:18] + [jnp.where(flags[0] == 0, -v, v) for v in low_out[18:]]
            high_out = [jnp.where(flags[1] == 0, -v, v) for v in high_out]
        if d == Z:
            put(zd, 0, low_out)
            put(zu, 0, high_out)
            continue
        swap_put(flags[2 + d // 2], (ta, tb) if d == T else (ra, rb), low_out, high_out)


def swap_put(even, refs, low, high):
    flag = even == 1
    for i in range(max(len(low), len(high))):
        a = low[i] if i < len(low) else high[i]
        b = high[i] if i < len(high) else low[i]
        refs[0][i] = jnp.where(flag, b, a)
        refs[1][i] = jnp.where(flag, a, b)


def swap_get(even, refs, n, low):
    flag = even == 1
    first, second = refs if low else (refs[1], refs[0])
    return [jnp.where(flag, first[i], second[i]) for i in range(n)]


def local_kernel(lref, xref, yref, wref, gyref, m2ref):
    sites = Sites()
    u = link(lref, Y)
    h = {k: tuple(sites.y_ahead(v) for v in c) for k, c in half(xref, Y, -1).items()}
    w = apply(u, h)
    g = {k: tuple(sites.y_behind(v) for v in c) for k, c in apply_dagger(u, half(xref, Y, 1)).items()}
    put(wref, 0, flat_half(w))
    put(gyref, 0, flat_half(g))
    for n in range(2):
        for s in range(2):
            for c in range(3):
                x = spinor(xref, n, s, c)
                store_spinor(yref, n, s, c, [x[i] - HOPPING * (w[n, s, c][i] + g[n, s, c][i]) for i in range(2)])
        for r in range(2):
            col, phase = BLOCKS[Y][r]
            for c in range(3):
                x = spinor(xref, n, 2 + col, c)
                diff = [g[n, r, c][i] - w[n, r, c][i] for i in range(2)]
                term = add_phase((0.0, 0.0), complex(phase).conjugate(), diff)
                store_spinor(yref, n, 2 + col, c, [x[i] - HOPPING * term[i] for i in range(2)])
    for mu in range(3):
        m = [[tuple(sites.y_ahead(v) for v in e) for e in row] for row in link(lref, mu)]
        m2 = matmul(u, m)
        put(m2ref, 18 * mu, [m2[a][b][c] for a in range(3) for b in range(3) for c in range(2)])


def store_spinor(ref, n, s, c, value):
    for k in range(2):
        ref[((n * 2 + k) * 4 + s) * 3 + c] = value[k]


def mat_at(ref, at):
    return [[(ref[at + (a * 3 + b) * 2], ref[at + (a * 3 + b) * 2 + 1]) for b in range(3)] for a in range(3)]


def put_mat(ref, at, m):
    put(ref, at, [m[a][b][c] for a in range(3) for b in range(3) for c in range(2)])


def middle_kernel(
    flags, lref, xref, gref, ylref, wyref, gyref, m2ref, zd, zu, ta, tb, ra, rb,
    ozu, ozd, ota, otb, ora, orb, oe, on, obase, oy, ow, nyref, fref, gsref,
):
    sites = Sites()
    put(oy, 0, get(ylref, 0, 48))
    put(ow, 72, get(wyref, 0, 24))
    slot = {}
    for d in range(3):
        if d == Z:
            low_in, high_in = get(zd, 0, 30), get(zu, 0, 12)
        else:
            refs = (ta, tb) if d == T else (ra, rb)
            low_in = swap_get(flags[2 + d // 2], refs, 30, True)
            high_in = swap_get(flags[2 + d // 2], refs, 12, False)
        own = low_values(lref, xref, d)
        ahead = []
        for i in range(30):
            ahead += sites.ahead(own[2 * i], own[2 * i + 1], low_in[i], d)
        for k, nu in enumerate(others(d)):
            f = ahead[12 * k : 12 * k + 12]
            two = [[(f[(a * 3 + b) * 2], f[(a * 3 + b) * 2 + 1]) for b in range(3)] for a in range(2)]
            put_mat(fref, 18 * (3 * d + k), third_row(two))
            slot[d, nu] = 18 * (3 * d + k)
        own = get(gref, 24 * d, 24)
        behind = []
        for i in range(12):
            behind += sites.behind(own[2 * i], own[2 * i + 1], high_in[i], d)
        put(gsref, 24 * d, behind)
        g = unflat_half(behind)
        w = apply(link(lref, d), unflat_half(ahead[36:]))
        put(ow, 24 * d, flat_half(w))
        for n in range(2):
            for s in range(2):
                for c in range(3):
                    y = spinor(oy, n, s, c)
                    store_spinor(oy, n, s, c, [y[i] - HOPPING * (w[n, s, c][i] + g[n, s, c][i]) for i in range(2)])
            for r in range(2):
                col, phase = BLOCKS[d][r]
                for c in range(3):
                    y = spinor(oy, n, 2 + col, c)
                    diff = [HOPPING * (g[n, r, c][i] - w[n, r, c][i]) for i in range(2)]
                    y = add_phase(y, -complex(phase).conjugate(), diff)
                    store_spinor(oy, n, 2 + col, c, y)
    base = [[0.0] * 8 for _ in range(4)]
    lower = {}
    for mu in range(4):
        for nu in range(mu + 1, 4):
            u_mu, u_nu = link(lref, mu), link(lref, nu)
            m1 = matmul(u_mu, mat_at(fref, slot[mu, nu]))
            m2 = mat_at(m2ref, 18 * mu) if nu == Y else matmul(u_nu, mat_at(fref, slot[nu, mu]))
            p = antihermitian(matmul_dagger(m1, m2), PLAQUETTE)
            base[mu] = [a + b for a, b in zip(base[mu], p)]
            base[nu] = [a - b for a, b in zip(base[nu], p)]
            lower[mu, nu] = [-v for v in transport(p, u_nu)]
            lower[nu, mu] = transport(p, u_mu)
    for mu in range(3):
        moved = [sites.y_behind(v) for v in lower[mu, Y]]
        base[mu] = [a + b for a, b in zip(base[mu], moved)]
    for mu in range(4):
        put(obase, 8 * mu, base[mu])
    for d in range(4):
        g = unflat_half(get(gsref, 24 * d, 24) if d < 3 else get(gyref, 0, 24))
        k = half(oy, d, 1)
        m = [
            [csum([cmulc(k[n, s, a], g[n, s, b]) for n in range(2) for s in range(2)]) for b in range(3)]
            for a in range(3)
        ]
        part = antihermitian(m, HOPPING)
        if d == Y:
            put(nyref, 0, [sites.y_ahead(v) for v in part])
            continue
        put(on, 8 * d, part)
        low_out = [sites.pack_low(part[2 * i], part[2 * i + 1], d) for i in range(4)]
        up = []
        for mu in others(d):
            up += lower[mu, d]
        put(oe, 24 * d, up)
        high_out = [sites.pack_high(up[2 * i], up[2 * i + 1], d) for i in range(12)]
        if d == Z:
            put(ozd, 0, low_out)
            put(ozu, 0, high_out)
        else:
            swap_put(flags[2 + d // 2], (ota, otb) if d == T else (ora, orb), low_out, high_out)


def inner_kernel(lref, yref, wref, nyref, baseref, oref):
    for mu in range(4):
        w = unflat_half(get(wref, 24 * mu, 24))
        k = half(yref, mu, -1)
        m = [
            [csum([cmulc(w[n, s, a], k[n, s, b]) for n in range(2) for s in range(2)]) for b in range(3)]
            for a in range(3)
        ]
        part = antihermitian(m, HOPPING)
        total = [a + b for a, b in zip(part, get(baseref, 8 * mu, 8))]
        if mu == Y:
            u = link(lref, Y)
            w_dagger = [[conj(u[j][a]) for j in range(3)] for a in range(3)]
            total = [a + b for a, b in zip(total, transport(get(nyref, 0, 8), w_dagger))]
        put(oref, 8 * mu, total)


def last_kernel(flags, lref, baseref, eref, nref, zu, zd, ta, tb, ra, rb, oref):
    sites = Sites()
    total = [get(baseref, 8 * mu, 8) for mu in range(4)]
    for d in range(3):
        if d == Z:
            low_in, high_in = get(zd, 0, 4), get(zu, 0, 12)
        else:
            refs = (ta, tb) if d == T else (ra, rb)
            low_in = swap_get(flags[2 + d // 2], refs, 4, True)
            high_in = swap_get(flags[2 + d // 2], refs, 12, False)
        own = get(eref, 24 * d, 24)
        behind = []
        for i in range(12):
            behind += sites.behind(own[2 * i], own[2 * i + 1], high_in[i], d)
        for k, mu in enumerate(others(d)):
            total[mu] = [a + b for a, b in zip(total[mu], behind[8 * k : 8 * k + 8])]
        own = get(nref, 8 * d, 8)
        ahead = []
        for i in range(4):
            ahead += sites.ahead(own[2 * i], own[2 * i + 1], low_in[i], d)
        u = link(lref, d)
        w_dagger = [[conj(u[j][a]) for j in range(3)] for a in range(3)]
        total[d] = [a + b for a, b in zip(total[d], transport(ahead, w_dagger))]
    zero = jnp.zeros((4, 128), jnp.float32)
    for mu in range(4):
        x = total[mu]
        at = mu * 18
        for i, (a, b) in enumerate(OFF):
            oref[at + a * 3 + b] = x[2 * i]
            oref[at + b * 3 + a] = -x[2 * i]
            oref[at + 9 + a * 3 + b] = x[2 * i + 1]
            oref[at + 9 + b * 3 + a] = x[2 * i + 1]
        for a in range(3):
            oref[at + a * 4] = zero
        oref[at + 9] = x[6]
        oref[at + 13] = x[7]
        oref[at + 17] = -(x[6] + x[7])


def call(body, operands, outs, flops, scratch=()):
    specs = [
        pl.BlockSpec(memory_space=pltpu.SMEM if o.dtype == jnp.int32 else pltpu.VMEM) for o in operands
    ]
    return pl.pallas_call(
        body,
        in_specs=specs,
        out_specs=[pl.BlockSpec(memory_space=pltpu.VMEM) for _ in outs],
        out_shape=[jax.ShapeDtypeStruct((n, 4, 128), jnp.float32) for n in outs],
        scratch_shapes=[pltpu.VMEM((n, 4, 128), jnp.float32) for n in scratch],
        cost_estimate=pl.CostEstimate(flops=flops, bytes_accessed=4 * 512 * 200, transcendentals=0),
        compiler_params=pltpu.CompilerParams(vmem_limit_bytes=8 * 1024 * 1024),
        interpret=INTERPRET,
    )(*operands)


def move(x, axis, by):
    size = lax.axis_size(axis)
    return lax.ppermute(x, axis, [(i, (i + by) % size) for i in range(size)])


def meet(x, axis, first):
    size = lax.axis_size(axis)
    pairs = []
    for i in range(0 if first else 1, size, 2):
        j = (i + 1) % size
        pairs += [(i, j), (j, i)]
    return lax.ppermute(x, axis, pairs)


def exchange(zd, zu, ta, tb, ra, rb):
    moves = {
        "zd": lambda: move(zd, "gz", -1),
        "zu": lambda: move(zu, "gz", 1),
        "ta": lambda: meet(ta, "ta", True),
        "tb": lambda: meet(tb, "ta", False),
        "ra": lambda: meet(ra, "xy", True),
        "rb": lambda: meet(rb, "xy", False),
    }
    out = {}
    for name in moves:
        out[name] = moves[name]()
    return [out[name] for name in moves]


def on_device(links, solutions):
    shape = links.shape
    lk = links.reshape(72, 4, 128)
    xs = solutions.reshape(48, 4, 128)
    t, r = lax.axis_index("ta"), lax.axis_index("xy")
    flags = jnp.stack([t, lax.axis_size("ta") - 1 - t, 1 - t % 2, 1 - r % 2]).astype(jnp.int32)
    zd, zu, ta, tb, ra, rb, g = call(pack_kernel, (flags, lk, xs), (30, 12, 30, 30, 30, 30, 72), 4_000_000)
    zd, zu, ta, tb, ra, rb = exchange(zd, zu, ta, tb, ra, rb)
    yl, wy, gy, m2 = call(local_kernel, (lk, xs), (48, 24, 24, 54), 20_000_000)
    ozu, ozd, ota, otb, ora, orb, e, n, base, y, w, ny = call(
        middle_kernel,
        (flags, lk, xs, g, yl, wy, gy, m2, zd, zu, ta, tb, ra, rb),
        (12, 4, 12, 12, 12, 12, 72, 24, 32, 48, 96, 8),
        20_000_000,
        (162, 72),
    )
    ozd, ozu, ota, otb, ora, orb = exchange(ozd, ozu, ota, otb, ora, orb)
    (base,) = call(inner_kernel, (lk, y, w, ny, base), (32,), 20_000_000)
    (force,) = call(last_kernel, (flags, lk, base, e, n, ozu, ozd, ota, otb, ora, orb), (72,), 4_000_000)
    return force.reshape(shape)


def solution(mesh):
    spec = P(None, None, None, None, "ta", "gz", "xy")

    return jax.shard_map(on_device, mesh=mesh, in_specs=(spec, spec), out_specs=spec, check_vma=False)
```

time: 166 us -> 84.5 us (0.51)
  other arithmetic: 34.4 us -> 0.08 us
  waiting for transfers between devices: 32.2 us -> 5.68 us
  starting transfers between devices: 83.6 us -> 71.4 us
  local copies, waits for them, and re-layouts: 12.2 us -> 1.81 us
  Pallas kernels: 0 us -> 4.9 us
  between operations: 2.44 us -> 0.19 us
    ppermute x15 -> x12, waiting for transfers between devices: 32.2 us -> 5.68 us  [the longest x8 5.49 us: meet(): return lax.ppermute(x, axis, pairs)]
    reduce_sum x43 -> x0, other arithmetic: 15.4 us -> none  [the longest x33 12.5 us: matrix_product(): jnp.sum(left_real[:, :, None] * right_real[None] - left_imaginary[:, :, N...]
    ppermute x15 -> x12, starting transfers between devices: 83.6 us -> 71.4 us  [the longest x4 39.5 us: move(): return lax.ppermute(x, axis, [(i, (i + by) % size) for i in range(size)])]
    slice x22 -> x0, local copies, waits for them, and re-layouts: 4.98 us -> none  [the longest x4 1.18 us: shift_rows(): jnp.roll(source, 1, -1)]
    pallas_call x0 -> x5, Pallas kernels: none -> 4.9 us  [call(): pl.pallas_call(body, in_specs=specs, out_specs=[pl.BlockSpec(memory_space...]
    concatenate x7 -> x0, other arithmetic: 3.76 us -> none  [the longest x2 2.59 us: padded_2(): x = jnp.concatenate([before, x, after], axis=dim)]
    reshape x14 -> x0, local copies, waits for them, and re-layouts: 3.63 us -> none  [the longest x8 1.59 us: face_window(): return region.reshape(flat_shape)]
    select_n x5 -> x0, other arithmetic: 3.24 us -> none  [the longest x2 1.9 us: shift_rows(): jnp.where(positions == row_length - 1, jnp.roll(source, row_length - 1, -...]
  transfers between devices with their start and end apart: 15 -> 12, of which waited for: 3 -> 4; matrix products, arithmetic and copies ran while one was open for 14% -> 0% of each run, Pallas kernels for 0% -> 1%
where the time goes in v1:
time: 84.5 us; the launch traced here: 84 us
  starting transfers between devices  71.4 us (84%)
  waiting for transfers between devices  5.68 us (7%)
  Pallas kernels  4.9 us (6%)
  local copies, waits for them, and re-layouts  1.81 us (2%)
    ppermute x4, starting transfers between devices, move(): return lax.ppermute(x, axis, [(i, (i + by) % size) for i in range(size)])  39.5 us
    ppermute x8, starting transfers between devices, meet(): return lax.ppermute(x, axis, pairs)  31.9 us
    ppermute x8, waiting for transfers between devices, meet(): return lax.ppermute(x, axis, pairs)  5.49 us
    pallas_call x5, Pallas kernels, call(): pl.pallas_call(body, in_specs=specs, out_specs=[pl.BlockSpec(memory_space...  4.9 us
    unnamed x8, local copies, waits for them, and re-layouts  1.81 us
  transfers between devices with their start and end apart: 12, of which 4 were waited for; matrix products, arithmetic and copies ran while one was open for 0% of the time, Pallas kernels for 1%

profile of v1, /device:TPU:1, one launch (start us, length us, event | category | flops | bytes accessed | tf_op | source)
XLA Modules:
  0.0 84.0 jit_solution(6317708991145270614)
XLA Ops:
  0.0 0.1 pad_add_fusion.flags
  0.1 0.9 %copy-done = f32[4,2,3,3,2,2,128]{6,5,4,3,2,1,0:T(2,128)S(1)} copy-done((f32[4,2,3,3,2,2,128]{6,5,4,3,2,1,0:T(2,128)S(1)}, f32[4,2,3,3,2,2,128]{6,5,4,3,2,1,0:T(2,128)}, u32[]{:S(2)}) %copy-start) | copy-done | bytes 147480
  1.0 0.9 %copy-done.2 = f32[2,2,4,3,2,2,128]{6,5,4,3,2,1,0:T(2,128)S(1)} copy-done((f32[2,2,4,3,2,2,128]{6,5,4,3,2,1,0:T(2,128)S(1)}, f32[2,2,4,3,2,2,128]{6,5,4,3,2,1,0:T(2,128)}, u32[]{:S(2)}) %copy-start.2) | copy-done | bytes 98328
  1.9 0.8 shard_map.28
  2.7 16.3 %collective-permute-start.1 = (f32[12,4,128]{2,1,0:T(4,128)S(1)}, f32[12,4,128]{2,1,0:T(4,128)S(1)}, u32[]{:S(2)}, u32[]{:S(2)}) collective-permute-start(f32[12,4,128]{2,1,0:T(4,128)S(1)} %get-tuple-element.34), channel_id=1, source_target_pairs={{0,8},{8,16},{16,24},{24,0},{1,9},{9,17},{17,25},{25,1},{2,10},{10... | collective-permute-start | bytes 73736 | tf_op jit(solution)/shard_map/ppermute | solution.py:443
  18.9 9.2 %collective-permute-start = (f32[30,4,128]{2,1,0:T(4,128)S(1)}, f32[30,4,128]{2,1,0:T(4,128)S(1)}, u32[]{:S(2)}, u32[]{:S(2)}) collective-permute-start(f32[30,4,128]{2,1,0:T(4,128)S(1)} %get-tuple-element.33), channel_id=1, source_target_pairs={{0,24},{8,0},{16,8},{24,16},{1,25},{9,1},{17,9},{25,17},{2,26},{10... | collective-permute-start | bytes 184328 | tf_op jit(solution)/shard_map/ppermute | solution.py:443
  28.1 3.1 %collective-permute-start.2 = (f32[30,4,128]{2,1,0:T(4,128)S(1)}, f32[30,4,128]{2,1,0:T(4,128)S(1)}, u32[]{:S(2)}, u32[]{:S(2)}) collective-permute-start(f32[30,4,128]{2,1,0:T(4,128)S(1)} %get-tuple-element.35), channel_id=1, source_target_pairs={{0,32},{32,0},{64,96},{96,64},{128,160},{160,128},{192,224},{224,1... | collective-permute-start | bytes 184328 | tf_op jit(solution)/shard_map/ppermute | solution.py:452
  31.3 7.1 %collective-permute-start.3 = (f32[30,4,128]{2,1,0:T(4,128)S(1)}, f32[30,4,128]{2,1,0:T(4,128)S(1)}, u32[]{:S(2)}, u32[]{:S(2)}) collective-permute-start(f32[30,4,128]{2,1,0:T(4,128)S(1)} %get-tuple-element.36), channel_id=1, source_target_pairs={{32,64},{64,32},{96,128},{128,96},{160,192},{192,160},{224,256},{2... | collective-permute-start | bytes 184328 | tf_op jit(solution)/shard_map/ppermute | solution.py:452
  38.4 3.4 %collective-permute-start.4 = (f32[30,4,128]{2,1,0:T(4,128)S(1)}, f32[30,4,128]{2,1,0:T(4,128)S(1)}, u32[]{:S(2)}, u32[]{:S(2)}) collective-permute-start(f32[30,4,128]{2,1,0:T(4,128)S(1)} %get-tuple-element.37), channel_id=1, source_target_pairs={{0,1},{1,0},{2,3},{3,2},{4,5},{5,4},{6,7},{7,6},{8,9},{9,8},{10,11... | collective-permute-start | bytes 184328 | tf_op jit(solution)/shard_map/ppermute | solution.py:452
  41.9 3.1 %collective-permute-start.5 = (f32[30,4,128]{2,1,0:T(4,128)S(1)}, f32[30,4,128]{2,1,0:T(4,128)S(1)}, u32[]{:S(2)}, u32[]{:S(2)}) collective-permute-start(f32[30,4,128]{2,1,0:T(4,128)S(1)} %get-tuple-element.38), channel_id=1, source_target_pairs={{1,2},{2,1},{3,4},{4,3},{5,6},{6,5},{7,0},{0,7},{9,10},{10,9},{11,... | collective-permute-start | bytes 184328 | tf_op jit(solution)/shard_map/ppermute | solution.py:452
  45.0 0.3 shard_map.29
  45.3 0.2 collective-permute-done.zd
  45.5 0.4 collective-permute-done.3.tb
  45.9 1.8 %collective-permute-done.5.rb = f32[30,4,128]{2,1,0:T(4,128)S(1)} collective-permute-done((f32[30,4,128]{2,1,0:T(4,128)S(1)}, f32[30,4,128]{2,1,0:T(4,128)S(1)}, u32[]{:S(2)}, u32[]{:S(2)}) %collective-permute-start.5) | collective-permute-done | bytes 61472 | tf_op jit(solution)/shard_map/ppermute | solution.py:452
  47.7 2.2 %shard_map.30 = (f32[12,4,128]{2,1,0:T(4,128)S(1)}, f32[4,4,128]{2,1,0:T(4,128)S(1)}, f32[12,4,128]{2,1,0:T(4,128)S(1)}, f32[12,4,128]{2,1,0:T(4,128)S(1)}, f32[...) custom-call(s32[4]{0:T(128)S(1)} %pad_add_fusion.flags, ...), custom_call_target="tpu_custom_call" | custom-call | flops 20000000 | bytes 409600 | tf_op jit(solution)/shard_map/pallas_call | solution.py:429
  49.9 11.8 %collective-permute-start.7 = (f32[4,4,128]{2,1,0:T(4,128)S(1)}, f32[4,4,128]{2,1,0:T(4,128)S(1)}, u32[]{:S(2)}, u32[]{:S(2)}) collective-permute-start(f32[4,4,128]{2,1,0:T(4,128)S(1)} %get-tuple-element.46), channel_id=1, source_target_pairs={{0,24},{8,0},{16,8},{24,16},{1,25},{9,1},{17,9},{25,17},{2,26},{10... | collective-permute-start | bytes 24584 | tf_op jit(solution)/shard_map/ppermute | solution.py:443
  61.8 2.2 %collective-permute-start.6 = (f32[12,4,128]{2,1,0:T(4,128)S(1)}, f32[12,4,128]{2,1,0:T(4,128)S(1)}, u32[]{:S(2)}, u32[]{:S(2)}) collective-permute-start(f32[12,4,128]{2,1,0:T(4,128)S(1)} %get-tuple-element.45), channel_id=1, source_target_pairs={{0,8},{8,16},{16,24},{24,0},{1,9},{9,17},{17,25},{25,1},{2,10},{10... | collective-permute-start | bytes 73736 | tf_op jit(solution)/shard_map/ppermute | solution.py:443
  63.9 1.9 %collective-permute-start.8 = (f32[12,4,128]{2,1,0:T(4,128)S(1)}, f32[12,4,128]{2,1,0:T(4,128)S(1)}, u32[]{:S(2)}, u32[]{:S(2)}) collective-permute-start(f32[12,4,128]{2,1,0:T(4,128)S(1)} %get-tuple-element.47), channel_id=1, source_target_pairs={{0,32},{32,0},{64,96},{96,64},{128,160},{160,128},{192,224},{224,1... | collective-permute-start | bytes 73736 | tf_op jit(solution)/shard_map/ppermute | solution.py:452
  65.9 7.6 %collective-permute-start.9 = (f32[12,4,128]{2,1,0:T(4,128)S(1)}, f32[12,4,128]{2,1,0:T(4,128)S(1)}, u32[]{:S(2)}, u32[]{:S(2)}) collective-permute-start(f32[12,4,128]{2,1,0:T(4,128)S(1)} %get-tuple-element.48), channel_id=1, source_target_pairs={{32,64},{64,32},{96,128},{128,96},{160,192},{192,160},{224,256},{2... | collective-permute-start | bytes 73736 | tf_op jit(solution)/shard_map/ppermute | solution.py:452
  73.5 3.7 %collective-permute-start.10 = (f32[12,4,128]{2,1,0:T(4,128)S(1)}, f32[12,4,128]{2,1,0:T(4,128)S(1)}, u32[]{:S(2)}, u32[]{:S(2)}) collective-permute-start(f32[12,4,128]{2,1,0:T(4,128)S(1)} %get-tuple-element.49), channel_id=1, source_target_pairs={{0,1},{1,0},{2,3},{3,2},{4,5},{5,4},{6,7},{7,6},{8,9},{9,8},{10,11... | collective-permute-start | bytes 73736 | tf_op jit(solution)/shard_map/ppermute | solution.py:452
  77.2 1.9 %collective-permute-start.11 = (f32[12,4,128]{2,1,0:T(4,128)S(1)}, f32[12,4,128]{2,1,0:T(4,128)S(1)}, u32[]{:S(2)}, u32[]{:S(2)}) collective-permute-start(f32[12,4,128]{2,1,0:T(4,128)S(1)} %get-tuple-element.50), channel_id=1, source_target_pairs={{1,2},{2,1},{3,4},{4,3},{5,6},{6,5},{7,0},{0,7},{9,10},{10,9},{11,... | collective-permute-start | bytes 73736 | tf_op jit(solution)/shard_map/ppermute | solution.py:452
  79.1 0.2 shard_map.31.baseref
  79.4 3.3 %collective-permute-done.11.rb = f32[12,4,128]{2,1,0:T(4,128)S(1)} collective-permute-done((f32[12,4,128]{2,1,0:T(4,128)S(1)}, f32[12,4,128]{2,1,0:T(4,128)S(1)}, u32[]{:S(2)}, u32[]{:S(2)}) %collective-permute-start.11) | collective-permute-done | bytes 24608 | tf_op jit(solution)/shard_map/ppermute | solution.py:452
  82.6 1.4 %shard_map.32 = f32[72,4,128]{2,1,0:T(4,128)} custom-call(s32[4]{0:T(128)S(1)} %pad_add_fusion.flags, f32[72,4,128]{2,1,0:T(4,128)S(1)} %bitcast.11, f32[32,4,128]{2,1,0:T(4,128)S(1)} %shard_map.31.baseref, f32[72,4,128]{2,1,0:T(4,128)S(1)} %get-tuple-element.43.eref, f32[24,4,128]{2,1,0:T(4,128)S(1)} %get-tuple-element.44.nref, ...), custom_call_target="tpu_custom_call" | custom-call | flops 4000000 | bytes 409600 | tf_op jit(solution)/shard_map/pallas_call | solution.py:429
  (14 shorter events, 0.0 us)
Async XLA Ops:
  0.1 0.9 %copy-start = (f32[4,2,3,3,2,2,128]{6,5,4,3,2,1,0:T(2,128)S(1)}, f32[4,2,3,3,2,2,128]{6,5,4,3,2,1,0:T(2,128)}, u32[]{:S(2)}) copy-start(f32[4,2,3,3,2,2,128]{6,5,4,3,2,1,0:T(2,128)} %param.2) | copy-start | bytes 442372
  1.0 0.9 %copy-start.2 = (f32[2,2,4,3,2,2,128]{6,5,4,3,2,1,0:T(2,128)S(1)}, f32[2,2,4,3,2,2,128]{6,5,4,3,2,1,0:T(2,128)}, u32[]{:S(2)}) copy-start(f32[2,2,4,3,2,2,128]{6,5,4,3,2,1,0:T(2,128)} %param.3) | copy-start | bytes 294916
  1.9 43.1 %copy-start.1 = (f32[4,2,3,3,2,2,128]{6,5,4,3,2,1,0:T(2,128)S(1)}, f32[4,2,3,3,2,2,128]{6,5,4,3,2,1,0:T(2,128)}, u32[]{:S(2)}) copy-start(f32[4,2,3,3,2,2,128]{6,5,4,3,2,1,0:T(2,128)} %param.2) | copy-start | bytes 442372
  1.9 43.1 %copy-start.3 = (f32[2,2,4,3,2,2,128]{6,5,4,3,2,1,0:T(2,128)S(1)}, f32[2,2,4,3,2,2,128]{6,5,4,3,2,1,0:T(2,128)}, u32[]{:S(2)}) copy-start(f32[2,2,4,3,2,2,128]{6,5,4,3,2,1,0:T(2,128)} %param.3) | copy-start | bytes 294916
  2.7 39.2 %collective-permute-start.1 = (f32[12,4,128]{2,1,0:T(4,128)S(1)}, f32[12,4,128]{2,1,0:T(4,128)S(1)}, u32[]{:S(2)}, u32[]{:S(2)}) collective-permute-start(f32[12,4,128]{2,1,0:T(4,128)S(1)} %get-tuple-element.34), channel_id=1, source_target_pairs={{0,8},{8,16},{16,24},{24,0},{1,9},{9,17},{17,25},{25,1},{2,10},{10... | collective-permute-start | bytes 73736 | tf_op jit(solution)/shard_map/ppermute | solution.py:443
  18.9 26.5 %collective-permute-start = (f32[30,4,128]{2,1,0:T(4,128)S(1)}, f32[30,4,128]{2,1,0:T(4,128)S(1)}, u32[]{:S(2)}, u32[]{:S(2)}) collective-permute-start(f32[30,4,128]{2,1,0:T(4,128)S(1)} %get-tuple-element.33), channel_id=1, source_target_pairs={{0,24},{8,0},{16,8},{24,16},{1,25},{9,1},{17,9},{25,17},{2,26},{10... | collective-permute-start | bytes 184328 | tf_op jit(solution)/shard_map/ppermute | solution.py:443
  28.1 17.3 %collective-permute-start.2 = (f32[30,4,128]{2,1,0:T(4,128)S(1)}, f32[30,4,128]{2,1,0:T(4,128)S(1)}, u32[]{:S(2)}, u32[]{:S(2)}) collective-permute-start(f32[30,4,128]{2,1,0:T(4,128)S(1)} %get-tuple-element.35), channel_id=1, source_target_pairs={{0,32},{32,0},{64,96},{96,64},{128,160},{160,128},{192,224},{224,1... | collective-permute-start | bytes 184328 | tf_op jit(solution)/shard_map/ppermute | solution.py:452
  31.3 14.6 %collective-permute-start.3 = (f32[30,4,128]{2,1,0:T(4,128)S(1)}, f32[30,4,128]{2,1,0:T(4,128)S(1)}, u32[]{:S(2)}, u32[]{:S(2)}) collective-permute-start(f32[30,4,128]{2,1,0:T(4,128)S(1)} %get-tuple-element.36), channel_id=1, source_target_pairs={{32,64},{64,32},{96,128},{128,96},{160,192},{192,160},{224,256},{2... | collective-permute-start | bytes 184328 | tf_op jit(solution)/shard_map/ppermute | solution.py:452
  38.4 7.5 %collective-permute-start.4 = (f32[30,4,128]{2,1,0:T(4,128)S(1)}, f32[30,4,128]{2,1,0:T(4,128)S(1)}, u32[]{:S(2)}, u32[]{:S(2)}) collective-permute-start(f32[30,4,128]{2,1,0:T(4,128)S(1)} %get-tuple-element.37), channel_id=1, source_target_pairs={{0,1},{1,0},{2,3},{3,2},{4,5},{5,4},{6,7},{7,6},{8,9},{9,8},{10,11... | collective-permute-start | bytes 184328 | tf_op jit(solution)/shard_map/ppermute | solution.py:452
  41.9 5.8 %collective-permute-start.5 = (f32[30,4,128]{2,1,0:T(4,128)S(1)}, f32[30,4,128]{2,1,0:T(4,128)S(1)}, u32[]{:S(2)}, u32[]{:S(2)}) collective-permute-start(f32[30,4,128]{2,1,0:T(4,128)S(1)} %get-tuple-element.38), channel_id=1, source_target_pairs={{1,2},{2,1},{3,4},{4,3},{5,6},{6,5},{7,0},{0,7},{9,10},{10,9},{11,... | collective-permute-start | bytes 184328 | tf_op jit(solution)/shard_map/ppermute | solution.py:452
  49.9 27.3 %collective-permute-start.7 = (f32[4,4,128]{2,1,0:T(4,128)S(1)}, f32[4,4,128]{2,1,0:T(4,128)S(1)}, u32[]{:S(2)}, u32[]{:S(2)}) collective-permute-start(f32[4,4,128]{2,1,0:T(4,128)S(1)} %get-tuple-element.46), channel_id=1, source_target_pairs={{0,24},{8,0},{16,8},{24,16},{1,25},{9,1},{17,9},{25,17},{2,26},{10... | collective-permute-start | bytes 24584 | tf_op jit(solution)/shard_map/ppermute | solution.py:443
  61.8 17.6 %collective-permute-start.6 = (f32[12,4,128]{2,1,0:T(4,128)S(1)}, f32[12,4,128]{2,1,0:T(4,128)S(1)}, u32[]{:S(2)}, u32[]{:S(2)}) collective-permute-start(f32[12,4,128]{2,1,0:T(4,128)S(1)} %get-tuple-element.45), channel_id=1, source_target_pairs={{0,8},{8,16},{16,24},{24,0},{1,9},{9,17},{17,25},{25,1},{2,10},{10... | collective-permute-start | bytes 73736 | tf_op jit(solution)/shard_map/ppermute | solution.py:443
  63.9 15.4 %collective-permute-start.8 = (f32[12,4,128]{2,1,0:T(4,128)S(1)}, f32[12,4,128]{2,1,0:T(4,128)S(1)}, u32[]{:S(2)}, u32[]{:S(2)}) collective-permute-start(f32[12,4,128]{2,1,0:T(4,128)S(1)} %get-tuple-element.47), channel_id=1, source_target_pairs={{0,32},{32,0},{64,96},{96,64},{128,160},{160,128},{192,224},{224,1... | collective-permute-start | bytes 73736 | tf_op jit(solution)/shard_map/ppermute | solution.py:452
  65.9 13.5 %collective-permute-start.9 = (f32[12,4,128]{2,1,0:T(4,128)S(1)}, f32[12,4,128]{2,1,0:T(4,128)S(1)}, u32[]{:S(2)}, u32[]{:S(2)}) collective-permute-start(f32[12,4,128]{2,1,0:T(4,128)S(1)} %get-tuple-element.48), channel_id=1, source_target_pairs={{32,64},{64,32},{96,128},{128,96},{160,192},{192,160},{224,256},{2... | collective-permute-start | bytes 73736 | tf_op jit(solution)/shard_map/ppermute | solution.py:452
  73.5 5.9 %collective-permute-start.10 = (f32[12,4,128]{2,1,0:T(4,128)S(1)}, f32[12,4,128]{2,1,0:T(4,128)S(1)}, u32[]{:S(2)}, u32[]{:S(2)}) collective-permute-start(f32[12,4,128]{2,1,0:T(4,128)S(1)} %get-tuple-element.49), channel_id=1, source_target_pairs={{0,1},{1,0},{2,3},{3,2},{4,5},{5,4},{6,7},{7,6},{8,9},{9,8},{10,11... | collective-permute-start | bytes 73736 | tf_op jit(solution)/shard_map/ppermute | solution.py:452
  77.2 5.4 %collective-permute-start.11 = (f32[12,4,128]{2,1,0:T(4,128)S(1)}, f32[12,4,128]{2,1,0:T(4,128)S(1)}, u32[]{:S(2)}, u32[]{:S(2)}) collective-permute-start(f32[12,4,128]{2,1,0:T(4,128)S(1)} %get-tuple-element.50), channel_id=1, source_target_pairs={{1,2},{2,1},{3,4},{4,3},{5,6},{6,5},{7,0},{0,7},{9,10},{10,9},{11,... | collective-permute-start | bytes 73736 | tf_op jit(solution)/shard_map/ppermute | solution.py:452

commit v2 on v1

--- a/solution.py
+++ b/solution.py
@@ -219,11 +219,11 @@
         if d == T:
             low_out = low_out[:18] + [jnp.where(flags[0] == 0, -v, v) for v in low_out[18:]]
             high_out = [jnp.where(flags[1] == 0, -v, v) for v in high_out]
-        if d == Z:
-            put(zd, 0, low_out)
-            put(zu, 0, high_out)
+        if d != T:
+            put(zd if d == Z else ra, 0, low_out)
+            put(zu if d == Z else rb, 0, high_out)
             continue
-        swap_put(flags[2 + d // 2], (ta, tb) if d == T else (ra, rb), low_out, high_out)
+        swap_put(flags[2], (ta, tb), low_out, high_out)
 
 
 def swap_put(even, refs, low, high):
@@ -289,8 +289,8 @@
     put(ow, 72, get(wyref, 0, 24))
     slot = {}
     for d in range(3):
-        if d == Z:
-            low_in, high_in = get(zd, 0, 30), get(zu, 0, 12)
+        if d != T:
+            low_in, high_in = get(zd if d == Z else ra, 0, 30), get(zu if d == Z else rb, 0, 12)
         else:
             refs = (ta, tb) if d == T else (ra, rb)
             low_in = swap_get(flags[2 + d // 2], refs, 30, True)
@@ -359,9 +359,9 @@
             up += lower[mu, d]
         put(oe, 24 * d, up)
         high_out = [sites.pack_high(up[2 * i], up[2 * i + 1], d) for i in range(12)]
-        if d == Z:
-            put(ozd, 0, low_out)
-            put(ozu, 0, high_out)
+        if d != T:
+            put(ozd if d == Z else ora, 0, low_out)
+            put(ozu if d == Z else orb, 0, high_out)
         else:
             swap_put(flags[2 + d // 2], (ota, otb) if d == T else (ora, orb), low_out, high_out)
 
@@ -387,8 +387,8 @@
     sites = Sites()
     total = [get(baseref, 8 * mu, 8) for mu in range(4)]
     for d in range(3):
-        if d == Z:
-            low_in, high_in = get(zd, 0, 4), get(zu, 0, 12)
+        if d != T:
+            low_in, high_in = get(zd if d == Z else ra, 0, 4), get(zu if d == Z else rb, 0, 12)
         else:
             refs = (ta, tb) if d == T else (ra, rb)
             low_in = swap_get(flags[2 + d // 2], refs, 4, True)
@@ -458,8 +458,8 @@
         "zu": lambda: move(zu, "gz", 1),
         "ta": lambda: meet(ta, "ta", True),
         "tb": lambda: meet(tb, "ta", False),
-        "ra": lambda: meet(ra, "xy", True),
-        "rb": lambda: meet(rb, "xy", False),
+        "ra": lambda: move(ra, "xy", -1),
+        "rb": lambda: move(rb, "xy", 1),
     }
     out = {}
     for name in moves:
@@ -473,13 +473,13 @@
     xs = solutions.reshape(48, 4, 128)
     t, r = lax.axis_index("ta"), lax.axis_index("xy")
     flags = jnp.stack([t, lax.axis_size("ta") - 1 - t, 1 - t % 2, 1 - r % 2]).astype(jnp.int32)
-    zd, zu, ta, tb, ra, rb, g = call(pack_kernel, (flags, lk, xs), (30, 12, 30, 30, 30, 30, 72), 4_000_000)
+    zd, zu, ta, tb, ra, rb, g = call(pack_kernel, (flags, lk, xs), (30, 12, 30, 30, 30, 12, 72), 4_000_000)
     zd, zu, ta, tb, ra, rb = exchange(zd, zu, ta, tb, ra, rb)
     yl, wy, gy, m2 = call(local_kernel, (lk, xs), (48, 24, 24, 54), 20_000_000)
     ozu, ozd, ota, otb, ora, orb, e, n, base, y, w, ny = call(
         middle_kernel,
         (flags, lk, xs, g, yl, wy, gy, m2, zd, zu, ta, tb, ra, rb),
-        (12, 4, 12, 12, 12, 12, 72, 24, 32, 48, 96, 8),
+        (12, 4, 12, 12, 4, 12, 72, 24, 32, 48, 96, 8),
         20_000_000,
         (162, 72),
     )

time: 84.5 us -> 90.4 us (1.070); the launches traced: 84 us -> 89 us
  waiting for transfers between devices: 5.68 us -> 13.9 us
  starting transfers between devices: 71.4 us -> 68.3 us
    ppermute x4 -> x8, waiting for transfers between devices: 0.19 us -> 13.9 us  [move(): return lax.ppermute(x, axis, [(i, (i + by) % size) for i in range(size)])]
    ppermute x8 -> x4, starting transfers between devices: 31.9 us -> 19.7 us  [meet(): return lax.ppermute(x, axis, pairs)]
    ppermute x4 -> x8, starting transfers between devices: 39.5 us -> 48.6 us  [move(): return lax.ppermute(x, axis, [(i, (i + by) % size) for i in range(size)])]
    ppermute x8 -> x4, waiting for transfers between devices: 5.49 us -> 0.01 us  [meet(): return lax.ppermute(x, axis, pairs)]
where the time goes in v2:
time: 90.4 us; the launch traced here: 89 us
  starting transfers between devices  68.3 us (76%)
  waiting for transfers between devices  13.9 us (15%)
  Pallas kernels  4.83 us (5%)
  local copies, waits for them, and re-layouts  1.81 us (2%)
    ppermute x8, starting transfers between devices, move(): return lax.ppermute(x, axis, [(i, (i + by) % size) for i in range(size)])  48.6 us
    ppermute x4, starting transfers between devices, meet(): return lax.ppermute(x, axis, pairs)  19.7 us
    ppermute x8, waiting for transfers between devices, move(): return lax.ppermute(x, axis, [(i, (i + by) % size) for i in range(size)])  13.9 us
    pallas_call x5, Pallas kernels, call(): pl.pallas_call(body, in_specs=specs, out_specs=[pl.BlockSpec(memory_space...  4.83 us
    unnamed x8, local copies, waits for them, and re-layouts  1.81 us
  transfers between devices with their start and end apart: 12, of which 4 were waited for; matrix products, arithmetic and copies ran while one was open for 0% of the time, Pallas kernels for 1%

profile of v2, /device:TPU:1, one launch (start us, length us, event | category | flops | bytes accessed | tf_op | source)
XLA Modules:
  0.0 89.0 jit_solution(17699120100185898245)
XLA Ops:
  0.0 0.1 pad_add_fusion.flags
  0.1 0.9 %copy-done = f32[4,2,3,3,2,2,128]{6,5,4,3,2,1,0:T(2,128)S(1)} copy-done((f32[4,2,3,3,2,2,128]{6,5,4,3,2,1,0:T(2,128)S(1)}, f32[4,2,3,3,2,2,128]{6,5,4,3,2,1,0:T(2,128)}, u32[]{:S(2)}) %copy-start) | copy-done | bytes 147480
  1.0 0.9 %copy-done.2 = f32[2,2,4,3,2,2,128]{6,5,4,3,2,1,0:T(2,128)S(1)} copy-done((f32[2,2,4,3,2,2,128]{6,5,4,3,2,1,0:T(2,128)S(1)}, f32[2,2,4,3,2,2,128]{6,5,4,3,2,1,0:T(2,128)}, u32[]{:S(2)}) %copy-start.2) | copy-done | bytes 98328
  1.9 0.8 shard_map.28
  2.7 23.5 %collective-permute-start = (f32[30,4,128]{2,1,0:T(4,128)S(1)}, f32[30,4,128]{2,1,0:T(4,128)S(1)}, u32[]{:S(2)}, u32[]{:S(2)}) collective-permute-start(f32[30,4,128]{2,1,0:T(4,128)S(1)} %get-tuple-element.33), channel_id=1, source_target_pairs={{0,24},{8,0},{16,8},{24,16},{1,25},{9,1},{17,9},{25,17},{2,26},{10... | collective-permute-start | bytes 184328 | tf_op jit(solution)/shard_map/ppermute | solution.py:443
  26.2 3.1 %collective-permute-start.2 = (f32[30,4,128]{2,1,0:T(4,128)S(1)}, f32[30,4,128]{2,1,0:T(4,128)S(1)}, u32[]{:S(2)}, u32[]{:S(2)}) collective-permute-start(f32[30,4,128]{2,1,0:T(4,128)S(1)} %get-tuple-element.35), channel_id=1, source_target_pairs={{0,32},{32,0},{64,96},{96,64},{128,160},{160,128},{192,224},{224,1... | collective-permute-start | bytes 184328 | tf_op jit(solution)/shard_map/ppermute | solution.py:452
  29.3 6.9 %collective-permute-start.3 = (f32[30,4,128]{2,1,0:T(4,128)S(1)}, f32[30,4,128]{2,1,0:T(4,128)S(1)}, u32[]{:S(2)}, u32[]{:S(2)}) collective-permute-start(f32[30,4,128]{2,1,0:T(4,128)S(1)} %get-tuple-element.36), channel_id=1, source_target_pairs={{32,64},{64,32},{96,128},{128,96},{160,192},{192,160},{224,256},{2... | collective-permute-start | bytes 184328 | tf_op jit(solution)/shard_map/ppermute | solution.py:452
  36.2 1.5 %collective-permute-start.4 = (f32[30,4,128]{2,1,0:T(4,128)S(1)}, f32[30,4,128]{2,1,0:T(4,128)S(1)}, u32[]{:S(2)}, u32[]{:S(2)}) collective-permute-start(f32[30,4,128]{2,1,0:T(4,128)S(1)} %get-tuple-element.37), channel_id=1, source_target_pairs={{0,7},{1,0},{2,1},{3,2},{4,3},{5,4},{6,5},{7,6},{8,15},{9,8},{10,9... | collective-permute-start | bytes 184328 | tf_op jit(solution)/shard_map/ppermute | solution.py:443
  37.8 1.9 %collective-permute-start.1 = (f32[12,4,128]{2,1,0:T(4,128)S(1)}, f32[12,4,128]{2,1,0:T(4,128)S(1)}, u32[]{:S(2)}, u32[]{:S(2)}) collective-permute-start(f32[12,4,128]{2,1,0:T(4,128)S(1)} %get-tuple-element.34), channel_id=1, source_target_pairs={{0,8},{8,16},{16,24},{24,0},{1,9},{9,17},{17,25},{25,1},{2,10},{10... | collective-permute-start | bytes 73736 | tf_op jit(solution)/shard_map/ppermute | solution.py:443
  39.7 11.4 %collective-permute-done.1.zu = f32[12,4,128]{2,1,0:T(4,128)S(1)} collective-permute-done((f32[12,4,128]{2,1,0:T(4,128)S(1)}, f32[12,4,128]{2,1,0:T(4,128)S(1)}, u32[]{:S(2)}, u32[]{:S(2)}) %collective-permute-start.1) | collective-permute-done | bytes 24608 | tf_op jit(solution)/shard_map/ppermute | solution.py:443
  51.1 2.7 %collective-permute-start.5 = (f32[12,4,128]{2,1,0:T(4,128)S(1)}, f32[12,4,128]{2,1,0:T(4,128)S(1)}, u32[]{:S(2)}, u32[]{:S(2)}) collective-permute-start(f32[12,4,128]{2,1,0:T(4,128)S(1)} %get-tuple-element.38), channel_id=1, source_target_pairs={{0,1},{1,2},{2,3},{3,4},{4,5},{5,6},{6,7},{7,0},{8,9},{9,10},{10,1... | collective-permute-start | bytes 73736 | tf_op jit(solution)/shard_map/ppermute | solution.py:443
  53.9 0.3 shard_map.29
  54.2 0.7 collective-permute-done.5.rb
  54.9 2.2 %shard_map.30 = (f32[12,4,128]{2,1,0:T(4,128)S(1)}, f32[4,4,128]{2,1,0:T(4,128)S(1)}, f32[12,4,128]{2,1,0:T(4,128)S(1)}, f32[12,4,128]{2,1,0:T(4,128)S(1)}, f32[...) custom-call(s32[4]{0:T(128)S(1)} %pad_add_fusion.flags, ...), custom_call_target="tpu_custom_call" | custom-call | flops 20000000 | bytes 409600 | tf_op jit(solution)/shard_map/pallas_call | solution.py:429
  57.1 1.9 %collective-permute-start.6 = (f32[12,4,128]{2,1,0:T(4,128)S(1)}, f32[12,4,128]{2,1,0:T(4,128)S(1)}, u32[]{:S(2)}, u32[]{:S(2)}) collective-permute-start(f32[12,4,128]{2,1,0:T(4,128)S(1)} %get-tuple-element.45), channel_id=1, source_target_pairs={{0,8},{8,16},{16,24},{24,0},{1,9},{9,17},{17,25},{25,1},{2,10},{10... | collective-permute-start | bytes 73736 | tf_op jit(solution)/shard_map/ppermute | solution.py:443
  59.0 1.9 %collective-permute-start.8 = (f32[12,4,128]{2,1,0:T(4,128)S(1)}, f32[12,4,128]{2,1,0:T(4,128)S(1)}, u32[]{:S(2)}, u32[]{:S(2)}) collective-permute-start(f32[12,4,128]{2,1,0:T(4,128)S(1)} %get-tuple-element.47), channel_id=1, source_target_pairs={{0,32},{32,0},{64,96},{96,64},{128,160},{160,128},{192,224},{224,1... | collective-permute-start | bytes 73736 | tf_op jit(solution)/shard_map/ppermute | solution.py:452
  61.0 7.7 %collective-permute-start.9 = (f32[12,4,128]{2,1,0:T(4,128)S(1)}, f32[12,4,128]{2,1,0:T(4,128)S(1)}, u32[]{:S(2)}, u32[]{:S(2)}) collective-permute-start(f32[12,4,128]{2,1,0:T(4,128)S(1)} %get-tuple-element.48), channel_id=1, source_target_pairs={{32,64},{64,32},{96,128},{128,96},{160,192},{192,160},{224,256},{2... | collective-permute-start | bytes 73736 | tf_op jit(solution)/shard_map/ppermute | solution.py:452
  68.7 2.7 %collective-permute-start.11 = (f32[12,4,128]{2,1,0:T(4,128)S(1)}, f32[12,4,128]{2,1,0:T(4,128)S(1)}, u32[]{:S(2)}, u32[]{:S(2)}) collective-permute-start(f32[12,4,128]{2,1,0:T(4,128)S(1)} %get-tuple-element.50), channel_id=1, source_target_pairs={{0,1},{1,2},{2,3},{3,4},{4,5},{5,6},{6,7},{7,0},{8,9},{9,10},{10,1... | collective-permute-start | bytes 73736 | tf_op jit(solution)/shard_map/ppermute | solution.py:443
  71.4 12.2 %collective-permute-start.7 = (f32[4,4,128]{2,1,0:T(4,128)S(1)}, f32[4,4,128]{2,1,0:T(4,128)S(1)}, u32[]{:S(2)}, u32[]{:S(2)}) collective-permute-start(f32[4,4,128]{2,1,0:T(4,128)S(1)} %get-tuple-element.46), channel_id=1, source_target_pairs={{0,24},{8,0},{16,8},{24,16},{1,25},{9,1},{17,9},{25,17},{2,26},{10... | collective-permute-start | bytes 24584 | tf_op jit(solution)/shard_map/ppermute | solution.py:443
  83.6 0.8 collective-permute-done.7.zd
  84.5 2.0 %collective-permute-start.10 = (f32[4,4,128]{2,1,0:T(4,128)S(1)}, f32[4,4,128]{2,1,0:T(4,128)S(1)}, u32[]{:S(2)}, u32[]{:S(2)}) collective-permute-start(f32[4,4,128]{2,1,0:T(4,128)S(1)} %get-tuple-element.49), channel_id=1, source_target_pairs={{0,7},{1,0},{2,1},{3,2},{4,3},{5,4},{6,5},{7,6},{8,15},{9,8},{10,9... | collective-permute-start | bytes 24584 | tf_op jit(solution)/shard_map/ppermute | solution.py:443
  86.5 0.2 shard_map.31.baseref
  86.7 0.8 collective-permute-done.10.ra
  87.6 1.4 %shard_map.32 = f32[72,4,128]{2,1,0:T(4,128)} custom-call(s32[4]{0:T(128)S(1)} %pad_add_fusion.flags, f32[72,4,128]{2,1,0:T(4,128)S(1)} %bitcast.11, f32[32,4,128]{2,1,0:T(4,128)S(1)} %shard_map.31.baseref, f32[72,4,128]{2,1,0:T(4,128)S(1)} %get-tuple-element.43.eref, f32[24,4,128]{2,1,0:T(4,128)S(1)} %get-tuple-element.44.nref, ...), custom_call_target="tpu_custom_call" | custom-call | flops 4000000 | bytes 409600 | tf_op jit(solution)/shard_map/pallas_call | solution.py:429
  (14 shorter events, 0.0 us)
Async XLA Ops:
  0.1 0.9 %copy-start = (f32[4,2,3,3,2,2,128]{6,5,4,3,2,1,0:T(2,128)S(1)}, f32[4,2,3,3,2,2,128]{6,5,4,3,2,1,0:T(2,128)}, u32[]{:S(2)}) copy-start(f32[4,2,3,3,2,2,128]{6,5,4,3,2,1,0:T(2,128)} %param.2) | copy-start | bytes 442372
  1.0 0.9 %copy-start.2 = (f32[2,2,4,3,2,2,128]{6,5,4,3,2,1,0:T(2,128)S(1)}, f32[2,2,4,3,2,2,128]{6,5,4,3,2,1,0:T(2,128)}, u32[]{:S(2)}) copy-start(f32[2,2,4,3,2,2,128]{6,5,4,3,2,1,0:T(2,128)} %param.3) | copy-start | bytes 294916
  1.9 52.0 %copy-start.1 = (f32[4,2,3,3,2,2,128]{6,5,4,3,2,1,0:T(2,128)S(1)}, f32[4,2,3,3,2,2,128]{6,5,4,3,2,1,0:T(2,128)}, u32[]{:S(2)}) copy-start(f32[4,2,3,3,2,2,128]{6,5,4,3,2,1,0:T(2,128)} %param.2) | copy-start | bytes 442372
  1.9 52.0 %copy-start.3 = (f32[2,2,4,3,2,2,128]{6,5,4,3,2,1,0:T(2,128)S(1)}, f32[2,2,4,3,2,2,128]{6,5,4,3,2,1,0:T(2,128)}, u32[]{:S(2)}) copy-start(f32[2,2,4,3,2,2,128]{6,5,4,3,2,1,0:T(2,128)} %param.3) | copy-start | bytes 294916
  2.7 52.2 %collective-permute-start = (f32[30,4,128]{2,1,0:T(4,128)S(1)}, f32[30,4,128]{2,1,0:T(4,128)S(1)}, u32[]{:S(2)}, u32[]{:S(2)}) collective-permute-start(f32[30,4,128]{2,1,0:T(4,128)S(1)} %get-tuple-element.33), channel_id=1, source_target_pairs={{0,24},{8,0},{16,8},{24,16},{1,25},{9,1},{17,9},{25,17},{2,26},{10... | collective-permute-start | bytes 184328 | tf_op jit(solution)/shard_map/ppermute | solution.py:443
  26.2 28.7 %collective-permute-start.2 = (f32[30,4,128]{2,1,0:T(4,128)S(1)}, f32[30,4,128]{2,1,0:T(4,128)S(1)}, u32[]{:S(2)}, u32[]{:S(2)}) collective-permute-start(f32[30,4,128]{2,1,0:T(4,128)S(1)} %get-tuple-element.35), channel_id=1, source_target_pairs={{0,32},{32,0},{64,96},{96,64},{128,160},{160,128},{192,224},{224,1... | collective-permute-start | bytes 184328 | tf_op jit(solution)/shard_map/ppermute | solution.py:452
  29.3 25.6 %collective-permute-start.3 = (f32[30,4,128]{2,1,0:T(4,128)S(1)}, f32[30,4,128]{2,1,0:T(4,128)S(1)}, u32[]{:S(2)}, u32[]{:S(2)}) collective-permute-start(f32[30,4,128]{2,1,0:T(4,128)S(1)} %get-tuple-element.36), channel_id=1, source_target_pairs={{32,64},{64,32},{96,128},{128,96},{160,192},{192,160},{224,256},{2... | collective-permute-start | bytes 184328 | tf_op jit(solution)/shard_map/ppermute | solution.py:452
  36.2 18.7 %collective-permute-start.4 = (f32[30,4,128]{2,1,0:T(4,128)S(1)}, f32[30,4,128]{2,1,0:T(4,128)S(1)}, u32[]{:S(2)}, u32[]{:S(2)}) collective-permute-start(f32[30,4,128]{2,1,0:T(4,128)S(1)} %get-tuple-element.37), channel_id=1, source_target_pairs={{0,7},{1,0},{2,1},{3,2},{4,3},{5,4},{6,5},{7,6},{8,15},{9,8},{10,9... | collective-permute-start | bytes 184328 | tf_op jit(solution)/shard_map/ppermute | solution.py:443
  37.8 13.3 %collective-permute-start.1 = (f32[12,4,128]{2,1,0:T(4,128)S(1)}, f32[12,4,128]{2,1,0:T(4,128)S(1)}, u32[]{:S(2)}, u32[]{:S(2)}) collective-permute-start(f32[12,4,128]{2,1,0:T(4,128)S(1)} %get-tuple-element.34), channel_id=1, source_target_pairs={{0,8},{8,16},{16,24},{24,0},{1,9},{9,17},{17,25},{25,1},{2,10},{10... | collective-permute-start | bytes 73736 | tf_op jit(solution)/shard_map/ppermute | solution.py:443
  51.1 3.8 %collective-permute-start.5 = (f32[12,4,128]{2,1,0:T(4,128)S(1)}, f32[12,4,128]{2,1,0:T(4,128)S(1)}, u32[]{:S(2)}, u32[]{:S(2)}) collective-permute-start(f32[12,4,128]{2,1,0:T(4,128)S(1)} %get-tuple-element.38), channel_id=1, source_target_pairs={{0,1},{1,2},{2,3},{3,4},{4,5},{5,6},{6,7},{7,0},{8,9},{9,10},{10,1... | collective-permute-start | bytes 73736 | tf_op jit(solution)/shard_map/ppermute | solution.py:443
  57.1 30.5 %collective-permute-start.6 = (f32[12,4,128]{2,1,0:T(4,128)S(1)}, f32[12,4,128]{2,1,0:T(4,128)S(1)}, u32[]{:S(2)}, u32[]{:S(2)}) collective-permute-start(f32[12,4,128]{2,1,0:T(4,128)S(1)} %get-tuple-element.45), channel_id=1, source_target_pairs={{0,8},{8,16},{16,24},{24,0},{1,9},{9,17},{17,25},{25,1},{2,10},{10... | collective-permute-start | bytes 73736 | tf_op jit(solution)/shard_map/ppermute | solution.py:443
  59.0 28.5 %collective-permute-start.8 = (f32[12,4,128]{2,1,0:T(4,128)S(1)}, f32[12,4,128]{2,1,0:T(4,128)S(1)}, u32[]{:S(2)}, u32[]{:S(2)}) collective-permute-start(f32[12,4,128]{2,1,0:T(4,128)S(1)} %get-tuple-element.47), channel_id=1, source_target_pairs={{0,32},{32,0},{64,96},{96,64},{128,160},{160,128},{192,224},{224,1... | collective-permute-start | bytes 73736 | tf_op jit(solution)/shard_map/ppermute | solution.py:452
  61.0 26.6 %collective-permute-start.9 = (f32[12,4,128]{2,1,0:T(4,128)S(1)}, f32[12,4,128]{2,1,0:T(4,128)S(1)}, u32[]{:S(2)}, u32[]{:S(2)}) collective-permute-start(f32[12,4,128]{2,1,0:T(4,128)S(1)} %get-tuple-element.48), channel_id=1, source_target_pairs={{32,64},{64,32},{96,128},{128,96},{160,192},{192,160},{224,256},{2... | collective-permute-start | bytes 73736 | tf_op jit(solution)/shard_map/ppermute | solution.py:452
  68.7 18.9 %collective-permute-start.11 = (f32[12,4,128]{2,1,0:T(4,128)S(1)}, f32[12,4,128]{2,1,0:T(4,128)S(1)}, u32[]{:S(2)}, u32[]{:S(2)}) collective-permute-start(f32[12,4,128]{2,1,0:T(4,128)S(1)} %get-tuple-element.50), channel_id=1, source_target_pairs={{0,1},{1,2},{2,3},{3,4},{4,5},{5,6},{6,7},{7,0},{8,9},{9,10},{10,1... | collective-permute-start | bytes 73736 | tf_op jit(solution)/shard_map/ppermute | solution.py:443
  71.4 13.1 %collective-permute-start.7 = (f32[4,4,128]{2,1,0:T(4,128)S(1)}, f32[4,4,128]{2,1,0:T(4,128)S(1)}, u32[]{:S(2)}, u32[]{:S(2)}) collective-permute-start(f32[4,4,128]{2,1,0:T(4,128)S(1)} %get-tuple-element.46), channel_id=1, source_target_pairs={{0,24},{8,0},{16,8},{24,16},{1,25},{9,1},{17,9},{25,17},{2,26},{10... | collective-permute-start | bytes 24584 | tf_op jit(solution)/shard_map/ppermute | solution.py:443
  84.5 3.1 %collective-permute-start.10 = (f32[4,4,128]{2,1,0:T(4,128)S(1)}, f32[4,4,128]{2,1,0:T(4,128)S(1)}, u32[]{:S(2)}, u32[]{:S(2)}) collective-permute-start(f32[4,4,128]{2,1,0:T(4,128)S(1)} %get-tuple-element.49), channel_id=1, source_target_pairs={{0,7},{1,0},{2,1},{3,2},{4,3},{5,4},{6,5},{7,6},{8,15},{9,8},{10,9... | collective-permute-start | bytes 24584 | tf_op jit(solution)/shard_map/ppermute | solution.py:443

commit v3 on v2

v3 whole, which is shorter than its diff:
```python
import jax
import jax.numpy as jnp
from jax import lax
from jax.experimental import pallas as pl
from jax.experimental.pallas import tpu as pltpu
from jax.sharding import PartitionSpec as P


HOPPING = 0.125
PLAQUETTE = 0.5
INTERPRET = False

BLOCKS = (
    ((0, 1), (1, 1)),
    ((0, 1j), (1, -1j)),
    ((1, 1j), (0, 1j)),
    ((1, -1), (0, 1)),
)
T, Z, R, Y = 0, 1, 2, 3
OFF = ((0, 1), (0, 2), (1, 2))
ROWS = tuple((a, b) for a in range(2) for b in range(3))
SPINS = tuple((n, s, c) for n in range(2) for s in range(2) for c in range(3))


def add_phase(a, phase, b):
    if phase == 1:
        return (a[0] + b[0], a[1] + b[1])
    if phase == -1:
        return (a[0] - b[0], a[1] - b[1])
    if phase == 1j:
        return (a[0] - b[1], a[1] + b[0])
    return (a[0] + b[1], a[1] - b[0])


def cmul(a, b):
    return (a[0] * b[0] - a[1] * b[1], a[0] * b[1] + a[1] * b[0])


def cmulc(a, b):
    return (a[0] * b[0] + a[1] * b[1], a[1] * b[0] - a[0] * b[1])


def conj(a):
    return (a[0], -a[1])


def csum(terms):
    re, im = terms[0]
    for t in terms[1:]:
        re, im = re + t[0], im + t[1]
    return (re, im)


def csub(a, b):
    return (a[0] - b[0], a[1] - b[1])


def matmul(left, right):
    return [[csum([cmul(left[a][k], right[k][b]) for k in range(3)]) for b in range(3)] for a in range(3)]


def matmul_dagger(left, right):
    return [[csum([cmulc(left[a][k], right[b][k]) for k in range(3)]) for b in range(3)] for a in range(3)]


def third_row(m):
    u, v = m
    cross = lambda i, j: conj(csub(cmul(u[i], v[j]), cmul(u[j], v[i])))
    return [u, v, [cross(1, 2), cross(2, 0), cross(0, 1)]]


def antihermitian(m, scale):
    out = []
    for a, b in OFF:
        out.append((0.5 * scale) * (m[a][b][0] - m[b][a][0]))
        out.append((0.5 * scale) * (m[a][b][1] + m[b][a][1]))
    third = (m[0][0][1] + m[1][1][1] + m[2][2][1]) * (1.0 / 3.0)
    out.append(scale * (m[0][0][1] - third))
    out.append(scale * (m[1][1][1] - third))
    return out


def transport(x, w):
    e = {}
    for i, (a, b) in enumerate(OFF):
        e[a, b] = (x[2 * i], x[2 * i + 1])
        e[b, a] = (-x[2 * i], x[2 * i + 1])
    d = (x[6], x[7], -(x[6] + x[7]))
    v = []
    for a in range(3):
        row = []
        for j in range(3):
            terms = [(-d[a] * w[a][j][1], d[a] * w[a][j][0])]
            terms += [cmul(e[a, b], w[b][j]) for b in range(3) if b != a]
            row.append(csum(terms))
        v.append(row)
    out = []
    for i, j in OFF:
        t = csum([cmulc(v[a][j], w[a][i]) for a in range(3)])
        out += [t[0], t[1]]
    for i in range(2):
        s = None
        for a in range(3):
            p = v[a][i][1] * w[a][i][0] - v[a][i][0] * w[a][i][1]
            s = p if s is None else s + p
        out.append(s)
    return out


class Sites:
    def __init__(self):
        rows = lax.broadcasted_iota(jnp.int32, (4, 128), 0)
        lanes = lax.broadcasted_iota(jnp.int32, (4, 128), 1)
        self.first = (rows < 2, rows % 2 == 0, lanes < 64)
        self.y_last = lanes % 64 == 63
        self.y_first = lanes % 64 == 0

    def swap(self, v, d):
        if d == R:
            return pltpu.roll(v, 64, 1)
        if d == T:
            return jnp.concatenate([v[2:4], v[0:2]], axis=0)
        return jnp.where(
            self.first[Z],
            jnp.concatenate([v[1:4], v[0:1]], axis=0),
            jnp.concatenate([v[3:4], v[0:3]], axis=0),
        )

    def pack_low(self, a, b, d):
        return jnp.where(self.first[d], a, self.swap(b, d))

    def pack_high(self, a, b, d):
        return jnp.where(self.first[d], self.swap(b, d), a)

    def ahead(self, a, b, m, d):
        return (
            self.swap(jnp.where(self.first[d], m, a), d),
            jnp.where(self.first[d], self.swap(b, d), m),
        )

    def behind(self, a, b, m, d):
        return (
            self.swap(jnp.where(self.first[d], a, m), d),
            jnp.where(self.first[d], m, self.swap(b, d)),
        )

    def y_ahead(self, v):
        return jnp.where(self.y_last, pltpu.roll(v, 63, 1), pltpu.roll(v, 127, 1))

    def y_behind(self, v):
        return jnp.where(self.y_first, pltpu.roll(v, 65, 1), pltpu.roll(v, 1, 1))


def link(ref, mu, rows=3):
    return [[tuple(ref[(mu * 2 + c) * 9 + a * 3 + b] for c in range(2)) for b in range(3)] for a in range(rows)]


def spinor(ref, n, s, c):
    return tuple(ref[((n * 2 + k) * 4 + s) * 3 + c] for k in range(2))


def upper(ref, mu, sign, n, s, c):
    col, phase = BLOCKS[mu][s]
    return add_phase(spinor(ref, n, s, c), sign * phase, spinor(ref, n, 2 + col, c))


def half(ref, mu, sign):
    return {k: upper(ref, mu, sign, *k) for k in SPINS}


def flat_half(h):
    return [h[k][c] for k in SPINS for c in range(2)]


def unflat_half(flat):
    return {k: (flat[2 * i], flat[2 * i + 1]) for i, k in enumerate(SPINS)}


def apply(m, h):
    return {(n, s, a): csum([cmul(m[a][b], h[n, s, b]) for b in range(3)]) for n, s, a in SPINS}


def apply_dagger(m, h):
    return {(n, s, a): csum([cmulc(h[n, s, b], m[b][a]) for b in range(3)]) for n, s, a in SPINS}


def others(d):
    return [nu for nu in range(4) if nu != d]


def row_values(lref, nus):
    out = []
    for nu in nus:
        m = link(lref, nu, 2)
        out += [m[a][b][c] for a, b in ROWS for c in range(2)]
    return out


def rows_of(flat):
    return [[(flat[(a * 3 + b) * 2], flat[(a * 3 + b) * 2 + 1]) for b in range(3)] for a in range(2)]


def put(ref, at, flat):
    for i, v in enumerate(flat):
        ref[at + i] = v


def get(ref, at, n):
    return [ref[at + i] for i in range(n)]


LOW_LINKS, LOW = 18, 30
HIGH_LINKS, HIGH = 24, 36
AGAIN = 16


def pack_kernel(flags, lref, xref, zd, zu, ta, tb, rd, ru, gref):
    sites = Sites()
    for d in (Z, T, R):
        g = flat_half(apply_dagger(link(lref, d), half(xref, d, 1)))
        put(gref, 24 * d, g)
        low = row_values(lref, others(d)) + flat_half(half(xref, d, -1))
        high = row_values(lref, range(4)) + g
        low = [sites.pack_low(low[2 * i], low[2 * i + 1], d) for i in range(LOW)]
        high = [sites.pack_high(high[2 * i], high[2 * i + 1], d) for i in range(HIGH)]
        if d != T:
            put(zd if d == Z else rd, 0, low)
            put(zu if d == Z else ru, 0, high)
            continue
        low = low[:LOW_LINKS] + [jnp.where(flags[0] == 0, -v, v) for v in low[LOW_LINKS:]]
        high = high[:HIGH_LINKS] + [jnp.where(flags[1] == 0, -v, v) for v in high[HIGH_LINKS:]]
        even = flags[2] == 1
        for i in range(HIGH):
            x = low[i] if i < LOW else high[i]
            ta[i] = jnp.where(even, high[i], x)
            tb[i] = jnp.where(even, x, high[i])


class Halo:
    def __init__(self, flags, zd, zu, ta, tb, rd, ru):
        self.even = flags[2] == 1
        self.refs = {Z: (zd, zu), T: (ta, tb), R: (rd, ru)}

    def low(self, d, i):
        first, second = self.refs[d]
        return jnp.where(self.even, first[i], second[i]) if d == T else first[i]

    def high(self, d, i):
        first, second = self.refs[d]
        return jnp.where(self.even, second[i], first[i]) if d == T else second[i]

    def ahead(self, sites, d, own, at):
        out = []
        for i in range(len(own) // 2):
            out += sites.ahead(own[2 * i], own[2 * i + 1], self.low(d, at + i), d)
        return out

    def behind(self, sites, d, own, at):
        out = []
        for i in range(len(own) // 2):
            out += sites.behind(own[2 * i], own[2 * i + 1], self.high(d, at + i), d)
        return out


def local_kernel(lref, xref, yref, wref, gyref, m2ref):
    sites = Sites()
    u = link(lref, Y)
    h = {k: tuple(sites.y_ahead(v) for v in c) for k, c in half(xref, Y, -1).items()}
    w = apply(u, h)
    g = {k: tuple(sites.y_behind(v) for v in c) for k, c in apply_dagger(u, half(xref, Y, 1)).items()}
    put(wref, 0, flat_half(w))
    put(gyref, 0, flat_half(g))
    for n in range(2):
        for s in range(2):
            for c in range(3):
                x = spinor(xref, n, s, c)
                store_spinor(yref, n, s, c, [x[i] - HOPPING * (w[n, s, c][i] + g[n, s, c][i]) for i in range(2)])
        for r in range(2):
            col, phase = BLOCKS[Y][r]
            for c in range(3):
                x = spinor(xref, n, 2 + col, c)
                diff = [g[n, r, c][i] - w[n, r, c][i] for i in range(2)]
                term = add_phase((0.0, 0.0), complex(phase).conjugate(), diff)
                store_spinor(yref, n, 2 + col, c, [x[i] - HOPPING * term[i] for i in range(2)])
    for mu in range(3):
        m = [[tuple(sites.y_ahead(v) for v in e) for e in row] for row in link(lref, mu)]
        m2 = matmul(u, m)
        put(m2ref, 18 * mu, [m2[a][b][c] for a in range(3) for b in range(3) for c in range(2)])


def store_spinor(ref, n, s, c, value):
    for k in range(2):
        ref[((n * 2 + k) * 4 + s) * 3 + c] = value[k]


def mat_at(ref, at):
    return [[(ref[at + (a * 3 + b) * 2], ref[at + (a * 3 + b) * 2 + 1]) for b in range(3)] for a in range(3)]


def put_mat(ref, at, m):
    put(ref, at, [m[a][b][c] for a in range(3) for b in range(3) for c in range(2)])


def add_hops(yref, d, w, g):
    for n in range(2):
        for s in range(2):
            for c in range(3):
                y = spinor(yref, n, s, c)
                store_spinor(yref, n, s, c, [y[i] - HOPPING * (w[n, s, c][i] + g[n, s, c][i]) for i in range(2)])
        for r in range(2):
            col, phase = BLOCKS[d][r]
            for c in range(3):
                diff = [HOPPING * (g[n, r, c][i] - w[n, r, c][i]) for i in range(2)]
                y = add_phase(spinor(yref, n, 2 + col, c), -complex(phase).conjugate(), diff)
                store_spinor(yref, n, 2 + col, c, y)


def outer(p, q):
    return [
        [csum([cmulc(p[n, s, a], q[n, s, b]) for n in range(2) for s in range(2)]) for b in range(3)]
        for a in range(3)
    ]


def partner_kernel(
    flags, lref, xref, gref, ylref, zd, zu, ta, tb, rd, ru,
    oz, ot, orow, oy, ow, on, ob,
):
    sites = Sites()
    halo = Halo(flags, zd, zu, ta, tb, rd, ru)
    put(oy, 0, get(ylref, 0, 48))
    kept = []
    for d in range(3):
        h = unflat_half(halo.ahead(sites, d, flat_half(half(xref, d, -1)), LOW_LINKS))
        g = unflat_half(halo.behind(sites, d, get(gref, 24 * d, 24), HIGH_LINKS))
        w = apply(link(lref, d), h)
        put(ow, 24 * d, flat_half(w))
        add_hops(oy, d, w, g)
        kept.append(g)
        put(ob, 12 * d, halo.behind(sites, d, row_values(lref, (d,)), 6 * d))
    for mu in (Z, T, R):
        part = antihermitian(outer(half(oy, mu, 1), kept[mu]), HOPPING)
        put(on, 8 * mu, part)
        moved = part + [v for d in range(3) if d != mu for v in get(ob, 12 * d, 12)]
        ref = {Z: oz, T: ot, R: orow}[mu]
        put(ref, 0, [sites.pack_low(moved[2 * i], moved[2 * i + 1], mu) for i in range(AGAIN)])


def adjoint(m):
    return [[conj(m[b][a]) for b in range(3)] for a in range(3)]


def gauge_kernel(
    flags, lref, yref, wref, wyref, gyref, m2ref, zd, zu, ta, tb, rd, ru, obase, oq, fref, bref,
):
    sites = Sites()
    halo = Halo(flags, zd, zu, ta, tb, rd, ru)
    slot = {}
    for d in range(3):
        flat = halo.ahead(sites, d, row_values(lref, others(d)), 0)
        for k, nu in enumerate(others(d)):
            slot[d, nu] = 18 * (3 * d + k)
            put_mat(fref, slot[d, nu], third_row(rows_of(flat[12 * k : 12 * k + 12])))
    base = [[0.0] * 8 for _ in range(4)]

    def add(mu, part):
        base[mu] = [a + b for a, b in zip(base[mu], part)]

    for mu in range(4):
        for nu in range(mu + 1, 4):
            m1 = matmul(link(lref, mu), mat_at(fref, slot[mu, nu]))
            m2 = mat_at(m2ref, 18 * mu) if nu == Y else matmul(link(lref, nu), mat_at(fref, slot[nu, mu]))
            p = antihermitian(matmul_dagger(m1, m2), PLAQUETTE)
            add(mu, p)
            add(nu, [-v for v in p])
            if nu == Y:
                add(mu, [-sites.y_behind(v) for v in transport(p, link(lref, Y))])
    for d in range(3):
        flat = halo.behind(sites, d, row_values(lref, range(4)), 0)
        for nu in range(4):
            put_mat(bref, 18 * nu, third_row(rows_of(flat[12 * nu : 12 * nu + 12])))
        b_d = mat_at(bref, 18 * d)
        slot_q = 0
        for mu in others(d):
            q = matmul(adjoint(mat_at(bref, 18 * mu)), b_d)
            if mu == Y:
                c = [[tuple(sites.y_ahead(v) for v in e) for e in row] for row in b_d]
                v = matmul(adjoint(c), q)
                add(Y, antihermitian(matmul(link(lref, Y), v), PLAQUETTE))
            else:
                put_mat(oq, 18 * (2 * d + slot_q), [[(PLAQUETTE * e[0], PLAQUETTE * e[1]) for e in row] for row in q])
                slot_q += 1
    for mu in range(4):
        w = unflat_half(get(wref, 24 * mu, 24) if mu != Y else get(wyref, 0, 24))
        add(mu, antihermitian(outer(w, half(yref, mu, -1)), HOPPING))
    part = antihermitian(outer(half(yref, Y, 1), unflat_half(get(gyref, 0, 24))), HOPPING)
    add(Y, transport([sites.y_ahead(v) for v in part], adjoint(link(lref, Y))))
    for mu in range(4):
        put(obase, 8 * mu, base[mu])


def times_dagger(x, u):
    e = {}
    for i, (a, b) in enumerate(OFF):
        e[a, b] = (x[2 * i], x[2 * i + 1])
        e[b, a] = (-x[2 * i], x[2 * i + 1])
    d = (x[6], x[7], -(x[6] + x[7]))
    return [
        [
            csum([(d[a] * u[j][a][1], d[a] * u[j][a][0])] + [cmulc(e[a, b], u[j][b]) for b in range(3) if b != a])
            for j in range(3)
        ]
        for a in range(3)
    ]


def last_kernel(lref, baseref, nref, bref, qref, zd, td, rd, oref):
    sites = Sites()
    zero = jnp.zeros((4, 128), jnp.float32)
    for mu in range(4):
        x = get(baseref, 8 * mu, 8)
        if mu != Y:
            m = {Z: zd, T: td, R: rd}[mu]
            others_of = [d for d in range(3) if d != mu]
            own = get(nref, 8 * mu, 8) + [v for d in others_of for v in get(bref, 12 * d, 12)]
            ahead = []
            for i in range(AGAIN):
                ahead += sites.ahead(own[2 * i], own[2 * i + 1], m[i], mu)
            u = link(lref, mu)
            total = times_dagger(ahead[:8], u)
            for k, d in enumerate(others_of):
                c = third_row(rows_of(ahead[8 + 12 * k : 20 + 12 * k]))
                slot_q = [e for e in others(d)].index(mu)
                v = matmul(adjoint(c), mat_at(qref, 18 * (2 * d + slot_q)))
                total = [[csum([total[a][b], v[a][b]]) for b in range(3)] for a in range(3)]
            x = [p + q for p, q in zip(x, antihermitian(matmul(u, total), 1.0))]
        at = mu * 18
        for i, (a, b) in enumerate(OFF):
            oref[at + a * 3 + b] = x[2 * i]
            oref[at + b * 3 + a] = -x[2 * i]
            oref[at + 9 + a * 3 + b] = x[2 * i + 1]
            oref[at + 9 + b * 3 + a] = x[2 * i + 1]
        for a in range(3):
            oref[at + a * 4] = zero
        oref[at + 9] = x[6]
        oref[at + 13] = x[7]
        oref[at + 17] = -(x[6] + x[7])


def call(body, operands, outs, flops, scratch=()):
    specs = [
        pl.BlockSpec(memory_space=pltpu.SMEM if o.dtype == jnp.int32 else pltpu.VMEM) for o in operands
    ]
    return pl.pallas_call(
        body,
        in_specs=specs,
        out_specs=[pl.BlockSpec(memory_space=pltpu.VMEM) for _ in outs],
        out_shape=[jax.ShapeDtypeStruct((n, 4, 128), jnp.float32) for n in outs],
        scratch_shapes=[pltpu.VMEM((n, 4, 128), jnp.float32) for n in scratch],
        cost_estimate=pl.CostEstimate(flops=flops, bytes_accessed=4 * 512 * 200, transcendentals=0),
        compiler_params=pltpu.CompilerParams(vmem_limit_bytes=8 * 1024 * 1024),
        interpret=INTERPRET,
    )(*operands)


def move(x, axis, by):
    size = lax.axis_size(axis)
    return lax.ppermute(x, axis, [(i, (i + by) % size) for i in range(size)])


def meet(x, axis, first):
    size = lax.axis_size(axis)
    pairs = []
    for i in range(0 if first else 1, size, 2):
        j = (i + 1) % size
        pairs += [(i, j), (j, i)]
    return lax.ppermute(x, axis, pairs)


def on_device(links, solutions):
    shape = links.shape
    lk = links.reshape(72, 4, 128)
    xs = solutions.reshape(48, 4, 128)
    t = lax.axis_index("ta")
    flags = jnp.stack([t, lax.axis_size("ta") - 1 - t, 1 - t % 2]).astype(jnp.int32)
    zd, zu, ta, tb, rd, ru, g = call(pack_kernel, (flags, lk, xs), (LOW, HIGH, HIGH, HIGH, LOW, HIGH, 72), 4_000_000)
    zu = move(zu, "gz", 1)
    zd = move(zd, "gz", -1)
    tb = meet(tb, "ta", False)
    ta = meet(ta, "ta", True)
    rd = move(rd, "xy", -1)
    ru = move(ru, "xy", 1)
    got = (zd, zu, ta, tb, rd, ru)
    yl, wy, gy, m2 = call(local_kernel, (lk, xs), (48, 24, 24, 54), 20_000_000)
    oz, ot, orow, y, w, n, b = call(
        partner_kernel, (flags, lk, xs, g, yl, *got), (AGAIN, AGAIN, AGAIN, 48, 72, 24, 36), 20_000_000
    )
    oz = move(oz, "gz", -1)
    ot = move(ot, "ta", -1)
    orow = move(orow, "xy", -1)
    base, q = call(gauge_kernel, (flags, lk, y, w, wy, gy, m2, *got), (32, 108), 20_000_000, (162, 72))
    (force,) = call(last_kernel, (lk, base, n, b, q, oz, ot, orow), (72,), 4_000_000)
    return force.reshape(shape)


def solution(mesh):
    spec = P(None, None, None, None, "ta", "gz", "xy")

    return jax.shard_map(on_device, mesh=mesh, in_specs=(spec, spec), out_specs=spec, check_vma=False)
```

time: 90.4 us -> 75 us (0.83); the launches traced: 89 us -> 74.7 us
  waiting for transfers between devices: 13.9 us -> 4.73 us
  starting transfers between devices: 68.3 us -> 62.4 us
    ppermute x8 -> x7, waiting for transfers between devices: 13.9 us -> 4.43 us  [move(): return lax.ppermute(x, axis, [(i, (i + by) % size) for i in range(size)])]
    ppermute x4 -> x2, starting transfers between devices: 19.7 us -> 10.3 us  [meet(): return lax.ppermute(x, axis, pairs)]
    ppermute x8 -> x7, starting transfers between devices: 48.6 us -> 52.1 us  [move(): return lax.ppermute(x, axis, [(i, (i + by) % size) for i in range(size)])]
  transfers between devices with their start and end apart: 12 -> 9, of which waited for: 4 -> 3; matrix products, arithmetic and copies ran while one was open for 0% -> 0% of each run, Pallas kernels for 1% -> 3%
where the time goes in v3:
time: 75 us; the launch traced here: 74.7 us
  starting transfers between devices  62.4 us (83%)
  Pallas kernels  5.62 us (7%)
  waiting for transfers between devices  4.73 us (6%)
  local copies, waits for them, and re-layouts  1.81 us (2%)
    ppermute x7, starting transfers between devices, move(): return lax.ppermute(x, axis, [(i, (i + by) % size) for i in range(size)])  52.1 us
    ppermute x2, starting transfers between devices, meet(): return lax.ppermute(x, axis, pairs)  10.3 us
    pallas_call x5, Pallas kernels, call(): pl.pallas_call(body, in_specs=specs, out_specs=[pl.BlockSpec(memory_space...  5.62 us
    ppermute x7, waiting for transfers between devices, move(): return lax.ppermute(x, axis, [(i, (i + by) % size) for i in range(size)])  4.43 us
    unnamed x8, local copies, waits for them, and re-layouts  1.81 us
  transfers between devices with their start and end apart: 9, of which 3 were waited for; matrix products, arithmetic and copies ran while one was open for 0% of the time, Pallas kernels for 3%

profile of v3, /device:TPU:1, one launch (start us, length us, event | category | flops | bytes accessed | tf_op | source)
XLA Modules:
  0.0 74.7 jit_solution(6887913774148385849)
XLA Ops:
  0.0 0.1 pad_add_fusion.flags
  0.1 0.9 %copy-done = f32[4,2,3,3,2,2,128]{6,5,4,3,2,1,0:T(2,128)S(1)} copy-done((f32[4,2,3,3,2,2,128]{6,5,4,3,2,1,0:T(2,128)S(1)}, f32[4,2,3,3,2,2,128]{6,5,4,3,2,1,0:T(2,128)}, u32[]{:S(2)}) %copy-start) | copy-done | bytes 147480
  1.0 0.9 %copy-done.2 = f32[2,2,4,3,2,2,128]{6,5,4,3,2,1,0:T(2,128)S(1)} copy-done((f32[2,2,4,3,2,2,128]{6,5,4,3,2,1,0:T(2,128)S(1)}, f32[2,2,4,3,2,2,128]{6,5,4,3,2,1,0:T(2,128)}, u32[]{:S(2)}) %copy-start.2) | copy-done | bytes 98328
  1.9 0.8 %shard_map.28 = (f32[30,4,128]{2,1,0:T(4,128)S(1)}, f32[36,4,128]{2,1,0:T(4,128)S(1)}, f32[36,4,128]{2,1,0:T(4,128)S(1)}, f32[36,4,128]{2,1,0:T(4,128)S(1)}, f32...) custom-call(s32[3]{0:T(128)S(1)} %pad_add_fusion.flags, f32[72,4,128]{2,1,0:T(4,128)S(1)} %bitcast.6, ...), custom_call_target="tpu_custom_call" | custom-call | flops 4000000 | bytes 409600 | tf_op jit(solution)/shard_map/pallas_call | solution.py:454
  2.7 23.5 %collective-permute-start = (f32[30,4,128]{2,1,0:T(4,128)S(1)}, f32[30,4,128]{2,1,0:T(4,128)S(1)}, u32[]{:S(2)}, u32[]{:S(2)}) collective-permute-start(f32[30,4,128]{2,1,0:T(4,128)S(1)} %get-tuple-element.27), channel_id=1, source_target_pairs={{0,24},{8,0},{16,8},{24,16},{1,25},{9,1},{17,9},{25,17},{2,26},{10... | collective-permute-start | bytes 184328 | tf_op jit(solution)/shard_map/ppermute | solution.py:468
  26.2 1.9 %collective-permute-start.1 = (f32[36,4,128]{2,1,0:T(4,128)S(1)}, f32[36,4,128]{2,1,0:T(4,128)S(1)}, u32[]{:S(2)}, u32[]{:S(2)}) collective-permute-start(f32[36,4,128]{2,1,0:T(4,128)S(1)} %get-tuple-element.28), channel_id=1, source_target_pairs={{0,8},{8,16},{16,24},{24,0},{1,9},{9,17},{17,25},{25,1},{2,10},{10... | collective-permute-start | bytes 221192 | tf_op jit(solution)/shard_map/ppermute | solution.py:468
  28.2 3.1 %collective-permute-start.2 = (f32[36,4,128]{2,1,0:T(4,128)S(1)}, f32[36,4,128]{2,1,0:T(4,128)S(1)}, u32[]{:S(2)}, u32[]{:S(2)}) collective-permute-start(f32[36,4,128]{2,1,0:T(4,128)S(1)} %get-tuple-element.29), channel_id=1, source_target_pairs={{0,32},{32,0},{64,96},{96,64},{128,160},{160,128},{192,224},{224,1... | collective-permute-start | bytes 221192 | tf_op jit(solution)/shard_map/ppermute | solution.py:477
  31.3 7.1 %collective-permute-start.3 = (f32[36,4,128]{2,1,0:T(4,128)S(1)}, f32[36,4,128]{2,1,0:T(4,128)S(1)}, u32[]{:S(2)}, u32[]{:S(2)}) collective-permute-start(f32[36,4,128]{2,1,0:T(4,128)S(1)} %get-tuple-element.30), channel_id=1, source_target_pairs={{32,64},{64,32},{96,128},{128,96},{160,192},{192,160},{224,256},{2... | collective-permute-start | bytes 221192 | tf_op jit(solution)/shard_map/ppermute | solution.py:477
  38.4 2.7 %collective-permute-start.5 = (f32[36,4,128]{2,1,0:T(4,128)S(1)}, f32[36,4,128]{2,1,0:T(4,128)S(1)}, u32[]{:S(2)}, u32[]{:S(2)}) collective-permute-start(f32[36,4,128]{2,1,0:T(4,128)S(1)} %get-tuple-element.32), channel_id=1, source_target_pairs={{0,1},{1,2},{2,3},{3,4},{4,5},{5,6},{6,7},{7,0},{8,9},{9,10},{10,1... | collective-permute-start | bytes 221192 | tf_op jit(solution)/shard_map/ppermute | solution.py:468
  41.2 0.0 collective-permute-done.zd
  41.2 0.3 shard_map.29
  41.5 3.6 %collective-permute-done.4.rd = f32[30,4,128]{2,1,0:T(4,128)S(1)} collective-permute-done((f32[30,4,128]{2,1,0:T(4,128)S(1)}, f32[30,4,128]{2,1,0:T(4,128)S(1)}, u32[]{:S(2)}, u32[]{:S(2)}) %collective-permute-start.4) | collective-permute-done | bytes 61472 | tf_op jit(solution)/shard_map/ppermute | solution.py:468
  45.1 0.0 collective-permute-done.1.zu
  45.1 0.0 collective-permute-done.2.ta
  45.1 0.3 collective-permute-done.3.tb
  45.4 0.0 collective-permute-done.5.ru
  45.4 1.1 %shard_map.30 = (f32[16,4,128]{2,1,0:T(4,128)S(1)}, f32[16,4,128]{2,1,0:T(4,128)S(1)}, f32[16,4,128]{2,1,0:T(4,128)S(1)}, f32[48,4,128]{2,1,0:T(4,128)S(1)}, f32...) custom-call(s32[3]{0:T(128)S(1)} %pad_add_fusion.flags, f32[72,4,128]{2,1,0:T(4,128)S(1)} %bitcast.8, ...), custom_call_target="tpu_custom_call" | custom-call | flops 20000000 | bytes 409600 | tf_op jit(solution)/shard_map/pallas_call | solution.py:454
  46.5 11.8 %collective-permute-start.6 = (f32[16,4,128]{2,1,0:T(4,128)S(1)}, f32[16,4,128]{2,1,0:T(4,128)S(1)}, u32[]{:S(2)}, u32[]{:S(2)}) collective-permute-start(f32[16,4,128]{2,1,0:T(4,128)S(1)} %get-tuple-element.42), channel_id=1, source_target_pairs={{0,24},{8,0},{16,8},{24,16},{1,25},{9,1},{17,9},{25,17},{2,26},{10... | collective-permute-start | bytes 98312 | tf_op jit(solution)/shard_map/ppermute | solution.py:468
  58.4 10.3 %collective-permute-start.7 = (f32[16,4,128]{2,1,0:T(4,128)S(1)}, f32[16,4,128]{2,1,0:T(4,128)S(1)}, u32[]{:S(2)}, u32[]{:S(2)}) collective-permute-start(f32[16,4,128]{2,1,0:T(4,128)S(1)} %get-tuple-element.43), channel_id=1, source_target_pairs={{0,992},{32,0},{64,32},{96,64},{128,96},{160,128},{192,160},{224,1... | collective-permute-start | bytes 98312 | tf_op jit(solution)/shard_map/ppermute | solution.py:468
  68.7 1.9 %collective-permute-start.8 = (f32[16,4,128]{2,1,0:T(4,128)S(1)}, f32[16,4,128]{2,1,0:T(4,128)S(1)}, u32[]{:S(2)}, u32[]{:S(2)}) collective-permute-start(f32[16,4,128]{2,1,0:T(4,128)S(1)} %get-tuple-element.44), channel_id=1, source_target_pairs={{0,7},{1,0},{2,1},{3,2},{4,3},{5,4},{6,5},{7,6},{8,15},{9,8},{10,9... | collective-permute-start | bytes 98312 | tf_op jit(solution)/shard_map/ppermute | solution.py:468
  70.5 2.2 %shard_map.31 = (f32[32,4,128]{2,1,0:T(4,128)S(1)}, f32[108,4,128]{2,1,0:T(4,128)S(1)}) custom-call(s32[3]{0:T(128)S(1)} %pad_add_fusion.flags, f32[72,4,128]{2,1,0:T(4,128)S(1)} %bitcast.9, f32[48,4,128]{2,1,0:T(4,128)S(1)} %get-tuple-element.33.yref, f32[72,4,128]{2,1,0:T(4,128)S(1)} %get-tuple-element.34.wref, f32[24,4,128]{2,1,0:T(4,128)S(1)} %get-tuple-element.35.wyref, ...), custom_call_target="tpu_custom_call" | custom-call | flops 20000000 | bytes 409600 | tf_op jit(solution)/shard_map/pallas_call | solution.py:454
  72.8 0.0 collective-permute-done.7.td
  72.8 0.8 %collective-permute-done.8.rd = f32[16,4,128]{2,1,0:T(4,128)S(1)} collective-permute-done((f32[16,4,128]{2,1,0:T(4,128)S(1)}, f32[16,4,128]{2,1,0:T(4,128)S(1)}, u32[]{:S(2)}, u32[]{:S(2)}) %collective-permute-start.8) | collective-permute-done | bytes 32800 | tf_op jit(solution)/shard_map/ppermute | solution.py:468
  73.6 1.2 %shard_map.32 = f32[72,4,128]{2,1,0:T(4,128)} custom-call(f32[72,4,128]{2,1,0:T(4,128)S(1)} %bitcast.10, f32[32,4,128]{2,1,0:T(4,128)S(1)} %get-tuple-element.38.baseref, f32[24,4,128]{2,1,0:T(4,128)S(1)} %get-tuple-element.39.nref, f32[36,4,128]{2,1,0:T(4,128)S(1)} %get-tuple-element.40.bref, f32[108,4,128]{2,1,0:T(4,128)S(1)} %get-tuple-element.41.qref, ...), custom_call_target="tpu_custom_call" | custom-call | flops 4000000 | bytes 409600 | tf_op jit(solution)/shard_map/pallas_call | solution.py:454
  (8 shorter events, 0.0 us)
Async XLA Ops:
  0.1 0.9 %copy-start = (f32[4,2,3,3,2,2,128]{6,5,4,3,2,1,0:T(2,128)S(1)}, f32[4,2,3,3,2,2,128]{6,5,4,3,2,1,0:T(2,128)}, u32[]{:S(2)}) copy-start(f32[4,2,3,3,2,2,128]{6,5,4,3,2,1,0:T(2,128)} %param.2) | copy-start | bytes 442372
  1.0 0.9 %copy-start.2 = (f32[2,2,4,3,2,2,128]{6,5,4,3,2,1,0:T(2,128)S(1)}, f32[2,2,4,3,2,2,128]{6,5,4,3,2,1,0:T(2,128)}, u32[]{:S(2)}) copy-start(f32[2,2,4,3,2,2,128]{6,5,4,3,2,1,0:T(2,128)} %param.3) | copy-start | bytes 294916
  1.9 39.3 %copy-start.1 = (f32[4,2,3,3,2,2,128]{6,5,4,3,2,1,0:T(2,128)S(1)}, f32[4,2,3,3,2,2,128]{6,5,4,3,2,1,0:T(2,128)}, u32[]{:S(2)}) copy-start(f32[4,2,3,3,2,2,128]{6,5,4,3,2,1,0:T(2,128)} %param.2) | copy-start | bytes 442372
  1.9 39.3 %copy-start.3 = (f32[2,2,4,3,2,2,128]{6,5,4,3,2,1,0:T(2,128)S(1)}, f32[2,2,4,3,2,2,128]{6,5,4,3,2,1,0:T(2,128)}, u32[]{:S(2)}) copy-start(f32[2,2,4,3,2,2,128]{6,5,4,3,2,1,0:T(2,128)} %param.3) | copy-start | bytes 294916
  2.7 38.5 %collective-permute-start = (f32[30,4,128]{2,1,0:T(4,128)S(1)}, f32[30,4,128]{2,1,0:T(4,128)S(1)}, u32[]{:S(2)}, u32[]{:S(2)}) collective-permute-start(f32[30,4,128]{2,1,0:T(4,128)S(1)} %get-tuple-element.27), channel_id=1, source_target_pairs={{0,24},{8,0},{16,8},{24,16},{1,25},{9,1},{17,9},{25,17},{2,26},{10... | collective-permute-start | bytes 184328 | tf_op jit(solution)/shard_map/ppermute | solution.py:468
  26.2 18.9 %collective-permute-start.1 = (f32[36,4,128]{2,1,0:T(4,128)S(1)}, f32[36,4,128]{2,1,0:T(4,128)S(1)}, u32[]{:S(2)}, u32[]{:S(2)}) collective-permute-start(f32[36,4,128]{2,1,0:T(4,128)S(1)} %get-tuple-element.28), channel_id=1, source_target_pairs={{0,8},{8,16},{16,24},{24,0},{1,9},{9,17},{17,25},{25,1},{2,10},{10... | collective-permute-start | bytes 221192 | tf_op jit(solution)/shard_map/ppermute | solution.py:468
  28.2 16.9 %collective-permute-start.2 = (f32[36,4,128]{2,1,0:T(4,128)S(1)}, f32[36,4,128]{2,1,0:T(4,128)S(1)}, u32[]{:S(2)}, u32[]{:S(2)}) collective-permute-start(f32[36,4,128]{2,1,0:T(4,128)S(1)} %get-tuple-element.29), channel_id=1, source_target_pairs={{0,32},{32,0},{64,96},{96,64},{128,160},{160,128},{192,224},{224,1... | collective-permute-start | bytes 221192 | tf_op jit(solution)/shard_map/ppermute | solution.py:477
  31.3 14.1 %collective-permute-start.3 = (f32[36,4,128]{2,1,0:T(4,128)S(1)}, f32[36,4,128]{2,1,0:T(4,128)S(1)}, u32[]{:S(2)}, u32[]{:S(2)}) collective-permute-start(f32[36,4,128]{2,1,0:T(4,128)S(1)} %get-tuple-element.30), channel_id=1, source_target_pairs={{32,64},{64,32},{96,128},{128,96},{160,192},{192,160},{224,256},{2... | collective-permute-start | bytes 221192 | tf_op jit(solution)/shard_map/ppermute | solution.py:477
  38.4 7.0 %collective-permute-start.5 = (f32[36,4,128]{2,1,0:T(4,128)S(1)}, f32[36,4,128]{2,1,0:T(4,128)S(1)}, u32[]{:S(2)}, u32[]{:S(2)}) collective-permute-start(f32[36,4,128]{2,1,0:T(4,128)S(1)} %get-tuple-element.32), channel_id=1, source_target_pairs={{0,1},{1,2},{2,3},{3,4},{4,5},{5,6},{6,7},{7,0},{8,9},{9,10},{10,1... | collective-permute-start | bytes 221192 | tf_op jit(solution)/shard_map/ppermute | solution.py:468
  41.2 3.9 %collective-permute-start.4 = (f32[30,4,128]{2,1,0:T(4,128)S(1)}, f32[30,4,128]{2,1,0:T(4,128)S(1)}, u32[]{:S(2)}, u32[]{:S(2)}) collective-permute-start(f32[30,4,128]{2,1,0:T(4,128)S(1)} %get-tuple-element.31), channel_id=1, source_target_pairs={{0,7},{1,0},{2,1},{3,2},{4,3},{5,4},{6,5},{7,6},{8,15},{9,8},{10,9... | collective-permute-start | bytes 184328 | tf_op jit(solution)/shard_map/ppermute | solution.py:468
  46.5 26.2 %collective-permute-start.6 = (f32[16,4,128]{2,1,0:T(4,128)S(1)}, f32[16,4,128]{2,1,0:T(4,128)S(1)}, u32[]{:S(2)}, u32[]{:S(2)}) collective-permute-start(f32[16,4,128]{2,1,0:T(4,128)S(1)} %get-tuple-element.42), channel_id=1, source_target_pairs={{0,24},{8,0},{16,8},{24,16},{1,25},{9,1},{17,9},{25,17},{2,26},{10... | collective-permute-start | bytes 98312 | tf_op jit(solution)/shard_map/ppermute | solution.py:468
  58.4 14.4 %collective-permute-start.7 = (f32[16,4,128]{2,1,0:T(4,128)S(1)}, f32[16,4,128]{2,1,0:T(4,128)S(1)}, u32[]{:S(2)}, u32[]{:S(2)}) collective-permute-start(f32[16,4,128]{2,1,0:T(4,128)S(1)} %get-tuple-element.43), channel_id=1, source_target_pairs={{0,992},{32,0},{64,32},{96,64},{128,96},{160,128},{192,160},{224,1... | collective-permute-start | bytes 98312 | tf_op jit(solution)/shard_map/ppermute | solution.py:468
  68.7 4.9 %collective-permute-start.8 = (f32[16,4,128]{2,1,0:T(4,128)S(1)}, f32[16,4,128]{2,1,0:T(4,128)S(1)}, u32[]{:S(2)}, u32[]{:S(2)}) collective-permute-start(f32[16,4,128]{2,1,0:T(4,128)S(1)} %get-tuple-element.44), channel_id=1, source_target_pairs={{0,7},{1,0},{2,1},{3,2},{4,3},{5,4},{6,5},{7,6},{8,15},{9,8},{10,9... | collective-permute-start | bytes 98312 | tf_op jit(solution)/shard_map/ppermute | solution.py:468

commit v4 on v3

--- a/solution.py
+++ b/solution.py
@@ -214,8 +214,16 @@
 AGAIN = 16
 
 
-def pack_kernel(flags, lref, xref, zd, zu, ta, tb, rd, ru, gref):
+def pack_kernel(flags, lhbm, xhbm, zd, zu, ta, tb, rd, ru, gref, lref, xref, sems):
+    copies = [
+        pltpu.make_async_copy(xhbm, xref, sems.at[0]),
+        pltpu.make_async_copy(lhbm, lref, sems.at[1]),
+    ]
+    for c in copies:
+        c.start()
     sites = Sites()
+    for c in copies:
+        c.wait()
     for d in (Z, T, R):
         g = flat_half(apply_dagger(link(lref, d), half(xref, d, 1)))
         put(gref, 24 * d, g)
@@ -238,7 +246,7 @@
 
 class Halo:
     def __init__(self, flags, zd, zu, ta, tb, rd, ru):
-        self.even = flags[2] == 1
+        self.even = None if flags is None else flags[2] == 1
         self.refs = {Z: (zd, zu), T: (ta, tb), R: (rd, ru)}
 
     def low(self, d, i):
@@ -260,32 +268,6 @@
         for i in range(len(own) // 2):
             out += sites.behind(own[2 * i], own[2 * i + 1], self.high(d, at + i), d)
         return out
-
-
-def local_kernel(lref, xref, yref, wref, gyref, m2ref):
-    sites = Sites()
-    u = link(lref, Y)
-    h = {k: tuple(sites.y_ahead(v) for v in c) for k, c in half(xref, Y, -1).items()}
-    w = apply(u, h)
-    g = {k: tuple(sites.y_behind(v) for v in c) for k, c in apply_dagger(u, half(xref, Y, 1)).items()}
-    put(wref, 0, flat_half(w))
-    put(gyref, 0, flat_half(g))
-    for n in range(2):
-        for s in range(2):
-            for c in range(3):
-                x = spinor(xref, n, s, c)
-                store_spinor(yref, n, s, c, [x[i] - HOPPING * (w[n, s, c][i] + g[n, s, c][i]) for i in range(2)])
-        for r in range(2):
-            col, phase = BLOCKS[Y][r]
-            for c in range(3):
-                x = spinor(xref, n, 2 + col, c)
-                diff = [g[n, r, c][i] - w[n, r, c][i] for i in range(2)]
-                term = add_phase((0.0, 0.0), complex(phase).conjugate(), diff)
-                store_spinor(yref, n, 2 + col, c, [x[i] - HOPPING * term[i] for i in range(2)])
-    for mu in range(3):
-        m = [[tuple(sites.y_ahead(v) for v in e) for e in row] for row in link(lref, mu)]
-        m2 = matmul(u, m)
-        put(m2ref, 18 * mu, [m2[a][b][c] for a in range(3) for b in range(3) for c in range(2)])
 
 
 def store_spinor(ref, n, s, c, value):
@@ -322,78 +304,134 @@
     ]
 
 
+def adjoint(m):
+    return [[conj(m[b][a]) for b in range(3)] for a in range(3)]
+
+
+def su3(left, right):
+    return third_row([[csum([cmul(left[a][k], right[k][b]) for k in range(3)]) for b in range(3)] for a in range(2)])
+
+
+def y_ahead(sites, m):
+    return [[tuple(sites.y_ahead(v) for v in e) for e in row] for row in m]
+
+
+def lower_y(sites, u_y, b_d, b_y):
+    return antihermitian(matmul(u_y, su3(adjoint(y_ahead(sites, b_d)), su3(adjoint(b_y), b_d))), PLAQUETTE)
+
+
+def scaled(m):
+    return [[(PLAQUETTE * e[0], PLAQUETTE * e[1]) for e in row] for row in m]
+
+
+def plane(sites, base, mu, nu, m1, m2, u_y):
+    def add(at, part):
+        base[at] = [a + b for a, b in zip(base[at], part)]
+
+    p = antihermitian(matmul_dagger(m1, m2), PLAQUETTE)
+    add(mu, p)
+    add(nu, [-v for v in p])
+    if nu == Y:
+        add(mu, [-sites.y_behind(v) for v in transport(p, u_y)])
+
+
+def early_kernel(lref, xref, gref, rd, ru, oy, ow, og, ob, om2, of, oq, obase):
+    sites = Sites()
+    halo = Halo(None, None, None, None, None, rd, ru)
+    u = link(lref, Y)
+    put(oy, 0, [xref[i] for i in range(48)])
+    h = {k: tuple(sites.y_ahead(v) for v in c) for k, c in half(xref, Y, -1).items()}
+    w = apply(u, h)
+    g = {k: tuple(sites.y_behind(v) for v in c) for k, c in apply_dagger(u, half(xref, Y, 1)).items()}
+    put(ow, 24, flat_half(w))
+    put(og, 24, flat_half(g))
+    add_hops(oy, Y, w, g)
+    for mu in (T, Z):
+        put_mat(om2, 18 * mu, su3(u, y_ahead(sites, link(lref, mu))))
+    h = unflat_half(halo.ahead(sites, R, flat_half(half(xref, R, -1)), LOW_LINKS))
+    g = unflat_half(halo.behind(sites, R, get(gref, 24 * R, 24), HIGH_LINKS))
+    w = apply(link(lref, R), h)
+    put(ow, 0, flat_half(w))
+    put(og, 0, flat_half(g))
+    add_hops(oy, R, w, g)
+    flat = halo.ahead(sites, R, row_values(lref, others(R)), 0)
+    f = [third_row(rows_of(flat[12 * k : 12 * k + 12])) for k in range(3)]
+    put_mat(of, 0, f[0])
+    put_mat(of, 18, f[1])
+    base = [[0.0] * 8 for _ in range(4)]
+    plane(sites, base, R, Y, su3(link(lref, R), f[2]), su3(u, y_ahead(sites, link(lref, R))), u)
+    flat = halo.behind(sites, R, row_values(lref, range(4)), 0)
+    put(ob, 0, flat[12 * R : 12 * R + 12])
+    b = [third_row(rows_of(flat[12 * nu : 12 * nu + 12])) for nu in range(4)]
+    for k in (T, Z):
+        put_mat(oq, 18 * k, scaled(su3(adjoint(b[k]), b[R])))
+    low = lower_y(sites, u, b[R], b[Y])
+    put(obase, 0, base[R])
+    put(obase, 8, [p + q for p, q in zip(base[Y], low)])
+
+
 def partner_kernel(
-    flags, lref, xref, gref, ylref, zd, zu, ta, tb, rd, ru,
+    flags, lref, xref, gref, ylref, gxref, bxref, zd, zu, ta, tb,
     oz, ot, orow, oy, ow, on, ob,
 ):
     sites = Sites()
-    halo = Halo(flags, zd, zu, ta, tb, rd, ru)
+    halo = Halo(flags, zd, zu, ta, tb, None, None)
     put(oy, 0, get(ylref, 0, 48))
-    kept = []
-    for d in range(3):
+    kept = {R: unflat_half(get(gxref, 0, 24))}
+    rows = {R: get(bxref, 0, 12)}
+    for d in (T, Z):
         h = unflat_half(halo.ahead(sites, d, flat_half(half(xref, d, -1)), LOW_LINKS))
         g = unflat_half(halo.behind(sites, d, get(gref, 24 * d, 24), HIGH_LINKS))
         w = apply(link(lref, d), h)
         put(ow, 24 * d, flat_half(w))
         add_hops(oy, d, w, g)
-        kept.append(g)
-        put(ob, 12 * d, halo.behind(sites, d, row_values(lref, (d,)), 6 * d))
+        kept[d] = g
+        rows[d] = halo.behind(sites, d, row_values(lref, (d,)), 6 * d)
+        put(ob, 12 * d, rows[d])
     for mu in (Z, T, R):
         part = antihermitian(outer(half(oy, mu, 1), kept[mu]), HOPPING)
         put(on, 8 * mu, part)
-        moved = part + [v for d in range(3) if d != mu for v in get(ob, 12 * d, 12)]
+        moved = part + [v for d in range(3) if d != mu for v in rows[d]]
         ref = {Z: oz, T: ot, R: orow}[mu]
         put(ref, 0, [sites.pack_low(moved[2 * i], moved[2 * i + 1], mu) for i in range(AGAIN)])
 
 
-def adjoint(m):
-    return [[conj(m[b][a]) for b in range(3)] for a in range(3)]
-
-
 def gauge_kernel(
-    flags, lref, yref, wref, wyref, gyref, m2ref, zd, zu, ta, tb, rd, ru, obase, oq, fref, bref,
+    flags, lref, yref, wref, wxyref, gxyref, m2ref, fxref, bxyref, zd, zu, ta, tb, obase, oq, fref, bref,
 ):
     sites = Sites()
-    halo = Halo(flags, zd, zu, ta, tb, rd, ru)
+    halo = Halo(flags, zd, zu, ta, tb, None, None)
     slot = {}
-    for d in range(3):
+    for d in (T, Z):
         flat = halo.ahead(sites, d, row_values(lref, others(d)), 0)
         for k, nu in enumerate(others(d)):
             slot[d, nu] = 18 * (3 * d + k)
             put_mat(fref, slot[d, nu], third_row(rows_of(flat[12 * k : 12 * k + 12])))
-    base = [[0.0] * 8 for _ in range(4)]
+    base = [[0.0] * 8, [0.0] * 8, get(bxyref, 0, 8), get(bxyref, 8, 8)]
 
     def add(mu, part):
         base[mu] = [a + b for a, b in zip(base[mu], part)]
 
-    for mu in range(4):
+    for mu in (T, Z):
         for nu in range(mu + 1, 4):
-            m1 = matmul(link(lref, mu), mat_at(fref, slot[mu, nu]))
-            m2 = mat_at(m2ref, 18 * mu) if nu == Y else matmul(link(lref, nu), mat_at(fref, slot[nu, mu]))
-            p = antihermitian(matmul_dagger(m1, m2), PLAQUETTE)
-            add(mu, p)
-            add(nu, [-v for v in p])
+            m1 = su3(link(lref, mu), mat_at(fref, slot[mu, nu]))
             if nu == Y:
-                add(mu, [-sites.y_behind(v) for v in transport(p, link(lref, Y))])
-    for d in range(3):
+                m2 = mat_at(m2ref, 18 * mu)
+            else:
+                m2 = su3(link(lref, nu), mat_at(fxref, 18 * mu) if nu == R else mat_at(fref, slot[nu, mu]))
+            plane(sites, base, mu, nu, m1, m2, link(lref, Y))
+    for d in (T, Z):
         flat = halo.behind(sites, d, row_values(lref, range(4)), 0)
         for nu in range(4):
             put_mat(bref, 18 * nu, third_row(rows_of(flat[12 * nu : 12 * nu + 12])))
         b_d = mat_at(bref, 18 * d)
-        slot_q = 0
-        for mu in others(d):
-            q = matmul(adjoint(mat_at(bref, 18 * mu)), b_d)
-            if mu == Y:
-                c = [[tuple(sites.y_ahead(v) for v in e) for e in row] for row in b_d]
-                v = matmul(adjoint(c), q)
-                add(Y, antihermitian(matmul(link(lref, Y), v), PLAQUETTE))
-            else:
-                put_mat(oq, 18 * (2 * d + slot_q), [[(PLAQUETTE * e[0], PLAQUETTE * e[1]) for e in row] for row in q])
-                slot_q += 1
+        for k, mu in enumerate([e for e in range(3) if e != d]):
+            put_mat(oq, 18 * (2 * d + k), scaled(su3(adjoint(mat_at(bref, 18 * mu)), b_d)))
+        add(Y, lower_y(sites, link(lref, Y), b_d, mat_at(bref, 18 * Y)))
     for mu in range(4):
-        w = unflat_half(get(wref, 24 * mu, 24) if mu != Y else get(wyref, 0, 24))
+        w = unflat_half(get(wref, 24 * mu, 24) if mu < R else get(wxyref, 24 * (mu - R), 24))
         add(mu, antihermitian(outer(w, half(yref, mu, -1)), HOPPING))
-    part = antihermitian(outer(half(yref, Y, 1), unflat_half(get(gyref, 0, 24))), HOPPING)
+    part = antihermitian(outer(half(yref, Y, 1), unflat_half(get(gxyref, 24, 24))), HOPPING)
     add(Y, transport([sites.y_ahead(v) for v in part], adjoint(link(lref, Y))))
     for mu in range(4):
         put(obase, 8 * mu, base[mu])
@@ -414,7 +452,7 @@
     ]
 
 
-def last_kernel(lref, baseref, nref, bref, qref, zd, td, rd, oref):
+def last_kernel(lref, baseref, nref, bref, bxref, qref, qxref, zd, td, rd, oref):
     sites = Sites()
     zero = jnp.zeros((4, 128), jnp.float32)
     for mu in range(4):
@@ -422,7 +460,7 @@
         if mu != Y:
             m = {Z: zd, T: td, R: rd}[mu]
             others_of = [d for d in range(3) if d != mu]
-            own = get(nref, 8 * mu, 8) + [v for d in others_of for v in get(bref, 12 * d, 12)]
+            own = get(nref, 8 * mu, 8) + [v for d in others_of for v in (get(bxref, 0, 12) if d == R else get(bref, 12 * d, 12))]
             ahead = []
             for i in range(AGAIN):
                 ahead += sites.ahead(own[2 * i], own[2 * i + 1], m[i], mu)
@@ -430,8 +468,8 @@
             total = times_dagger(ahead[:8], u)
             for k, d in enumerate(others_of):
                 c = third_row(rows_of(ahead[8 + 12 * k : 20 + 12 * k]))
-                slot_q = [e for e in others(d)].index(mu)
-                v = matmul(adjoint(c), mat_at(qref, 18 * (2 * d + slot_q)))
+                q = mat_at(qxref, 18 * mu) if d == R else mat_at(qref, 18 * (2 * d + [e for e in range(3) if e != d].index(mu)))
+                v = matmul(adjoint(c), q)
                 total = [[csum([total[a][b], v[a][b]]) for b in range(3)] for a in range(3)]
             x = [p + q for p, q in zip(x, antihermitian(matmul(u, total), 1.0))]
         at = mu * 18
@@ -447,16 +485,20 @@
         oref[at + 17] = -(x[6] + x[7])
 
 
-def call(body, operands, outs, flops, scratch=()):
+def call(body, operands, outs, flops, scratch=(), hbm=(), sems=0):
     specs = [
-        pl.BlockSpec(memory_space=pltpu.SMEM if o.dtype == jnp.int32 else pltpu.VMEM) for o in operands
+        pl.BlockSpec(
+            memory_space=pltpu.SMEM if o.dtype == jnp.int32 else pltpu.HBM if i in hbm else pltpu.VMEM
+        )
+        for i, o in enumerate(operands)
     ]
+    scratch = [pltpu.VMEM((n, 4, 128), jnp.float32) for n in scratch]
     return pl.pallas_call(
         body,
         in_specs=specs,
         out_specs=[pl.BlockSpec(memory_space=pltpu.VMEM) for _ in outs],
         out_shape=[jax.ShapeDtypeStruct((n, 4, 128), jnp.float32) for n in outs],
-        scratch_shapes=[pltpu.VMEM((n, 4, 128), jnp.float32) for n in scratch],
+        scratch_shapes=scratch + ([pltpu.SemaphoreType.DMA((sems,))] if sems else []),
         cost_estimate=pl.CostEstimate(flops=flops, bytes_accessed=4 * 512 * 200, transcendentals=0),
         compiler_params=pltpu.CompilerParams(vmem_limit_bytes=8 * 1024 * 1024),
         interpret=INTERPRET,
@@ -483,23 +525,32 @@
     xs = solutions.reshape(48, 4, 128)
     t = lax.axis_index("ta")
     flags = jnp.stack([t, lax.axis_size("ta") - 1 - t, 1 - t % 2]).astype(jnp.int32)
-    zd, zu, ta, tb, rd, ru, g = call(pack_kernel, (flags, lk, xs), (LOW, HIGH, HIGH, HIGH, LOW, HIGH, 72), 4_000_000)
+    zd, zu, ta, tb, rd, ru, g, lk, xs = call(
+        pack_kernel,
+        (flags, pltpu.with_memory_space_constraint(lk, pltpu.HBM), pltpu.with_memory_space_constraint(xs, pltpu.HBM)),
+        (LOW, HIGH, HIGH, HIGH, LOW, HIGH, 72, 72, 48),
+        4_000_000,
+        hbm=(1, 2),
+        sems=2,
+    )
     zu = move(zu, "gz", 1)
     zd = move(zd, "gz", -1)
     tb = meet(tb, "ta", False)
     ta = meet(ta, "ta", True)
     rd = move(rd, "xy", -1)
     ru = move(ru, "xy", 1)
-    got = (zd, zu, ta, tb, rd, ru)
-    yl, wy, gy, m2 = call(local_kernel, (lk, xs), (48, 24, 24, 54), 20_000_000)
+    got = (zd, zu, ta, tb)
+    yl, wxy, gxy, bx, m2, fx, qx, bxy = call(
+        early_kernel, (lk, xs, g, rd, ru), (48, 48, 48, 12, 36, 36, 36, 16), 20_000_000
+    )
     oz, ot, orow, y, w, n, b = call(
-        partner_kernel, (flags, lk, xs, g, yl, *got), (AGAIN, AGAIN, AGAIN, 48, 72, 24, 36), 20_000_000
+        partner_kernel, (flags, lk, xs, g, yl, gxy, bx, *got), (AGAIN, AGAIN, AGAIN, 48, 48, 24, 24), 20_000_000
     )
     oz = move(oz, "gz", -1)
     ot = move(ot, "ta", -1)
     orow = move(orow, "xy", -1)
-    base, q = call(gauge_kernel, (flags, lk, y, w, wy, gy, m2, *got), (32, 108), 20_000_000, (162, 72))
-    (force,) = call(last_kernel, (lk, base, n, b, q, oz, ot, orow), (72,), 4_000_000)
+    base, q = call(gauge_kernel, (flags, lk, y, w, wxy, gxy, m2, fx, bxy, *got), (32, 72), 20_000_000, (108, 72))
+    (force,) = call(last_kernel, (lk, base, n, b, bx, q, qx, oz, ot, orow), (72,), 4_000_000)
     return force.reshape(shape)
 
 

time: 75 us -> 72.8 us (0.971)
  starting transfers between devices: 62.4 us -> 49.2 us
  waiting for transfers between devices: 4.73 us -> 16.8 us
  local copies, waits for them, and re-layouts: 1.81 us -> 0 us
  Pallas kernels: 5.62 us -> 6.38 us
    ppermute x7, starting transfers between devices: 52.1 us -> 31.7 us  [move(): return lax.ppermute(x, axis, [(i, (i + by) % size) for i in range(size)])]
    ppermute x7, waiting for transfers between devices: 4.43 us -> 16.8 us  [move(): return lax.ppermute(x, axis, [(i, (i + by) % size) for i in range(size)])]
    ppermute x2, starting transfers between devices: 10.3 us -> 17.5 us  [meet(): return lax.ppermute(x, axis, pairs)]
    unnamed x8 -> x0, local copies, waits for them, and re-layouts: 1.81 us -> none
    pallas_call x5, Pallas kernels: 5.62 us -> 6.38 us  [call(): pl.pallas_call(body, in_specs=specs, out_specs=[pl.BlockSpec(memory_space...]
where the time goes in v4:
time: 72.8 us; the launch traced here: 72.6 us
  starting transfers between devices  49.2 us (68%)
  waiting for transfers between devices  16.8 us (23%)
  Pallas kernels  6.38 us (9%)
    ppermute x7, starting transfers between devices, move(): return lax.ppermute(x, axis, [(i, (i + by) % size) for i in range(size)])  31.7 us
    ppermute x2, starting transfers between devices, meet(): return lax.ppermute(x, axis, pairs)  17.5 us
    ppermute x7, waiting for transfers between devices, move(): return lax.ppermute(x, axis, [(i, (i + by) % size) for i in range(size)])  16.8 us
    pallas_call x5, Pallas kernels, call(): pl.pallas_call(body, in_specs=specs, out_specs=[pl.BlockSpec(memory_space...  6.38 us
  transfers between devices with their start and end apart: 9, of which 3 were waited for; matrix products, arithmetic and copies ran while one was open for 0% of the time, Pallas kernels for 3%

profile of v4, /device:TPU:1, one launch (start us, length us, event | category | flops | bytes accessed | tf_op | source)
XLA Modules:
  0.0 72.6 jit_solution(3319464545332671969)
XLA Ops:
  0.0 0.1 pad_add_fusion.flags
  0.1 1.8 %shard_map.28 = (f32[30,4,128]{2,1,0:T(4,128)S(1)}, f32[36,4,128]{2,1,0:T(4,128)S(1)}, f32[36,4,128]{2,1,0:T(4,128)S(1)}, f32[36,4,128]{2,1,0:T(4,128)S(1)}, f32...) custom-call(s32[3]{0:T(128)S(1)} %pad_add_fusion.flags, ...), custom_call_target="tpu_custom_call" | custom-call | flops 4000000 | bytes 409600 | tf_op jit(solution)/shard_map/pallas_call | solution.py:496
  1.9 14.1 %collective-permute-start = (f32[30,4,128]{2,1,0:T(4,128)S(1)}, f32[30,4,128]{2,1,0:T(4,128)S(1)}, u32[]{:S(2)}, u32[]{:S(2)}) collective-permute-start(f32[30,4,128]{2,1,0:T(4,128)S(1)} %get-tuple-element.34), channel_id=1, source_target_pairs={{0,7},{1,0},{2,1},{3,2},{4,3},{5,4},{6,5},{7,6},{8,15},{9,8},{10,9... | collective-permute-start | bytes 184328 | tf_op jit(solution)/shard_map/ppermute | solution.py:510
  16.0 0.0 collective-permute-start.1
  16.0 4.0 %collective-permute-start.3 = (f32[36,4,128]{2,1,0:T(4,128)S(1)}, f32[36,4,128]{2,1,0:T(4,128)S(1)}, u32[]{:S(2)}, u32[]{:S(2)}) collective-permute-start(f32[36,4,128]{2,1,0:T(4,128)S(1)} %get-tuple-element.40), channel_id=1, source_target_pairs={{0,8},{8,16},{16,24},{24,0},{1,9},{9,17},{17,25},{25,1},{2,10},{10... | collective-permute-start | bytes 221192 | tf_op jit(solution)/shard_map/ppermute | solution.py:510
  20.1 3.1 %collective-permute-start.4 = (f32[36,4,128]{2,1,0:T(4,128)S(1)}, f32[36,4,128]{2,1,0:T(4,128)S(1)}, u32[]{:S(2)}, u32[]{:S(2)}) collective-permute-start(f32[36,4,128]{2,1,0:T(4,128)S(1)} %get-tuple-element.41), channel_id=1, source_target_pairs={{0,32},{32,0},{64,96},{96,64},{128,160},{160,128},{192,224},{224,1... | collective-permute-start | bytes 221192 | tf_op jit(solution)/shard_map/ppermute | solution.py:519
  23.2 14.4 %collective-permute-start.5 = (f32[36,4,128]{2,1,0:T(4,128)S(1)}, f32[36,4,128]{2,1,0:T(4,128)S(1)}, u32[]{:S(2)}, u32[]{:S(2)}) collective-permute-start(f32[36,4,128]{2,1,0:T(4,128)S(1)} %get-tuple-element.42), channel_id=1, source_target_pairs={{32,64},{64,32},{96,128},{128,96},{160,192},{192,160},{224,256},{2... | collective-permute-start | bytes 221192 | tf_op jit(solution)/shard_map/ppermute | solution.py:519
  37.6 0.0 collective-permute-done.rd
  37.6 1.9 %collective-permute-start.2 = (f32[30,4,128]{2,1,0:T(4,128)S(1)}, f32[30,4,128]{2,1,0:T(4,128)S(1)}, u32[]{:S(2)}, u32[]{:S(2)}) collective-permute-start(f32[30,4,128]{2,1,0:T(4,128)S(1)} %get-tuple-element.39), channel_id=1, source_target_pairs={{0,24},{8,0},{16,8},{24,16},{1,25},{9,1},{17,9},{25,17},{2,26},{10... | collective-permute-start | bytes 184328 | tf_op jit(solution)/shard_map/ppermute | solution.py:510
  39.5 0.0 collective-permute-done.1.ru
  39.5 0.7 shard_map.29
  40.3 15.4 %collective-permute-done.2.zd = f32[30,4,128]{2,1,0:T(4,128)S(1)} collective-permute-done((f32[30,4,128]{2,1,0:T(4,128)S(1)}, f32[30,4,128]{2,1,0:T(4,128)S(1)}, u32[]{:S(2)}, u32[]{:S(2)}) %collective-permute-start.2) | collective-permute-done | bytes 61472 | tf_op jit(solution)/shard_map/ppermute | solution.py:510
  55.6 0.0 collective-permute-done.3.zu
  55.6 0.0 collective-permute-done.4.ta
  55.6 0.0 collective-permute-done.5.tb
  55.7 0.9 %shard_map.30 = (f32[16,4,128]{2,1,0:T(4,128)S(1)}, f32[16,4,128]{2,1,0:T(4,128)S(1)}, f32[16,4,128]{2,1,0:T(4,128)S(1)}, f32[48,4,128]{2,1,0:T(4,128)S(1)}, f32...) custom-call(s32[3]{0:T(128)S(1)} %pad_add_fusion.flags, ...), custom_call_target="tpu_custom_call" | custom-call | flops 20000000 | bytes 409600 | tf_op jit(solution)/shard_map/pallas_call | solution.py:496
  56.6 5.2 %collective-permute-start.6 = (f32[16,4,128]{2,1,0:T(4,128)S(1)}, f32[16,4,128]{2,1,0:T(4,128)S(1)}, u32[]{:S(2)}, u32[]{:S(2)}) collective-permute-start(f32[16,4,128]{2,1,0:T(4,128)S(1)} %get-tuple-element.54), channel_id=1, source_target_pairs={{0,24},{8,0},{16,8},{24,16},{1,25},{9,1},{17,9},{25,17},{2,26},{10... | collective-permute-start | bytes 98312 | tf_op jit(solution)/shard_map/ppermute | solution.py:510
  61.8 5.2 %collective-permute-start.7 = (f32[16,4,128]{2,1,0:T(4,128)S(1)}, f32[16,4,128]{2,1,0:T(4,128)S(1)}, u32[]{:S(2)}, u32[]{:S(2)}) collective-permute-start(f32[16,4,128]{2,1,0:T(4,128)S(1)} %get-tuple-element.55), channel_id=1, source_target_pairs={{0,992},{32,0},{64,32},{96,64},{128,96},{160,128},{192,160},{224,1... | collective-permute-start | bytes 98312 | tf_op jit(solution)/shard_map/ppermute | solution.py:510
  67.0 1.3 %collective-permute-start.8 = (f32[16,4,128]{2,1,0:T(4,128)S(1)}, f32[16,4,128]{2,1,0:T(4,128)S(1)}, u32[]{:S(2)}, u32[]{:S(2)}) collective-permute-start(f32[16,4,128]{2,1,0:T(4,128)S(1)} %get-tuple-element.56), channel_id=1, source_target_pairs={{0,7},{1,0},{2,1},{3,2},{4,3},{5,4},{6,5},{7,6},{8,15},{9,8},{10,9... | collective-permute-start | bytes 98312 | tf_op jit(solution)/shard_map/ppermute | solution.py:510
  68.3 1.8 %shard_map.31 = (f32[32,4,128]{2,1,0:T(4,128)S(1)}, f32[72,4,128]{2,1,0:T(4,128)S(1)}) custom-call(s32[3]{0:T(128)S(1)} %pad_add_fusion.flags, f32[72,4,128]{2,1,0:T(4,128)S(1)} %get-tuple-element.31.lref, f32[48,4,128]{2,1,0:T(4,128)S(1)} %get-tuple-element.43.yref, f32[48,4,128]{2,1,0:T(4,128)S(1)} %get-tuple-element.44.wref, ...), custom_call_target="tpu_custom_call" | custom-call | flops 20000000 | bytes 409600 | tf_op jit(solution)/shard_map/pallas_call | solution.py:496
  70.0 0.4 collective-permute-done.6.zd
  70.5 0.0 collective-permute-done.7.td
  70.5 0.9 %collective-permute-done.8.rd = f32[16,4,128]{2,1,0:T(4,128)S(1)} collective-permute-done((f32[16,4,128]{2,1,0:T(4,128)S(1)}, f32[16,4,128]{2,1,0:T(4,128)S(1)}, u32[]{:S(2)}, u32[]{:S(2)}) %collective-permute-start.8) | collective-permute-done | bytes 32800 | tf_op jit(solution)/shard_map/ppermute | solution.py:510
  71.4 1.2 %shard_map.32 = f32[72,4,128]{2,1,0:T(4,128)} custom-call(f32[72,4,128]{2,1,0:T(4,128)S(1)} %get-tuple-element.31.lref, f32[32,4,128]{2,1,0:T(4,128)S(1)} %get-tuple-element.49.baseref, f32[24,4,128]{2,1,0:T(4,128)S(1)} %get-tuple-element.50.nref, f32[24,4,128]{2,1,0:T(4,128)S(1)} %get-tuple-element.51.bref, f32[12,4,128]{2,1,0:T(4,128)S(1)} %get-tuple-element.38.bxref, ...), custom_call_target="tpu_custom_call" | custom-call | flops 4000000 | bytes 409600 | tf_op jit(solution)/shard_map/pallas_call | solution.py:496
Async XLA Ops:
  1.9 35.7 %collective-permute-start = (f32[30,4,128]{2,1,0:T(4,128)S(1)}, f32[30,4,128]{2,1,0:T(4,128)S(1)}, u32[]{:S(2)}, u32[]{:S(2)}) collective-permute-start(f32[30,4,128]{2,1,0:T(4,128)S(1)} %get-tuple-element.34), channel_id=1, source_target_pairs={{0,7},{1,0},{2,1},{3,2},{4,3},{5,4},{6,5},{7,6},{8,15},{9,8},{10,9... | collective-permute-start | bytes 184328 | tf_op jit(solution)/shard_map/ppermute | solution.py:510
  16.0 23.5 %collective-permute-start.1 = (f32[36,4,128]{2,1,0:T(4,128)S(1)}, f32[36,4,128]{2,1,0:T(4,128)S(1)}, u32[]{:S(2)}, u32[]{:S(2)}) collective-permute-start(f32[36,4,128]{2,1,0:T(4,128)S(1)} %get-tuple-element.35), channel_id=1, source_target_pairs={{0,1},{1,2},{2,3},{3,4},{4,5},{5,6},{6,7},{7,0},{8,9},{9,10},{10,1... | collective-permute-start | bytes 221192 | tf_op jit(solution)/shard_map/ppermute | solution.py:510
  16.0 39.6 %collective-permute-start.3 = (f32[36,4,128]{2,1,0:T(4,128)S(1)}, f32[36,4,128]{2,1,0:T(4,128)S(1)}, u32[]{:S(2)}, u32[]{:S(2)}) collective-permute-start(f32[36,4,128]{2,1,0:T(4,128)S(1)} %get-tuple-element.40), channel_id=1, source_target_pairs={{0,8},{8,16},{16,24},{24,0},{1,9},{9,17},{17,25},{25,1},{2,10},{10... | collective-permute-start | bytes 221192 | tf_op jit(solution)/shard_map/ppermute | solution.py:510
  20.1 35.6 %collective-permute-start.4 = (f32[36,4,128]{2,1,0:T(4,128)S(1)}, f32[36,4,128]{2,1,0:T(4,128)S(1)}, u32[]{:S(2)}, u32[]{:S(2)}) collective-permute-start(f32[36,4,128]{2,1,0:T(4,128)S(1)} %get-tuple-element.41), channel_id=1, source_target_pairs={{0,32},{32,0},{64,96},{96,64},{128,160},{160,128},{192,224},{224,1... | collective-permute-start | bytes 221192 | tf_op jit(solution)/shard_map/ppermute | solution.py:519
  23.2 32.5 %collective-permute-start.5 = (f32[36,4,128]{2,1,0:T(4,128)S(1)}, f32[36,4,128]{2,1,0:T(4,128)S(1)}, u32[]{:S(2)}, u32[]{:S(2)}) collective-permute-start(f32[36,4,128]{2,1,0:T(4,128)S(1)} %get-tuple-element.42), channel_id=1, source_target_pairs={{32,64},{64,32},{96,128},{128,96},{160,192},{192,160},{224,256},{2... | collective-permute-start | bytes 221192 | tf_op jit(solution)/shard_map/ppermute | solution.py:519
  37.6 18.0 %collective-permute-start.2 = (f32[30,4,128]{2,1,0:T(4,128)S(1)}, f32[30,4,128]{2,1,0:T(4,128)S(1)}, u32[]{:S(2)}, u32[]{:S(2)}) collective-permute-start(f32[30,4,128]{2,1,0:T(4,128)S(1)} %get-tuple-element.39), channel_id=1, source_target_pairs={{0,24},{8,0},{16,8},{24,16},{1,25},{9,1},{17,9},{25,17},{2,26},{10... | collective-permute-start | bytes 184328 | tf_op jit(solution)/shard_map/ppermute | solution.py:510
  56.6 13.9 %collective-permute-start.6 = (f32[16,4,128]{2,1,0:T(4,128)S(1)}, f32[16,4,128]{2,1,0:T(4,128)S(1)}, u32[]{:S(2)}, u32[]{:S(2)}) collective-permute-start(f32[16,4,128]{2,1,0:T(4,128)S(1)} %get-tuple-element.54), channel_id=1, source_target_pairs={{0,24},{8,0},{16,8},{24,16},{1,25},{9,1},{17,9},{25,17},{2,26},{10... | collective-permute-start | bytes 98312 | tf_op jit(solution)/shard_map/ppermute | solution.py:510
  61.8 8.7 %collective-permute-start.7 = (f32[16,4,128]{2,1,0:T(4,128)S(1)}, f32[16,4,128]{2,1,0:T(4,128)S(1)}, u32[]{:S(2)}, u32[]{:S(2)}) collective-permute-start(f32[16,4,128]{2,1,0:T(4,128)S(1)} %get-tuple-element.55), channel_id=1, source_target_pairs={{0,992},{32,0},{64,32},{96,64},{128,96},{160,128},{192,160},{224,1... | collective-permute-start | bytes 98312 | tf_op jit(solution)/shard_map/ppermute | solution.py:510
  67.0 4.4 %collective-permute-start.8 = (f32[16,4,128]{2,1,0:T(4,128)S(1)}, f32[16,4,128]{2,1,0:T(4,128)S(1)}, u32[]{:S(2)}, u32[]{:S(2)}) collective-permute-start(f32[16,4,128]{2,1,0:T(4,128)S(1)} %get-tuple-element.56), channel_id=1, source_target_pairs={{0,7},{1,0},{2,1},{3,2},{4,3},{5,4},{6,5},{7,6},{8,15},{9,8},{10,9... | collective-permute-start | bytes 98312 | tf_op jit(solution)/shard_map/ppermute | solution.py:510

commit v5 on v4

--- a/solution.py
+++ b/solution.py
@@ -370,24 +370,46 @@
     put(obase, 8, [p + q for p, q in zip(base[Y], low)])
 
 
-def partner_kernel(
-    flags, lref, xref, gref, ylref, gxref, bxref, zd, zu, ta, tb,
-    oz, ot, orow, oy, ow, on, ob,
-):
+def depth_kernel(lref, xref, gref, yref, m2ref, fxref, bxyref, zd, zu, oy, ow, og, ob, of, oq, obase):
     sites = Sites()
-    halo = Halo(flags, zd, zu, ta, tb, None, None)
-    put(oy, 0, get(ylref, 0, 48))
-    kept = {R: unflat_half(get(gxref, 0, 24))}
-    rows = {R: get(bxref, 0, 12)}
-    for d in (T, Z):
-        h = unflat_half(halo.ahead(sites, d, flat_half(half(xref, d, -1)), LOW_LINKS))
-        g = unflat_half(halo.behind(sites, d, get(gref, 24 * d, 24), HIGH_LINKS))
-        w = apply(link(lref, d), h)
-        put(ow, 24 * d, flat_half(w))
-        add_hops(oy, d, w, g)
-        kept[d] = g
-        rows[d] = halo.behind(sites, d, row_values(lref, (d,)), 6 * d)
-        put(ob, 12 * d, rows[d])
+    halo = Halo(None, zd, zu, None, None, None, None)
+    u = link(lref, Y)
+    put(oy, 0, get(yref, 0, 48))
+    h = unflat_half(halo.ahead(sites, Z, flat_half(half(xref, Z, -1)), LOW_LINKS))
+    g = unflat_half(halo.behind(sites, Z, get(gref, 24 * Z, 24), HIGH_LINKS))
+    w = apply(link(lref, Z), h)
+    put(ow, 0, flat_half(w))
+    put(og, 0, flat_half(g))
+    add_hops(oy, Z, w, g)
+    flat = halo.ahead(sites, Z, row_values(lref, others(Z)), 0)
+    f = [third_row(rows_of(flat[12 * k : 12 * k + 12])) for k in range(3)]
+    put_mat(of, 0, f[0])
+    base = [[0.0] * 8, [0.0] * 8, get(bxyref, 0, 8), get(bxyref, 8, 8)]
+    plane(sites, base, Z, R, su3(link(lref, Z), f[1]), su3(link(lref, R), mat_at(fxref, 18)), u)
+    plane(sites, base, Z, Y, su3(link(lref, Z), f[2]), mat_at(m2ref, 18), u)
+    flat = halo.behind(sites, Z, row_values(lref, range(4)), 0)
+    put(ob, 0, flat[12 * Z : 12 * Z + 12])
+    b = [third_row(rows_of(flat[12 * nu : 12 * nu + 12])) for nu in range(4)]
+    for k, mu in enumerate((T, R)):
+        put_mat(oq, 18 * k, scaled(su3(adjoint(b[mu]), b[Z])))
+    low = lower_y(sites, u, b[Z], b[Y])
+    put(obase, 0, base[Z])
+    put(obase, 8, base[R])
+    put(obase, 16, [p + q for p, q in zip(base[Y], low)])
+
+
+def partner_kernel(flags, lref, xref, gref, yinref, gxref, gzref, bxref, bzref, ta, tb, oz, ot, orow, oy, ow, on, ob):
+    sites = Sites()
+    halo = Halo(flags, None, None, ta, tb, None, None)
+    put(oy, 0, get(yinref, 0, 48))
+    h = unflat_half(halo.ahead(sites, T, flat_half(half(xref, T, -1)), LOW_LINKS))
+    g = unflat_half(halo.behind(sites, T, get(gref, 24 * T, 24), HIGH_LINKS))
+    w = apply(link(lref, T), h)
+    put(ow, 0, flat_half(w))
+    add_hops(oy, T, w, g)
+    kept = {T: g, Z: unflat_half(get(gzref, 0, 24)), R: unflat_half(get(gxref, 0, 24))}
+    rows = {T: halo.behind(sites, T, row_values(lref, (T,)), 6 * T), Z: get(bzref, 0, 12), R: get(bxref, 0, 12)}
+    put(ob, 0, rows[T])
     for mu in (Z, T, R):
         part = antihermitian(outer(half(oy, mu, 1), kept[mu]), HOPPING)
         put(on, 8 * mu, part)
@@ -396,43 +418,30 @@
         put(ref, 0, [sites.pack_low(moved[2 * i], moved[2 * i + 1], mu) for i in range(AGAIN)])
 
 
-def gauge_kernel(
-    flags, lref, yref, wref, wxyref, gxyref, m2ref, fxref, bxyref, zd, zu, ta, tb, obase, oq, fref, bref,
-):
+def gauge_kernel(flags, lref, yref, wref, wzref, wxyref, gxyref, m2ref, fxref, fzref, bzxyref, ta, tb, obase, oq):
     sites = Sites()
-    halo = Halo(flags, zd, zu, ta, tb, None, None)
-    slot = {}
-    for d in (T, Z):
-        flat = halo.ahead(sites, d, row_values(lref, others(d)), 0)
-        for k, nu in enumerate(others(d)):
-            slot[d, nu] = 18 * (3 * d + k)
-            put_mat(fref, slot[d, nu], third_row(rows_of(flat[12 * k : 12 * k + 12])))
-    base = [[0.0] * 8, [0.0] * 8, get(bxyref, 0, 8), get(bxyref, 8, 8)]
+    halo = Halo(flags, None, None, ta, tb, None, None)
+    u = link(lref, Y)
+    flat = halo.ahead(sites, T, row_values(lref, others(T)), 0)
+    f = [third_row(rows_of(flat[12 * k : 12 * k + 12])) for k in range(3)]
+    base = [[0.0] * 8] + [get(bzxyref, 8 * k, 8) for k in range(3)]
 
     def add(mu, part):
         base[mu] = [a + b for a, b in zip(base[mu], part)]
 
-    for mu in (T, Z):
-        for nu in range(mu + 1, 4):
-            m1 = su3(link(lref, mu), mat_at(fref, slot[mu, nu]))
-            if nu == Y:
-                m2 = mat_at(m2ref, 18 * mu)
-            else:
-                m2 = su3(link(lref, nu), mat_at(fxref, 18 * mu) if nu == R else mat_at(fref, slot[nu, mu]))
-            plane(sites, base, mu, nu, m1, m2, link(lref, Y))
-    for d in (T, Z):
-        flat = halo.behind(sites, d, row_values(lref, range(4)), 0)
-        for nu in range(4):
-            put_mat(bref, 18 * nu, third_row(rows_of(flat[12 * nu : 12 * nu + 12])))
-        b_d = mat_at(bref, 18 * d)
-        for k, mu in enumerate([e for e in range(3) if e != d]):
-            put_mat(oq, 18 * (2 * d + k), scaled(su3(adjoint(mat_at(bref, 18 * mu)), b_d)))
-        add(Y, lower_y(sites, link(lref, Y), b_d, mat_at(bref, 18 * Y)))
-    for mu in range(4):
-        w = unflat_half(get(wref, 24 * mu, 24) if mu < R else get(wxyref, 24 * (mu - R), 24))
-        add(mu, antihermitian(outer(w, half(yref, mu, -1)), HOPPING))
+    for nu in (Z, R, Y):
+        m1 = su3(link(lref, T), f[nu - 1])
+        m2 = mat_at(m2ref, 0) if nu == Y else su3(link(lref, nu), mat_at(fzref if nu == Z else fxref, 0))
+        plane(sites, base, T, nu, m1, m2, u)
+    flat = halo.behind(sites, T, row_values(lref, range(4)), 0)
+    b = [third_row(rows_of(flat[12 * nu : 12 * nu + 12])) for nu in range(4)]
+    for k, mu in enumerate((Z, R)):
+        put_mat(oq, 18 * k, scaled(su3(adjoint(b[mu]), b[T])))
+    add(Y, lower_y(sites, u, b[T], b[Y]))
+    for mu, (ref, at) in enumerate(((wref, 0), (wzref, 0), (wxyref, 0), (wxyref, 24))):
+        add(mu, antihermitian(outer(unflat_half(get(ref, at, 24)), half(yref, mu, -1)), HOPPING))
     part = antihermitian(outer(half(yref, Y, 1), unflat_half(get(gxyref, 24, 24))), HOPPING)
-    add(Y, transport([sites.y_ahead(v) for v in part], adjoint(link(lref, Y))))
+    add(Y, transport([sites.y_ahead(v) for v in part], adjoint(u)))
     for mu in range(4):
         put(obase, 8 * mu, base[mu])
 
@@ -452,7 +461,7 @@
     ]
 
 
-def last_kernel(lref, baseref, nref, bref, bxref, qref, qxref, zd, td, rd, oref):
+def last_kernel(lref, baseref, nref, btref, bzref, bxref, qtref, qzref, qxref, zd, td, rd, oref):
     sites = Sites()
     zero = jnp.zeros((4, 128), jnp.float32)
     for mu in range(4):
@@ -460,7 +469,7 @@
         if mu != Y:
             m = {Z: zd, T: td, R: rd}[mu]
             others_of = [d for d in range(3) if d != mu]
-            own = get(nref, 8 * mu, 8) + [v for d in others_of for v in (get(bxref, 0, 12) if d == R else get(bref, 12 * d, 12))]
+            own = get(nref, 8 * mu, 8) + [v for d in others_of for v in get((btref, bzref, bxref)[d], 0, 12)]
             ahead = []
             for i in range(AGAIN):
                 ahead += sites.ahead(own[2 * i], own[2 * i + 1], m[i], mu)
@@ -468,7 +477,7 @@
             total = times_dagger(ahead[:8], u)
             for k, d in enumerate(others_of):
                 c = third_row(rows_of(ahead[8 + 12 * k : 20 + 12 * k]))
-                q = mat_at(qxref, 18 * mu) if d == R else mat_at(qref, 18 * (2 * d + [e for e in range(3) if e != d].index(mu)))
+                q = mat_at((qtref, qzref, qxref)[d], 18 * [e for e in range(3) if e != d].index(mu))
                 v = matmul(adjoint(c), q)
                 total = [[csum([total[a][b], v[a][b]]) for b in range(3)] for a in range(3)]
             x = [p + q for p, q in zip(x, antihermitian(matmul(u, total), 1.0))]
@@ -539,18 +548,23 @@
     ta = meet(ta, "ta", True)
     rd = move(rd, "xy", -1)
     ru = move(ru, "xy", 1)
-    got = (zd, zu, ta, tb)
     yl, wxy, gxy, bx, m2, fx, qx, bxy = call(
         early_kernel, (lk, xs, g, rd, ru), (48, 48, 48, 12, 36, 36, 36, 16), 20_000_000
     )
-    oz, ot, orow, y, w, n, b = call(
-        partner_kernel, (flags, lk, xs, g, yl, gxy, bx, *got), (AGAIN, AGAIN, AGAIN, 48, 48, 24, 24), 20_000_000
+    yl, wz, gz, bz, fz, qz, bzxy = call(
+        depth_kernel, (lk, xs, g, yl, m2, fx, bxy, zd, zu), (48, 24, 24, 12, 18, 36, 24), 20_000_000
+    )
+    oz, ot, orow, y, w, n, bt = call(
+        partner_kernel,
+        (flags, lk, xs, g, yl, gxy, gz, bx, bz, ta, tb),
+        (AGAIN, AGAIN, AGAIN, 48, 24, 24, 12),
+        20_000_000,
     )
     oz = move(oz, "gz", -1)
     ot = move(ot, "ta", -1)
     orow = move(orow, "xy", -1)
-    base, q = call(gauge_kernel, (flags, lk, y, w, wxy, gxy, m2, fx, bxy, *got), (32, 72), 20_000_000, (108, 72))
-    (force,) = call(last_kernel, (lk, base, n, b, bx, q, qx, oz, ot, orow), (72,), 4_000_000)
+    base, qt = call(gauge_kernel, (flags, lk, y, w, wz, wxy, gxy, m2, fx, fz, bzxy, ta, tb), (32, 36), 20_000_000)
+    (force,) = call(last_kernel, (lk, base, n, bt, bz, bx, qt, qz, qx, oz, ot, orow), (72,), 4_000_000)
     return force.reshape(shape)
 
 

time: 72.8 us -> 73.2 us (level)
    pallas_call x5 -> x6, Pallas kernels: 6.38 us -> 6.33 us  [call(): pl.pallas_call(body, in_specs=specs, out_specs=[pl.BlockSpec(memory_space...]
where the time goes in v5:
time: 73.2 us; the launch traced here: 72.9 us
  starting transfers between devices  49.2 us (67%)
  waiting for transfers between devices  17.2 us (23%)
  Pallas kernels  6.33 us (9%)
    ppermute x7, starting transfers between devices, move(): return lax.ppermute(x, axis, [(i, (i + by) % size) for i in range(size)])  31.7 us
    ppermute x2, starting transfers between devices, meet(): return lax.ppermute(x, axis, pairs)  17.5 us
    ppermute x7, waiting for transfers between devices, move(): return lax.ppermute(x, axis, [(i, (i + by) % size) for i in range(size)])  17.2 us
    pallas_call x6, Pallas kernels, call(): pl.pallas_call(body, in_specs=specs, out_specs=[pl.BlockSpec(memory_space...  6.33 us
  transfers between devices with their start and end apart: 9, of which 3 were waited for; matrix products, arithmetic and copies ran while one was open for 0% of the time, Pallas kernels for 3%

profile of v5, /device:TPU:1, one launch (start us, length us, event | category | flops | bytes accessed | tf_op | source)
XLA Modules:
  0.0 72.9 jit_solution(15553594047785019524)
XLA Ops:
  0.0 0.1 pad_add_fusion.flags
  0.1 1.8 %shard_map.28 = (f32[30,4,128]{2,1,0:T(4,128)S(1)}, f32[36,4,128]{2,1,0:T(4,128)S(1)}, f32[36,4,128]{2,1,0:T(4,128)S(1)}, f32[36,4,128]{2,1,0:T(4,128)S(1)}, f32...) custom-call(s32[3]{0:T(128)S(1)} %pad_add_fusion.flags, ...), custom_call_target="tpu_custom_call" | custom-call | flops 4000000 | bytes 409600 | tf_op jit(solution)/shard_map/pallas_call | solution.py:505
  1.9 14.1 %collective-permute-start = (f32[30,4,128]{2,1,0:T(4,128)S(1)}, f32[30,4,128]{2,1,0:T(4,128)S(1)}, u32[]{:S(2)}, u32[]{:S(2)}) collective-permute-start(f32[30,4,128]{2,1,0:T(4,128)S(1)} %get-tuple-element.41), channel_id=1, source_target_pairs={{0,7},{1,0},{2,1},{3,2},{4,3},{5,4},{6,5},{7,6},{8,15},{9,8},{10,9... | collective-permute-start | bytes 184328 | tf_op jit(solution)/shard_map/ppermute | solution.py:519
  16.0 0.0 collective-permute-start.1
  16.0 4.0 %collective-permute-start.3 = (f32[36,4,128]{2,1,0:T(4,128)S(1)}, f32[36,4,128]{2,1,0:T(4,128)S(1)}, u32[]{:S(2)}, u32[]{:S(2)}) collective-permute-start(f32[36,4,128]{2,1,0:T(4,128)S(1)} %get-tuple-element.48), channel_id=1, source_target_pairs={{0,8},{8,16},{16,24},{24,0},{1,9},{9,17},{17,25},{25,1},{2,10},{10... | collective-permute-start | bytes 221192 | tf_op jit(solution)/shard_map/ppermute | solution.py:519
  20.1 3.1 %collective-permute-start.4 = (f32[36,4,128]{2,1,0:T(4,128)S(1)}, f32[36,4,128]{2,1,0:T(4,128)S(1)}, u32[]{:S(2)}, u32[]{:S(2)}) collective-permute-start(f32[36,4,128]{2,1,0:T(4,128)S(1)} %get-tuple-element.54), channel_id=1, source_target_pairs={{0,32},{32,0},{64,96},{96,64},{128,160},{160,128},{192,224},{224,1... | collective-permute-start | bytes 221192 | tf_op jit(solution)/shard_map/ppermute | solution.py:528
  23.2 14.4 %collective-permute-start.5 = (f32[36,4,128]{2,1,0:T(4,128)S(1)}, f32[36,4,128]{2,1,0:T(4,128)S(1)}, u32[]{:S(2)}, u32[]{:S(2)}) collective-permute-start(f32[36,4,128]{2,1,0:T(4,128)S(1)} %get-tuple-element.55), channel_id=1, source_target_pairs={{32,64},{64,32},{96,128},{128,96},{160,192},{192,160},{224,256},{2... | collective-permute-start | bytes 221192 | tf_op jit(solution)/shard_map/ppermute | solution.py:528
  37.6 0.0 collective-permute-done.rd
  37.6 1.9 %collective-permute-start.2 = (f32[30,4,128]{2,1,0:T(4,128)S(1)}, f32[30,4,128]{2,1,0:T(4,128)S(1)}, u32[]{:S(2)}, u32[]{:S(2)}) collective-permute-start(f32[30,4,128]{2,1,0:T(4,128)S(1)} %get-tuple-element.47), channel_id=1, source_target_pairs={{0,24},{8,0},{16,8},{24,16},{1,25},{9,1},{17,9},{25,17},{2,26},{10... | collective-permute-start | bytes 184328 | tf_op jit(solution)/shard_map/ppermute | solution.py:519
  39.5 0.0 collective-permute-done.1.ru
  39.6 0.7 shard_map.29
  40.3 15.4 %collective-permute-done.2.zd = f32[30,4,128]{2,1,0:T(4,128)S(1)} collective-permute-done((f32[30,4,128]{2,1,0:T(4,128)S(1)}, f32[30,4,128]{2,1,0:T(4,128)S(1)}, u32[]{:S(2)}, u32[]{:S(2)}) %collective-permute-start.2) | collective-permute-done | bytes 61472 | tf_op jit(solution)/shard_map/ppermute | solution.py:519
  55.6 0.0 collective-permute-done.3.zu
  55.6 0.5 shard_map.30
  56.2 0.0 collective-permute-done.4.ta
  56.2 0.0 collective-permute-done.5.tb
  56.2 0.8 %shard_map.31 = (f32[16,4,128]{2,1,0:T(4,128)S(1)}, f32[16,4,128]{2,1,0:T(4,128)S(1)}, f32[16,4,128]{2,1,0:T(4,128)S(1)}, f32[48,4,128]{2,1,0:T(4,128)S(1)}, f32...) custom-call(s32[3]{0:T(128)S(1)} %pad_add_fusion.flags, ...), custom_call_target="tpu_custom_call" | custom-call | flops 20000000 | bytes 409600 | tf_op jit(solution)/shard_map/pallas_call | solution.py:505
  57.0 5.2 %collective-permute-start.6 = (f32[16,4,128]{2,1,0:T(4,128)S(1)}, f32[16,4,128]{2,1,0:T(4,128)S(1)}, u32[]{:S(2)}, u32[]{:S(2)}) collective-permute-start(f32[16,4,128]{2,1,0:T(4,128)S(1)} %get-tuple-element.68), channel_id=1, source_target_pairs={{0,24},{8,0},{16,8},{24,16},{1,25},{9,1},{17,9},{25,17},{2,26},{10... | collective-permute-start | bytes 98312 | tf_op jit(solution)/shard_map/ppermute | solution.py:519
  62.2 5.2 %collective-permute-start.7 = (f32[16,4,128]{2,1,0:T(4,128)S(1)}, f32[16,4,128]{2,1,0:T(4,128)S(1)}, u32[]{:S(2)}, u32[]{:S(2)}) collective-permute-start(f32[16,4,128]{2,1,0:T(4,128)S(1)} %get-tuple-element.69), channel_id=1, source_target_pairs={{0,992},{32,0},{64,32},{96,64},{128,96},{160,128},{192,160},{224,1... | collective-permute-start | bytes 98312 | tf_op jit(solution)/shard_map/ppermute | solution.py:519
  67.4 1.3 %collective-permute-start.8 = (f32[16,4,128]{2,1,0:T(4,128)S(1)}, f32[16,4,128]{2,1,0:T(4,128)S(1)}, u32[]{:S(2)}, u32[]{:S(2)}) collective-permute-start(f32[16,4,128]{2,1,0:T(4,128)S(1)} %get-tuple-element.70), channel_id=1, source_target_pairs={{0,7},{1,0},{2,1},{3,2},{4,3},{5,4},{6,5},{7,6},{8,15},{9,8},{10,9... | collective-permute-start | bytes 98312 | tf_op jit(solution)/shard_map/ppermute | solution.py:519
  68.7 1.3 %shard_map.32 = (f32[32,4,128]{2,1,0:T(4,128)S(1)}, f32[36,4,128]{2,1,0:T(4,128)S(1)}) custom-call(s32[3]{0:T(128)S(1)} %pad_add_fusion.flags, f32[72,4,128]{2,1,0:T(4,128)S(1)} %get-tuple-element.38.lref, f32[48,4,128]{2,1,0:T(4,128)S(1)} %get-tuple-element.56.yref, f32[24,4,128]{2,1,0:T(4,128)S(1)} %get-tuple-element.57.wref, ...), custom_call_target="tpu_custom_call" | custom-call | flops 20000000 | bytes 409600 | tf_op jit(solution)/shard_map/pallas_call | solution.py:505
  70.0 0.9 %collective-permute-done.6.zd = f32[16,4,128]{2,1,0:T(4,128)S(1)} collective-permute-done((f32[16,4,128]{2,1,0:T(4,128)S(1)}, f32[16,4,128]{2,1,0:T(4,128)S(1)}, u32[]{:S(2)}, u32[]{:S(2)}) %collective-permute-start.6) | collective-permute-done | bytes 32800 | tf_op jit(solution)/shard_map/ppermute | solution.py:519
  70.9 0.9 %collective-permute-done.8.rd = f32[16,4,128]{2,1,0:T(4,128)S(1)} collective-permute-done((f32[16,4,128]{2,1,0:T(4,128)S(1)}, f32[16,4,128]{2,1,0:T(4,128)S(1)}, u32[]{:S(2)}, u32[]{:S(2)}) %collective-permute-start.8) | collective-permute-done | bytes 32800 | tf_op jit(solution)/shard_map/ppermute | solution.py:519
  71.8 1.2 %shard_map.33 = f32[72,4,128]{2,1,0:T(4,128)} custom-call(f32[72,4,128]{2,1,0:T(4,128)S(1)} %get-tuple-element.38.lref, f32[32,4,128]{2,1,0:T(4,128)S(1)} %get-tuple-element.62.baseref, f32[24,4,128]{2,1,0:T(4,128)S(1)} %get-tuple-element.63.nref, f32[12,4,128]{2,1,0:T(4,128)S(1)} %get-tuple-element.64.btref, f32[12,4,128]{2,1,0:T(4,128)S(1)} %get-tuple-element.53.bzref, ...), custom_call_target="tpu_custom_call" | custom-call | flops 4000000 | bytes 409600 | tf_op jit(solution)/shard_map/pallas_call | solution.py:505
  (1 shorter events, 0.0 us)
Async XLA Ops:
  1.9 35.7 %collective-permute-start = (f32[30,4,128]{2,1,0:T(4,128)S(1)}, f32[30,4,128]{2,1,0:T(4,128)S(1)}, u32[]{:S(2)}, u32[]{:S(2)}) collective-permute-start(f32[30,4,128]{2,1,0:T(4,128)S(1)} %get-tuple-element.41), channel_id=1, source_target_pairs={{0,7},{1,0},{2,1},{3,2},{4,3},{5,4},{6,5},{7,6},{8,15},{9,8},{10,9... | collective-permute-start | bytes 184328 | tf_op jit(solution)/shard_map/ppermute | solution.py:519
  16.0 23.5 %collective-permute-start.1 = (f32[36,4,128]{2,1,0:T(4,128)S(1)}, f32[36,4,128]{2,1,0:T(4,128)S(1)}, u32[]{:S(2)}, u32[]{:S(2)}) collective-permute-start(f32[36,4,128]{2,1,0:T(4,128)S(1)} %get-tuple-element.42), channel_id=1, source_target_pairs={{0,1},{1,2},{2,3},{3,4},{4,5},{5,6},{6,7},{7,0},{8,9},{9,10},{10,1... | collective-permute-start | bytes 221192 | tf_op jit(solution)/shard_map/ppermute | solution.py:519
  16.0 39.6 %collective-permute-start.3 = (f32[36,4,128]{2,1,0:T(4,128)S(1)}, f32[36,4,128]{2,1,0:T(4,128)S(1)}, u32[]{:S(2)}, u32[]{:S(2)}) collective-permute-start(f32[36,4,128]{2,1,0:T(4,128)S(1)} %get-tuple-element.48), channel_id=1, source_target_pairs={{0,8},{8,16},{16,24},{24,0},{1,9},{9,17},{17,25},{25,1},{2,10},{10... | collective-permute-start | bytes 221192 | tf_op jit(solution)/shard_map/ppermute | solution.py:519
  20.1 36.1 %collective-permute-start.4 = (f32[36,4,128]{2,1,0:T(4,128)S(1)}, f32[36,4,128]{2,1,0:T(4,128)S(1)}, u32[]{:S(2)}, u32[]{:S(2)}) collective-permute-start(f32[36,4,128]{2,1,0:T(4,128)S(1)} %get-tuple-element.54), channel_id=1, source_target_pairs={{0,32},{32,0},{64,96},{96,64},{128,160},{160,128},{192,224},{224,1... | collective-permute-start | bytes 221192 | tf_op jit(solution)/shard_map/ppermute | solution.py:528
  23.2 33.0 %collective-permute-start.5 = (f32[36,4,128]{2,1,0:T(4,128)S(1)}, f32[36,4,128]{2,1,0:T(4,128)S(1)}, u32[]{:S(2)}, u32[]{:S(2)}) collective-permute-start(f32[36,4,128]{2,1,0:T(4,128)S(1)} %get-tuple-element.55), channel_id=1, source_target_pairs={{32,64},{64,32},{96,128},{128,96},{160,192},{192,160},{224,256},{2... | collective-permute-start | bytes 221192 | tf_op jit(solution)/shard_map/ppermute | solution.py:528
  37.6 18.0 %collective-permute-start.2 = (f32[30,4,128]{2,1,0:T(4,128)S(1)}, f32[30,4,128]{2,1,0:T(4,128)S(1)}, u32[]{:S(2)}, u32[]{:S(2)}) collective-permute-start(f32[30,4,128]{2,1,0:T(4,128)S(1)} %get-tuple-element.47), channel_id=1, source_target_pairs={{0,24},{8,0},{16,8},{24,16},{1,25},{9,1},{17,9},{25,17},{2,26},{10... | collective-permute-start | bytes 184328 | tf_op jit(solution)/shard_map/ppermute | solution.py:519
  57.0 13.9 %collective-permute-start.6 = (f32[16,4,128]{2,1,0:T(4,128)S(1)}, f32[16,4,128]{2,1,0:T(4,128)S(1)}, u32[]{:S(2)}, u32[]{:S(2)}) collective-permute-start(f32[16,4,128]{2,1,0:T(4,128)S(1)} %get-tuple-element.68), channel_id=1, source_target_pairs={{0,24},{8,0},{16,8},{24,16},{1,25},{9,1},{17,9},{25,17},{2,26},{10... | collective-permute-start | bytes 98312 | tf_op jit(solution)/shard_map/ppermute | solution.py:519
  62.2 8.7 %collective-permute-start.7 = (f32[16,4,128]{2,1,0:T(4,128)S(1)}, f32[16,4,128]{2,1,0:T(4,128)S(1)}, u32[]{:S(2)}, u32[]{:S(2)}) collective-permute-start(f32[16,4,128]{2,1,0:T(4,128)S(1)} %get-tuple-element.69), channel_id=1, source_target_pairs={{0,992},{32,0},{64,32},{96,64},{128,96},{160,128},{192,160},{224,1... | collective-permute-start | bytes 98312 | tf_op jit(solution)/shard_map/ppermute | solution.py:519
  67.4 4.3 %collective-permute-start.8 = (f32[16,4,128]{2,1,0:T(4,128)S(1)}, f32[16,4,128]{2,1,0:T(4,128)S(1)}, u32[]{:S(2)}, u32[]{:S(2)}) collective-permute-start(f32[16,4,128]{2,1,0:T(4,128)S(1)} %get-tuple-element.70), channel_id=1, source_target_pairs={{0,7},{1,0},{2,1},{3,2},{4,3},{5,4},{6,5},{7,6},{8,15},{9,8},{10,9... | collective-permute-start | bytes 98312 | tf_op jit(solution)/shard_map/ppermute | solution.py:519

commit v6 on v5

--- a/solution.py
+++ b/solution.py
@@ -210,8 +210,9 @@
 
 
 LOW_LINKS, LOW = 18, 30
+LOW_LINKS_Z, LOW_Z = 12, 24
 HIGH_LINKS, HIGH = 24, 36
-AGAIN = 16
+AGAIN, AGAIN_Z = 16, 20
 
 
 def pack_kernel(flags, lhbm, xhbm, zd, zu, ta, tb, rd, ru, gref, lref, xref, sems):
@@ -227,9 +228,9 @@
     for d in (Z, T, R):
         g = flat_half(apply_dagger(link(lref, d), half(xref, d, 1)))
         put(gref, 24 * d, g)
-        low = row_values(lref, others(d)) + flat_half(half(xref, d, -1))
+        low = row_values(lref, (T, R) if d == Z else others(d)) + flat_half(half(xref, d, -1))
         high = row_values(lref, range(4)) + g
-        low = [sites.pack_low(low[2 * i], low[2 * i + 1], d) for i in range(LOW)]
+        low = [sites.pack_low(low[2 * i], low[2 * i + 1], d) for i in range(len(low) // 2)]
         high = [sites.pack_high(high[2 * i], high[2 * i + 1], d) for i in range(HIGH)]
         if d != T:
             put(zd if d == Z else rd, 0, low)
@@ -346,8 +347,7 @@
     put(ow, 24, flat_half(w))
     put(og, 24, flat_half(g))
     add_hops(oy, Y, w, g)
-    for mu in (T, Z):
-        put_mat(om2, 18 * mu, su3(u, y_ahead(sites, link(lref, mu))))
+    put_mat(om2, 0, su3(u, y_ahead(sites, link(lref, T))))
     h = unflat_half(halo.ahead(sites, R, flat_half(half(xref, R, -1)), LOW_LINKS))
     g = unflat_half(halo.behind(sites, R, get(gref, 24 * R, 24), HIGH_LINKS))
     w = apply(link(lref, R), h)
@@ -370,35 +370,37 @@
     put(obase, 8, [p + q for p, q in zip(base[Y], low)])
 
 
-def depth_kernel(lref, xref, gref, yref, m2ref, fxref, bxyref, zd, zu, oy, ow, og, ob, of, oq, obase):
+def depth_kernel(lref, xref, gref, yref, fxref, bxyref, zd, zu, oy, ow, og, ob, of, oq, obase, olow):
     sites = Sites()
     halo = Halo(None, zd, zu, None, None, None, None)
     u = link(lref, Y)
     put(oy, 0, get(yref, 0, 48))
-    h = unflat_half(halo.ahead(sites, Z, flat_half(half(xref, Z, -1)), LOW_LINKS))
+    h = unflat_half(halo.ahead(sites, Z, flat_half(half(xref, Z, -1)), LOW_LINKS_Z))
     g = unflat_half(halo.behind(sites, Z, get(gref, 24 * Z, 24), HIGH_LINKS))
     w = apply(link(lref, Z), h)
     put(ow, 0, flat_half(w))
     put(og, 0, flat_half(g))
     add_hops(oy, Z, w, g)
-    flat = halo.ahead(sites, Z, row_values(lref, others(Z)), 0)
-    f = [third_row(rows_of(flat[12 * k : 12 * k + 12])) for k in range(3)]
+    flat = halo.ahead(sites, Z, row_values(lref, (T, R)), 0)
+    f = [third_row(rows_of(flat[12 * k : 12 * k + 12])) for k in range(2)]
     put_mat(of, 0, f[0])
     base = [[0.0] * 8, [0.0] * 8, get(bxyref, 0, 8), get(bxyref, 8, 8)]
     plane(sites, base, Z, R, su3(link(lref, Z), f[1]), su3(link(lref, R), mat_at(fxref, 18)), u)
-    plane(sites, base, Z, Y, su3(link(lref, Z), f[2]), mat_at(m2ref, 18), u)
     flat = halo.behind(sites, Z, row_values(lref, range(4)), 0)
     put(ob, 0, flat[12 * Z : 12 * Z + 12])
     b = [third_row(rows_of(flat[12 * nu : 12 * nu + 12])) for nu in range(4)]
     for k, mu in enumerate((T, R)):
         put_mat(oq, 18 * k, scaled(su3(adjoint(b[mu]), b[Z])))
     low = lower_y(sites, u, b[Z], b[Y])
+    put(olow, 0, low)
     put(obase, 0, base[Z])
     put(obase, 8, base[R])
     put(obase, 16, [p + q for p, q in zip(base[Y], low)])
 
 
-def partner_kernel(flags, lref, xref, gref, yinref, gxref, gzref, bxref, bzref, ta, tb, oz, ot, orow, oy, ow, on, ob):
+def partner_kernel(
+    flags, lref, xref, gref, yinref, gxref, gzref, bxref, bzref, lowref, ta, tb, oz, ot, orow, oy, ow, on, ob
+):
     sites = Sites()
     halo = Halo(flags, None, None, ta, tb, None, None)
     put(oy, 0, get(yinref, 0, 48))
@@ -414,8 +416,10 @@
         part = antihermitian(outer(half(oy, mu, 1), kept[mu]), HOPPING)
         put(on, 8 * mu, part)
         moved = part + [v for d in range(3) if d != mu for v in rows[d]]
+        if mu == Z:
+            moved += get(lowref, 0, 8)
         ref = {Z: oz, T: ot, R: orow}[mu]
-        put(ref, 0, [sites.pack_low(moved[2 * i], moved[2 * i + 1], mu) for i in range(AGAIN)])
+        put(ref, 0, [sites.pack_low(moved[2 * i], moved[2 * i + 1], mu) for i in range(len(moved) // 2)])
 
 
 def gauge_kernel(flags, lref, yref, wref, wzref, wxyref, gxyref, m2ref, fxref, fzref, bzxyref, ta, tb, obase, oq):
@@ -461,19 +465,27 @@
     ]
 
 
-def last_kernel(lref, baseref, nref, btref, bzref, bxref, qtref, qzref, qxref, zd, td, rd, oref):
+def last_kernel(lref, baseref, nref, btref, bzref, bxref, lowref, qtref, qzref, qxref, zd, td, rd, oref):
     sites = Sites()
     zero = jnp.zeros((4, 128), jnp.float32)
+    base = [get(baseref, 8 * mu, 8) for mu in range(4)]
     for mu in range(4):
-        x = get(baseref, 8 * mu, 8)
+        x = base[mu]
         if mu != Y:
             m = {Z: zd, T: td, R: rd}[mu]
             others_of = [d for d in range(3) if d != mu]
             own = get(nref, 8 * mu, 8) + [v for d in others_of for v in get((btref, bzref, bxref)[d], 0, 12)]
+            if mu == Z:
+                own += get(lowref, 0, 8)
             ahead = []
-            for i in range(AGAIN):
+            for i in range(len(own) // 2):
                 ahead += sites.ahead(own[2 * i], own[2 * i + 1], m[i], mu)
             u = link(lref, mu)
+            if mu == Z:
+                p = transport(ahead[32:], adjoint(u))
+                back = transport(p, link(lref, Y))
+                x = [a + b - sites.y_behind(c) for a, b, c in zip(x, p, back)]
+                base[Y] = [a - b for a, b in zip(base[Y], p)]
             total = times_dagger(ahead[:8], u)
             for k, d in enumerate(others_of):
                 c = third_row(rows_of(ahead[8 + 12 * k : 20 + 12 * k]))
@@ -537,7 +549,7 @@
     zd, zu, ta, tb, rd, ru, g, lk, xs = call(
         pack_kernel,
         (flags, pltpu.with_memory_space_constraint(lk, pltpu.HBM), pltpu.with_memory_space_constraint(xs, pltpu.HBM)),
-        (LOW, HIGH, HIGH, HIGH, LOW, HIGH, 72, 72, 48),
+        (LOW_Z, HIGH, HIGH, HIGH, LOW, HIGH, 72, 72, 48),
         4_000_000,
         hbm=(1, 2),
         sems=2,
@@ -549,22 +561,22 @@
     rd = move(rd, "xy", -1)
     ru = move(ru, "xy", 1)
     yl, wxy, gxy, bx, m2, fx, qx, bxy = call(
-        early_kernel, (lk, xs, g, rd, ru), (48, 48, 48, 12, 36, 36, 36, 16), 20_000_000
+        early_kernel, (lk, xs, g, rd, ru), (48, 48, 48, 12, 18, 36, 36, 16), 20_000_000
     )
-    yl, wz, gz, bz, fz, qz, bzxy = call(
-        depth_kernel, (lk, xs, g, yl, m2, fx, bxy, zd, zu), (48, 24, 24, 12, 18, 36, 24), 20_000_000
+    yl, wz, gz, bz, fz, qz, bzxy, low = call(
+        depth_kernel, (lk, xs, g, yl, fx, bxy, zd, zu), (48, 24, 24, 12, 18, 36, 24, 8), 20_000_000
     )
     oz, ot, orow, y, w, n, bt = call(
         partner_kernel,
-        (flags, lk, xs, g, yl, gxy, gz, bx, bz, ta, tb),
-        (AGAIN, AGAIN, AGAIN, 48, 24, 24, 12),
+        (flags, lk, xs, g, yl, gxy, gz, bx, bz, low, ta, tb),
+        (AGAIN_Z, AGAIN, AGAIN, 48, 24, 24, 12),
         20_000_000,
     )
     oz = move(oz, "gz", -1)
     ot = move(ot, "ta", -1)
     orow = move(orow, "xy", -1)
     base, qt = call(gauge_kernel, (flags, lk, y, w, wz, wxy, gxy, m2, fx, fz, bzxy, ta, tb), (32, 36), 20_000_000)
-    (force,) = call(last_kernel, (lk, base, n, bt, bz, bx, qt, qz, qx, oz, ot, orow), (72,), 4_000_000)
+    (force,) = call(last_kernel, (lk, base, n, bt, bz, bx, low, qt, qz, qx, oz, ot, orow), (72,), 4_000_000)
     return force.reshape(shape)
 
 

time: 73.2 us -> 71.9 us (0.982)
  waiting for transfers between devices: 17.2 us -> 14.6 us
  starting transfers between devices: 49.2 us -> 50.3 us
    ppermute x7, waiting for transfers between devices: 17.2 us -> 14.6 us  [move(): return lax.ppermute(x, axis, [(i, (i + by) % size) for i in range(size)])]
    ppermute x7, starting transfers between devices: 31.7 us -> 32.7 us  [move(): return lax.ppermute(x, axis, [(i, (i + by) % size) for i in range(size)])]
  transfers between devices with their start and end apart: 9 -> 9, of which waited for: 3 -> 2; matrix products, arithmetic and copies ran while one was open for 0% -> 0% of each run, Pallas kernels for 3% -> 3%
where the time goes in v6:
time: 71.9 us; the launch traced here: 71.3 us
  starting transfers between devices  50.3 us (70%)
  waiting for transfers between devices  14.6 us (20%)
  Pallas kernels  6.21 us (9%)
    ppermute x7, starting transfers between devices, move(): return lax.ppermute(x, axis, [(i, (i + by) % size) for i in range(size)])  32.7 us
    ppermute x2, starting transfers between devices, meet(): return lax.ppermute(x, axis, pairs)  17.5 us
    ppermute x7, waiting for transfers between devices, move(): return lax.ppermute(x, axis, [(i, (i + by) % size) for i in range(size)])  14.6 us
    pallas_call x6, Pallas kernels, call(): pl.pallas_call(body, in_specs=specs, out_specs=[pl.BlockSpec(memory_space...  6.21 us
  transfers between devices with their start and end apart: 9, of which 2 were waited for; matrix products, arithmetic and copies ran while one was open for 0% of the time, Pallas kernels for 3%

profile of v6, /device:TPU:1, one launch (start us, length us, event | category | flops | bytes accessed | tf_op | source)
XLA Modules:
  0.0 71.3 jit_solution(7791999257812013801)
XLA Ops:
  0.0 0.1 pad_add_fusion.flags
  0.1 1.8 %shard_map.28 = (f32[24,4,128]{2,1,0:T(4,128)S(1)}, f32[36,4,128]{2,1,0:T(4,128)S(1)}, f32[36,4,128]{2,1,0:T(4,128)S(1)}, f32[36,4,128]{2,1,0:T(4,128)S(1)}, f32...) custom-call(s32[3]{0:T(128)S(1)} %pad_add_fusion.flags, ...), custom_call_target="tpu_custom_call" | custom-call | flops 4000000 | bytes 409600 | tf_op jit(solution)/shard_map/pallas_call | solution.py:517
  1.9 14.1 %collective-permute-start = (f32[30,4,128]{2,1,0:T(4,128)S(1)}, f32[30,4,128]{2,1,0:T(4,128)S(1)}, u32[]{:S(2)}, u32[]{:S(2)}) collective-permute-start(f32[30,4,128]{2,1,0:T(4,128)S(1)} %get-tuple-element.42), channel_id=1, source_target_pairs={{0,7},{1,0},{2,1},{3,2},{4,3},{5,4},{6,5},{7,6},{8,15},{9,8},{10,9... | collective-permute-start | bytes 184328 | tf_op jit(solution)/shard_map/ppermute | solution.py:531
  16.0 0.0 collective-permute-start.1
  16.0 4.0 %collective-permute-start.3 = (f32[36,4,128]{2,1,0:T(4,128)S(1)}, f32[36,4,128]{2,1,0:T(4,128)S(1)}, u32[]{:S(2)}, u32[]{:S(2)}) collective-permute-start(f32[36,4,128]{2,1,0:T(4,128)S(1)} %get-tuple-element.48), channel_id=1, source_target_pairs={{0,8},{8,16},{16,24},{24,0},{1,9},{9,17},{17,25},{25,1},{2,10},{10... | collective-permute-start | bytes 221192 | tf_op jit(solution)/shard_map/ppermute | solution.py:531
  20.1 3.1 %collective-permute-start.4 = (f32[36,4,128]{2,1,0:T(4,128)S(1)}, f32[36,4,128]{2,1,0:T(4,128)S(1)}, u32[]{:S(2)}, u32[]{:S(2)}) collective-permute-start(f32[36,4,128]{2,1,0:T(4,128)S(1)} %get-tuple-element.55), channel_id=1, source_target_pairs={{0,32},{32,0},{64,96},{96,64},{128,160},{160,128},{192,224},{224,1... | collective-permute-start | bytes 221192 | tf_op jit(solution)/shard_map/ppermute | solution.py:540
  23.2 14.4 %collective-permute-start.5 = (f32[36,4,128]{2,1,0:T(4,128)S(1)}, f32[36,4,128]{2,1,0:T(4,128)S(1)}, u32[]{:S(2)}, u32[]{:S(2)}) collective-permute-start(f32[36,4,128]{2,1,0:T(4,128)S(1)} %get-tuple-element.56), channel_id=1, source_target_pairs={{32,64},{64,32},{96,128},{128,96},{160,192},{192,160},{224,256},{2... | collective-permute-start | bytes 221192 | tf_op jit(solution)/shard_map/ppermute | solution.py:540
  37.6 0.0 collective-permute-done.rd
  37.6 1.9 %collective-permute-start.2 = (f32[24,4,128]{2,1,0:T(4,128)S(1)}, f32[24,4,128]{2,1,0:T(4,128)S(1)}, u32[]{:S(2)}, u32[]{:S(2)}) collective-permute-start(f32[24,4,128]{2,1,0:T(4,128)S(1)} %get-tuple-element.47), channel_id=1, source_target_pairs={{0,24},{8,0},{16,8},{24,16},{1,25},{9,1},{17,9},{25,17},{2,26},{10... | collective-permute-start | bytes 147464 | tf_op jit(solution)/shard_map/ppermute | solution.py:531
  39.5 0.0 collective-permute-done.1.ru
  39.5 0.7 shard_map.29
  40.2 12.1 %collective-permute-done.2.zd = f32[24,4,128]{2,1,0:T(4,128)S(1)} collective-permute-done((f32[24,4,128]{2,1,0:T(4,128)S(1)}, f32[24,4,128]{2,1,0:T(4,128)S(1)}, u32[]{:S(2)}, u32[]{:S(2)}) %collective-permute-start.2) | collective-permute-done | bytes 49184 | tf_op jit(solution)/shard_map/ppermute | solution.py:531
  52.4 0.4 shard_map.30
  52.8 0.0 collective-permute-done.4.ta
  52.8 0.0 collective-permute-done.5.tb
  52.8 0.8 %shard_map.31 = (f32[20,4,128]{2,1,0:T(4,128)S(1)}, f32[16,4,128]{2,1,0:T(4,128)S(1)}, f32[16,4,128]{2,1,0:T(4,128)S(1)}, f32[48,4,128]{2,1,0:T(4,128)S(1)}, f32...) custom-call(s32[3]{0:T(128)S(1)} %pad_add_fusion.flags, ...), custom_call_target="tpu_custom_call" | custom-call | flops 20000000 | bytes 409600 | tf_op jit(solution)/shard_map/pallas_call | solution.py:517
  53.6 6.6 %collective-permute-start.6 = (f32[20,4,128]{2,1,0:T(4,128)S(1)}, f32[20,4,128]{2,1,0:T(4,128)S(1)}, u32[]{:S(2)}, u32[]{:S(2)}) collective-permute-start(f32[20,4,128]{2,1,0:T(4,128)S(1)} %get-tuple-element.70), channel_id=1, source_target_pairs={{0,24},{8,0},{16,8},{24,16},{1,25},{9,1},{17,9},{25,17},{2,26},{10... | collective-permute-start | bytes 122888 | tf_op jit(solution)/shard_map/ppermute | solution.py:531
  60.2 1.9 %collective-permute-start.7 = (f32[16,4,128]{2,1,0:T(4,128)S(1)}, f32[16,4,128]{2,1,0:T(4,128)S(1)}, u32[]{:S(2)}, u32[]{:S(2)}) collective-permute-start(f32[16,4,128]{2,1,0:T(4,128)S(1)} %get-tuple-element.71), channel_id=1, source_target_pairs={{0,992},{32,0},{64,32},{96,64},{128,96},{160,128},{192,160},{224,1... | collective-permute-start | bytes 98312 | tf_op jit(solution)/shard_map/ppermute | solution.py:531
  62.1 4.2 %collective-permute-start.8 = (f32[16,4,128]{2,1,0:T(4,128)S(1)}, f32[16,4,128]{2,1,0:T(4,128)S(1)}, u32[]{:S(2)}, u32[]{:S(2)}) collective-permute-start(f32[16,4,128]{2,1,0:T(4,128)S(1)} %get-tuple-element.72), channel_id=1, source_target_pairs={{0,7},{1,0},{2,1},{3,2},{4,3},{5,4},{6,5},{7,6},{8,15},{9,8},{10,9... | collective-permute-start | bytes 98312 | tf_op jit(solution)/shard_map/ppermute | solution.py:531
  66.3 1.3 %shard_map.32 = (f32[32,4,128]{2,1,0:T(4,128)S(1)}, f32[36,4,128]{2,1,0:T(4,128)S(1)}) custom-call(s32[3]{0:T(128)S(1)} %pad_add_fusion.flags, f32[72,4,128]{2,1,0:T(4,128)S(1)} %get-tuple-element.39.lref, f32[48,4,128]{2,1,0:T(4,128)S(1)} %get-tuple-element.57.yref, f32[24,4,128]{2,1,0:T(4,128)S(1)} %get-tuple-element.58.wref, ...), custom_call_target="tpu_custom_call" | custom-call | flops 20000000 | bytes 409600 | tf_op jit(solution)/shard_map/pallas_call | solution.py:517
  67.6 0.0 collective-permute-done.7.td
  67.6 2.4 %collective-permute-done.8.rd = f32[16,4,128]{2,1,0:T(4,128)S(1)} collective-permute-done((f32[16,4,128]{2,1,0:T(4,128)S(1)}, f32[16,4,128]{2,1,0:T(4,128)S(1)}, u32[]{:S(2)}, u32[]{:S(2)}) %collective-permute-start.8) | collective-permute-done | bytes 32800 | tf_op jit(solution)/shard_map/ppermute | solution.py:531
  70.1 0.0 collective-permute-done.6.zd
  70.1 1.2 %shard_map.33 = f32[72,4,128]{2,1,0:T(4,128)} custom-call(f32[72,4,128]{2,1,0:T(4,128)S(1)} %get-tuple-element.39.lref, f32[32,4,128]{2,1,0:T(4,128)S(1)} %get-tuple-element.64.baseref, f32[24,4,128]{2,1,0:T(4,128)S(1)} %get-tuple-element.65.nref, f32[12,4,128]{2,1,0:T(4,128)S(1)} %get-tuple-element.66.btref, f32[12,4,128]{2,1,0:T(4,128)S(1)} %get-tuple-element.53.bzref, ...), custom_call_target="tpu_custom_call" | custom-call | flops 4000000 | bytes 409600 | tf_op jit(solution)/shard_map/pallas_call | solution.py:517
  (1 shorter events, 0.0 us)
Async XLA Ops:
  1.9 35.7 %collective-permute-start = (f32[30,4,128]{2,1,0:T(4,128)S(1)}, f32[30,4,128]{2,1,0:T(4,128)S(1)}, u32[]{:S(2)}, u32[]{:S(2)}) collective-permute-start(f32[30,4,128]{2,1,0:T(4,128)S(1)} %get-tuple-element.42), channel_id=1, source_target_pairs={{0,7},{1,0},{2,1},{3,2},{4,3},{5,4},{6,5},{7,6},{8,15},{9,8},{10,9... | collective-permute-start | bytes 184328 | tf_op jit(solution)/shard_map/ppermute | solution.py:531
  16.0 23.5 %collective-permute-start.1 = (f32[36,4,128]{2,1,0:T(4,128)S(1)}, f32[36,4,128]{2,1,0:T(4,128)S(1)}, u32[]{:S(2)}, u32[]{:S(2)}) collective-permute-start(f32[36,4,128]{2,1,0:T(4,128)S(1)} %get-tuple-element.43), channel_id=1, source_target_pairs={{0,1},{1,2},{2,3},{3,4},{4,5},{5,6},{6,7},{7,0},{8,9},{9,10},{10,1... | collective-permute-start | bytes 221192 | tf_op jit(solution)/shard_map/ppermute | solution.py:531
  16.0 36.3 %collective-permute-start.3 = (f32[36,4,128]{2,1,0:T(4,128)S(1)}, f32[36,4,128]{2,1,0:T(4,128)S(1)}, u32[]{:S(2)}, u32[]{:S(2)}) collective-permute-start(f32[36,4,128]{2,1,0:T(4,128)S(1)} %get-tuple-element.48), channel_id=1, source_target_pairs={{0,8},{8,16},{16,24},{24,0},{1,9},{9,17},{17,25},{25,1},{2,10},{10... | collective-permute-start | bytes 221192 | tf_op jit(solution)/shard_map/ppermute | solution.py:531
  20.1 32.7 %collective-permute-start.4 = (f32[36,4,128]{2,1,0:T(4,128)S(1)}, f32[36,4,128]{2,1,0:T(4,128)S(1)}, u32[]{:S(2)}, u32[]{:S(2)}) collective-permute-start(f32[36,4,128]{2,1,0:T(4,128)S(1)} %get-tuple-element.55), channel_id=1, source_target_pairs={{0,32},{32,0},{64,96},{96,64},{128,160},{160,128},{192,224},{224,1... | collective-permute-start | bytes 221192 | tf_op jit(solution)/shard_map/ppermute | solution.py:540
  23.2 29.6 %collective-permute-start.5 = (f32[36,4,128]{2,1,0:T(4,128)S(1)}, f32[36,4,128]{2,1,0:T(4,128)S(1)}, u32[]{:S(2)}, u32[]{:S(2)}) collective-permute-start(f32[36,4,128]{2,1,0:T(4,128)S(1)} %get-tuple-element.56), channel_id=1, source_target_pairs={{32,64},{64,32},{96,128},{128,96},{160,192},{192,160},{224,256},{2... | collective-permute-start | bytes 221192 | tf_op jit(solution)/shard_map/ppermute | solution.py:540
  37.6 14.8 %collective-permute-start.2 = (f32[24,4,128]{2,1,0:T(4,128)S(1)}, f32[24,4,128]{2,1,0:T(4,128)S(1)}, u32[]{:S(2)}, u32[]{:S(2)}) collective-permute-start(f32[24,4,128]{2,1,0:T(4,128)S(1)} %get-tuple-element.47), channel_id=1, source_target_pairs={{0,24},{8,0},{16,8},{24,16},{1,25},{9,1},{17,9},{25,17},{2,26},{10... | collective-permute-start | bytes 147464 | tf_op jit(solution)/shard_map/ppermute | solution.py:531
  53.6 16.4 %collective-permute-start.6 = (f32[20,4,128]{2,1,0:T(4,128)S(1)}, f32[20,4,128]{2,1,0:T(4,128)S(1)}, u32[]{:S(2)}, u32[]{:S(2)}) collective-permute-start(f32[20,4,128]{2,1,0:T(4,128)S(1)} %get-tuple-element.70), channel_id=1, source_target_pairs={{0,24},{8,0},{16,8},{24,16},{1,25},{9,1},{17,9},{25,17},{2,26},{10... | collective-permute-start | bytes 122888 | tf_op jit(solution)/shard_map/ppermute | solution.py:531
  60.2 7.4 %collective-permute-start.7 = (f32[16,4,128]{2,1,0:T(4,128)S(1)}, f32[16,4,128]{2,1,0:T(4,128)S(1)}, u32[]{:S(2)}, u32[]{:S(2)}) collective-permute-start(f32[16,4,128]{2,1,0:T(4,128)S(1)} %get-tuple-element.71), channel_id=1, source_target_pairs={{0,992},{32,0},{64,32},{96,64},{128,96},{160,128},{192,160},{224,1... | collective-permute-start | bytes 98312 | tf_op jit(solution)/shard_map/ppermute | solution.py:531
  62.1 7.9 %collective-permute-start.8 = (f32[16,4,128]{2,1,0:T(4,128)S(1)}, f32[16,4,128]{2,1,0:T(4,128)S(1)}, u32[]{:S(2)}, u32[]{:S(2)}) collective-permute-start(f32[16,4,128]{2,1,0:T(4,128)S(1)} %get-tuple-element.72), channel_id=1, source_target_pairs={{0,7},{1,0},{2,1},{3,2},{4,3},{5,4},{6,5},{7,6},{8,15},{9,8},{10,9... | collective-permute-start | bytes 98312 | tf_op jit(solution)/shard_map/ppermute | solution.py:531

commit v7 on v6

--- a/solution.py
+++ b/solution.py
@@ -465,11 +465,12 @@
     ]
 
 
-def last_kernel(lref, baseref, nref, btref, bzref, bxref, lowref, qtref, qzref, qxref, zd, td, rd, oref):
+def last_kernel(lref, baseref, nref, btref, bzref, bxref, lowref, qtref, qzref, qxref, zd, td, rd, out, oref, sems):
     sites = Sites()
     zero = jnp.zeros((4, 128), jnp.float32)
     base = [get(baseref, 8 * mu, 8) for mu in range(4)]
-    for mu in range(4):
+    copies = []
+    for mu in (Z, Y, T, R):
         x = base[mu]
         if mu != Y:
             m = {Z: zd, T: td, R: rd}[mu]
@@ -504,9 +505,14 @@
         oref[at + 9] = x[6]
         oref[at + 13] = x[7]
         oref[at + 17] = -(x[6] + x[7])
-
-
-def call(body, operands, outs, flops, scratch=(), hbm=(), sems=0):
+        copy = pltpu.make_async_copy(oref.at[pl.ds(at, 18)], out.at[pl.ds(at, 18)], sems.at[mu])
+        copy.start()
+        copies.append(copy)
+    for copy in copies:
+        copy.wait()
+
+
+def call(body, operands, outs, flops, scratch=(), hbm=(), sems=0, out_space=pltpu.VMEM):
     specs = [
         pl.BlockSpec(
             memory_space=pltpu.SMEM if o.dtype == jnp.int32 else pltpu.HBM if i in hbm else pltpu.VMEM
@@ -517,7 +523,7 @@
     return pl.pallas_call(
         body,
         in_specs=specs,
-        out_specs=[pl.BlockSpec(memory_space=pltpu.VMEM) for _ in outs],
+        out_specs=[pl.BlockSpec(memory_space=out_space) for _ in outs],
         out_shape=[jax.ShapeDtypeStruct((n, 4, 128), jnp.float32) for n in outs],
         scratch_shapes=scratch + ([pltpu.SemaphoreType.DMA((sems,))] if sems else []),
         cost_estimate=pl.CostEstimate(flops=flops, bytes_accessed=4 * 512 * 200, transcendentals=0),
@@ -576,7 +582,15 @@
     ot = move(ot, "ta", -1)
     orow = move(orow, "xy", -1)
     base, qt = call(gauge_kernel, (flags, lk, y, w, wz, wxy, gxy, m2, fx, fz, bzxy, ta, tb), (32, 36), 20_000_000)
-    (force,) = call(last_kernel, (lk, base, n, bt, bz, bx, low, qt, qz, qx, oz, ot, orow), (72,), 4_000_000)
+    (force,) = call(
+        last_kernel,
+        (lk, base, n, bt, bz, bx, low, qt, qz, qx, oz, ot, orow),
+        (72,),
+        4_000_000,
+        (72,),
+        sems=4,
+        out_space=pltpu.HBM,
+    )
     return force.reshape(shape)
 
 

time: 71.9 us -> 71.9 us (level)
  no operation moved by 1% of the time
where the time goes in v7:
time: 71.9 us; the launch traced here: 71.3 us
  starting transfers between devices  50.3 us (70%)
  waiting for transfers between devices  14.6 us (20%)
  Pallas kernels  6.24 us (9%)
    ppermute x7, starting transfers between devices, move(): return lax.ppermute(x, axis, [(i, (i + by) % size) for i in range(size)])  32.7 us
    ppermute x2, starting transfers between devices, meet(): return lax.ppermute(x, axis, pairs)  17.5 us
    ppermute x7, waiting for transfers between devices, move(): return lax.ppermute(x, axis, [(i, (i + by) % size) for i in range(size)])  14.6 us
    pallas_call x6, Pallas kernels, call(): pl.pallas_call(body, in_specs=specs, out_specs=[pl.BlockSpec(memory_space...  6.24 us
  transfers between devices with their start and end apart: 9, of which 2 were waited for; matrix products, arithmetic and copies ran while one was open for 0% of the time, Pallas kernels for 3%

profile of v7, /device:TPU:1, one launch (start us, length us, event | category | flops | bytes accessed | tf_op | source)
XLA Modules:
  0.0 71.3 jit_solution(14373793393045553043)
XLA Ops:
  0.0 0.1 pad_add_fusion.flags
  0.1 1.8 %shard_map.28 = (f32[24,4,128]{2,1,0:T(4,128)S(1)}, f32[36,4,128]{2,1,0:T(4,128)S(1)}, f32[36,4,128]{2,1,0:T(4,128)S(1)}, f32[36,4,128]{2,1,0:T(4,128)S(1)}, f32...) custom-call(s32[3]{0:T(128)S(1)} %pad_add_fusion.flags, ...), custom_call_target="tpu_custom_call" | custom-call | flops 4000000 | bytes 409600 | tf_op jit(solution)/shard_map/pallas_call | solution.py:523
  1.9 14.1 %collective-permute-start = (f32[30,4,128]{2,1,0:T(4,128)S(1)}, f32[30,4,128]{2,1,0:T(4,128)S(1)}, u32[]{:S(2)}, u32[]{:S(2)}) collective-permute-start(f32[30,4,128]{2,1,0:T(4,128)S(1)} %get-tuple-element.42), channel_id=1, source_target_pairs={{0,7},{1,0},{2,1},{3,2},{4,3},{5,4},{6,5},{7,6},{8,15},{9,8},{10,9... | collective-permute-start | bytes 184328 | tf_op jit(solution)/shard_map/ppermute | solution.py:537
  16.0 0.0 collective-permute-start.1
  16.0 4.0 %collective-permute-start.3 = (f32[36,4,128]{2,1,0:T(4,128)S(1)}, f32[36,4,128]{2,1,0:T(4,128)S(1)}, u32[]{:S(2)}, u32[]{:S(2)}) collective-permute-start(f32[36,4,128]{2,1,0:T(4,128)S(1)} %get-tuple-element.48), channel_id=1, source_target_pairs={{0,8},{8,16},{16,24},{24,0},{1,9},{9,17},{17,25},{25,1},{2,10},{10... | collective-permute-start | bytes 221192 | tf_op jit(solution)/shard_map/ppermute | solution.py:537
  20.1 3.1 %collective-permute-start.4 = (f32[36,4,128]{2,1,0:T(4,128)S(1)}, f32[36,4,128]{2,1,0:T(4,128)S(1)}, u32[]{:S(2)}, u32[]{:S(2)}) collective-permute-start(f32[36,4,128]{2,1,0:T(4,128)S(1)} %get-tuple-element.55), channel_id=1, source_target_pairs={{0,32},{32,0},{64,96},{96,64},{128,160},{160,128},{192,224},{224,1... | collective-permute-start | bytes 221192 | tf_op jit(solution)/shard_map/ppermute | solution.py:546
  23.2 14.4 %collective-permute-start.5 = (f32[36,4,128]{2,1,0:T(4,128)S(1)}, f32[36,4,128]{2,1,0:T(4,128)S(1)}, u32[]{:S(2)}, u32[]{:S(2)}) collective-permute-start(f32[36,4,128]{2,1,0:T(4,128)S(1)} %get-tuple-element.56), channel_id=1, source_target_pairs={{32,64},{64,32},{96,128},{128,96},{160,192},{192,160},{224,256},{2... | collective-permute-start | bytes 221192 | tf_op jit(solution)/shard_map/ppermute | solution.py:546
  37.6 0.0 collective-permute-done.rd
  37.6 1.9 %collective-permute-start.2 = (f32[24,4,128]{2,1,0:T(4,128)S(1)}, f32[24,4,128]{2,1,0:T(4,128)S(1)}, u32[]{:S(2)}, u32[]{:S(2)}) collective-permute-start(f32[24,4,128]{2,1,0:T(4,128)S(1)} %get-tuple-element.47), channel_id=1, source_target_pairs={{0,24},{8,0},{16,8},{24,16},{1,25},{9,1},{17,9},{25,17},{2,26},{10... | collective-permute-start | bytes 147464 | tf_op jit(solution)/shard_map/ppermute | solution.py:537
  39.5 0.0 collective-permute-done.1.ru
  39.5 0.7 shard_map.29
  40.2 12.1 %collective-permute-done.2.zd = f32[24,4,128]{2,1,0:T(4,128)S(1)} collective-permute-done((f32[24,4,128]{2,1,0:T(4,128)S(1)}, f32[24,4,128]{2,1,0:T(4,128)S(1)}, u32[]{:S(2)}, u32[]{:S(2)}) %collective-permute-start.2) | collective-permute-done | bytes 49184 | tf_op jit(solution)/shard_map/ppermute | solution.py:537
  52.4 0.4 shard_map.30
  52.8 0.0 collective-permute-done.4.ta
  52.8 0.0 collective-permute-done.5.tb
  52.8 0.8 %shard_map.31 = (f32[20,4,128]{2,1,0:T(4,128)S(1)}, f32[16,4,128]{2,1,0:T(4,128)S(1)}, f32[16,4,128]{2,1,0:T(4,128)S(1)}, f32[48,4,128]{2,1,0:T(4,128)S(1)}, f32...) custom-call(s32[3]{0:T(128)S(1)} %pad_add_fusion.flags, ...), custom_call_target="tpu_custom_call" | custom-call | flops 20000000 | bytes 409600 | tf_op jit(solution)/shard_map/pallas_call | solution.py:523
  53.6 6.6 %collective-permute-start.6 = (f32[20,4,128]{2,1,0:T(4,128)S(1)}, f32[20,4,128]{2,1,0:T(4,128)S(1)}, u32[]{:S(2)}, u32[]{:S(2)}) collective-permute-start(f32[20,4,128]{2,1,0:T(4,128)S(1)} %get-tuple-element.70), channel_id=1, source_target_pairs={{0,24},{8,0},{16,8},{24,16},{1,25},{9,1},{17,9},{25,17},{2,26},{10... | collective-permute-start | bytes 122888 | tf_op jit(solution)/shard_map/ppermute | solution.py:537
  60.2 1.9 %collective-permute-start.7 = (f32[16,4,128]{2,1,0:T(4,128)S(1)}, f32[16,4,128]{2,1,0:T(4,128)S(1)}, u32[]{:S(2)}, u32[]{:S(2)}) collective-permute-start(f32[16,4,128]{2,1,0:T(4,128)S(1)} %get-tuple-element.71), channel_id=1, source_target_pairs={{0,992},{32,0},{64,32},{96,64},{128,96},{160,128},{192,160},{224,1... | collective-permute-start | bytes 98312 | tf_op jit(solution)/shard_map/ppermute | solution.py:537
  62.1 4.2 %collective-permute-start.8 = (f32[16,4,128]{2,1,0:T(4,128)S(1)}, f32[16,4,128]{2,1,0:T(4,128)S(1)}, u32[]{:S(2)}, u32[]{:S(2)}) collective-permute-start(f32[16,4,128]{2,1,0:T(4,128)S(1)} %get-tuple-element.72), channel_id=1, source_target_pairs={{0,7},{1,0},{2,1},{3,2},{4,3},{5,4},{6,5},{7,6},{8,15},{9,8},{10,9... | collective-permute-start | bytes 98312 | tf_op jit(solution)/shard_map/ppermute | solution.py:537
  66.3 1.3 %shard_map.32 = (f32[32,4,128]{2,1,0:T(4,128)S(1)}, f32[36,4,128]{2,1,0:T(4,128)S(1)}) custom-call(s32[3]{0:T(128)S(1)} %pad_add_fusion.flags, f32[72,4,128]{2,1,0:T(4,128)S(1)} %get-tuple-element.39.lref, f32[48,4,128]{2,1,0:T(4,128)S(1)} %get-tuple-element.57.yref, f32[24,4,128]{2,1,0:T(4,128)S(1)} %get-tuple-element.58.wref, ...), custom_call_target="tpu_custom_call" | custom-call | flops 20000000 | bytes 409600 | tf_op jit(solution)/shard_map/pallas_call | solution.py:523
  67.6 0.0 collective-permute-done.7.td
  67.6 2.4 %collective-permute-done.8.rd = f32[16,4,128]{2,1,0:T(4,128)S(1)} collective-permute-done((f32[16,4,128]{2,1,0:T(4,128)S(1)}, f32[16,4,128]{2,1,0:T(4,128)S(1)}, u32[]{:S(2)}, u32[]{:S(2)}) %collective-permute-start.8) | collective-permute-done | bytes 32800 | tf_op jit(solution)/shard_map/ppermute | solution.py:537
  70.1 0.0 collective-permute-done.6.zd
  70.1 1.2 %shard_map.33 = f32[72,4,128]{2,1,0:T(4,128)} custom-call(f32[72,4,128]{2,1,0:T(4,128)S(1)} %get-tuple-element.39.lref, f32[32,4,128]{2,1,0:T(4,128)S(1)} %get-tuple-element.64.baseref, f32[24,4,128]{2,1,0:T(4,128)S(1)} %get-tuple-element.65.nref, f32[12,4,128]{2,1,0:T(4,128)S(1)} %get-tuple-element.66.btref, f32[12,4,128]{2,1,0:T(4,128)S(1)} %get-tuple-element.53.bzref, ...), custom_call_target="tpu_custom_call" | custom-call | flops 4000000 | bytes 409600 | tf_op jit(solution)/shard_map/pallas_call | solution.py:523
  (1 shorter events, 0.0 us)
Async XLA Ops:
  1.9 35.7 %collective-permute-start = (f32[30,4,128]{2,1,0:T(4,128)S(1)}, f32[30,4,128]{2,1,0:T(4,128)S(1)}, u32[]{:S(2)}, u32[]{:S(2)}) collective-permute-start(f32[30,4,128]{2,1,0:T(4,128)S(1)} %get-tuple-element.42), channel_id=1, source_target_pairs={{0,7},{1,0},{2,1},{3,2},{4,3},{5,4},{6,5},{7,6},{8,15},{9,8},{10,9... | collective-permute-start | bytes 184328 | tf_op jit(solution)/shard_map/ppermute | solution.py:537
  16.0 23.5 %collective-permute-start.1 = (f32[36,4,128]{2,1,0:T(4,128)S(1)}, f32[36,4,128]{2,1,0:T(4,128)S(1)}, u32[]{:S(2)}, u32[]{:S(2)}) collective-permute-start(f32[36,4,128]{2,1,0:T(4,128)S(1)} %get-tuple-element.43), channel_id=1, source_target_pairs={{0,1},{1,2},{2,3},{3,4},{4,5},{5,6},{6,7},{7,0},{8,9},{9,10},{10,1... | collective-permute-start | bytes 221192 | tf_op jit(solution)/shard_map/ppermute | solution.py:537
  16.0 36.3 %collective-permute-start.3 = (f32[36,4,128]{2,1,0:T(4,128)S(1)}, f32[36,4,128]{2,1,0:T(4,128)S(1)}, u32[]{:S(2)}, u32[]{:S(2)}) collective-permute-start(f32[36,4,128]{2,1,0:T(4,128)S(1)} %get-tuple-element.48), channel_id=1, source_target_pairs={{0,8},{8,16},{16,24},{24,0},{1,9},{9,17},{17,25},{25,1},{2,10},{10... | collective-permute-start | bytes 221192 | tf_op jit(solution)/shard_map/ppermute | solution.py:537
  20.1 32.7 %collective-permute-start.4 = (f32[36,4,128]{2,1,0:T(4,128)S(1)}, f32[36,4,128]{2,1,0:T(4,128)S(1)}, u32[]{:S(2)}, u32[]{:S(2)}) collective-permute-start(f32[36,4,128]{2,1,0:T(4,128)S(1)} %get-tuple-element.55), channel_id=1, source_target_pairs={{0,32},{32,0},{64,96},{96,64},{128,160},{160,128},{192,224},{224,1... | collective-permute-start | bytes 221192 | tf_op jit(solution)/shard_map/ppermute | solution.py:546
  23.2 29.6 %collective-permute-start.5 = (f32[36,4,128]{2,1,0:T(4,128)S(1)}, f32[36,4,128]{2,1,0:T(4,128)S(1)}, u32[]{:S(2)}, u32[]{:S(2)}) collective-permute-start(f32[36,4,128]{2,1,0:T(4,128)S(1)} %get-tuple-element.56), channel_id=1, source_target_pairs={{32,64},{64,32},{96,128},{128,96},{160,192},{192,160},{224,256},{2... | collective-permute-start | bytes 221192 | tf_op jit(solution)/shard_map/ppermute | solution.py:546
  37.6 14.8 %collective-permute-start.2 = (f32[24,4,128]{2,1,0:T(4,128)S(1)}, f32[24,4,128]{2,1,0:T(4,128)S(1)}, u32[]{:S(2)}, u32[]{:S(2)}) collective-permute-start(f32[24,4,128]{2,1,0:T(4,128)S(1)} %get-tuple-element.47), channel_id=1, source_target_pairs={{0,24},{8,0},{16,8},{24,16},{1,25},{9,1},{17,9},{25,17},{2,26},{10... | collective-permute-start | bytes 147464 | tf_op jit(solution)/shard_map/ppermute | solution.py:537
  53.6 16.4 %collective-permute-start.6 = (f32[20,4,128]{2,1,0:T(4,128)S(1)}, f32[20,4,128]{2,1,0:T(4,128)S(1)}, u32[]{:S(2)}, u32[]{:S(2)}) collective-permute-start(f32[20,4,128]{2,1,0:T(4,128)S(1)} %get-tuple-element.70), channel_id=1, source_target_pairs={{0,24},{8,0},{16,8},{24,16},{1,25},{9,1},{17,9},{25,17},{2,26},{10... | collective-permute-start | bytes 122888 | tf_op jit(solution)/shard_map/ppermute | solution.py:537
  60.2 7.4 %collective-permute-start.7 = (f32[16,4,128]{2,1,0:T(4,128)S(1)}, f32[16,4,128]{2,1,0:T(4,128)S(1)}, u32[]{:S(2)}, u32[]{:S(2)}) collective-permute-start(f32[16,4,128]{2,1,0:T(4,128)S(1)} %get-tuple-element.71), channel_id=1, source_target_pairs={{0,992},{32,0},{64,32},{96,64},{128,96},{160,128},{192,160},{224,1... | collective-permute-start | bytes 98312 | tf_op jit(solution)/shard_map/ppermute | solution.py:537
  62.1 7.9 %collective-permute-start.8 = (f32[16,4,128]{2,1,0:T(4,128)S(1)}, f32[16,4,128]{2,1,0:T(4,128)S(1)}, u32[]{:S(2)}, u32[]{:S(2)}) collective-permute-start(f32[16,4,128]{2,1,0:T(4,128)S(1)} %get-tuple-element.72), channel_id=1, source_target_pairs={{0,7},{1,0},{2,1},{3,2},{4,3},{5,4},{6,5},{7,6},{8,15},{9,8},{10,9... | collective-permute-start | bytes 98312 | tf_op jit(solution)/shard_map/ppermute | solution.py:537
